TPU v7x, 32 devices: a whole 2x2x4 slice. The times are simulated.
32 devices in a mesh: section: 2 (over core), ctx: 4 (over y, x), shard: 4 (over z).
Axes of the slice: x: 2, y: 2, z: 4, core: 2. Of those that a mesh axis runs over, the one named last changes fastest.
Arguments:
- inputs: bfloat16 [4, 2, 512, 1088], P('shard', None, 'ctx'), may hold values from -6 to 6
- cotangent: bfloat16 [4, 2, 512, 1088], P('shard', None, 'ctx'), may hold values from -6 to 6
- qkv_weight: bfloat16 [2, 1088, 3264], P('section', 'shard'), may hold values from -0.1875 to 0.1875
- out_weight: bfloat16 [2, 1088, 1088], P('section', 'shard'), may hold values from -1.5 to 1.5
- up_weight: bfloat16 [2, 1088, 4352], P('section', 'shard'), may hold values from -0.1875 to 0.1875
- down_weight: bfloat16 [2, 4352, 1088], P('section', None, 'shard'), may hold values from -0.09375 to 0.09375
- norm_gain: bfloat16 [2, 2, 1088], P('section', None, 'shard'), may hold values from 0.5 to 1.5
- norm_bias: bfloat16 [2, 2, 1088], P('section', None, 'shard'), may hold values from -3 to 3
Outputs:
- layer_outputs: bfloat16 [2, 4, 2, 512, 1088], P('section', 'shard', None, 'ctx')
- input_grads: bfloat16 [2, 4, 2, 512, 1088], P('section', 'shard', None, 'ctx')
- qkv_grad: float32 [2, 1088, 3264], P('section', ('ctx', 'shard'))
- out_grad: float32 [2, 1088, 1088], P('section', ('ctx', 'shard'))
- up_grad: float32 [2, 1088, 4352], P('section', ('ctx', 'shard'))
- down_grad: float32 [2, 4352, 1088], P('section', None, ('ctx', 'shard'))
- gain_grad: float32 [2, 2, 1088], P('section', None, ('ctx', 'shard'))
- bias_grad: float32 [2, 2, 1088], P('section', None, ('ctx', 'shard'))
All inputs are finite; a program needn't handle non-finite values.
Results may differ from a plain program's by a relative error of at most 0.02.
Values may be sent and summed in bfloat16 or wider, within the bound.
A program may use at most 320 MiB of HBM per device.

v0:
```python
import jax
import jax.numpy as jnp
from jax import lax
from jax.sharding import PartitionSpec as P

HEAD = 64


eps_norm = 1e-05
score_scale = 0.125


def passed_along(value, axis, steps):
    count = lax.axis_size(axis)
    initial, last = (max(0, -steps), min(count, count - steps))
    return lax.ppermute(value, axis, [(source, source + steps) for source in range(initial, last)])


def layer_norm(values, gain, shift):
    mean = jnp.mean(values, axis=-1, keepdims=True)
    centred = values - mean
    var = jnp.mean(centred * centred, axis=-1, keepdims=True)
    return centred * lax.rsqrt(var + eps_norm) * gain + shift


def gelu_tanh(values):
    return jax.nn.gelu(values, approximate=True)


def split_pair(key_value, head_count):
    block_len, seq_count, double = key_value.shape
    model_width = double // 2
    key_rows = key_value[..., :model_width].reshape(block_len, seq_count, head_count, HEAD)
    value_rows = key_value[..., model_width:].reshape(block_len, seq_count, head_count, HEAD)
    return (key_rows, value_rows)


def causal_mask(query_pos, key_pos):
    return (key_pos[None, :] <= query_pos[:, None])[None, :, None, :]


def forward_block(running, queries, query_pos, key_value, key_pos):
    row_max, row_sum, accum = running
    key_rows, value_rows = split_pair(key_value, queries.shape[2])
    scores = (
        jnp.einsum("sqhe,kshe->sqhk", queries, key_rows, preferred_element_type=jnp.float32)
        * score_scale
    )
    causal = causal_mask(query_pos, key_pos)
    new_max = jnp.maximum(row_max, jnp.max(jnp.where(causal, scores, -1e30), axis=-1))
    softmax_w = jnp.where(causal, jnp.exp(scores - new_max[..., None]), 0.0)
    factor = jnp.exp(row_max - new_max)
    row_sum = row_sum * factor + jnp.sum(softmax_w, axis=-1)
    accum = accum * factor[..., None] + jnp.einsum(
        "sqhk,kshe->sqhe",
        softmax_w.astype(jnp.bfloat16),
        value_rows,
        preferred_element_type=jnp.float32,
    )
    return (new_max, row_sum, accum)


def split_rows(whole):
    key_count = whole.shape[0]
    block_size = 512
    blocks = whole.reshape((key_count // block_size, block_size) + whole.shape[1:])
    offsets = jnp.arange(key_count // block_size, dtype=jnp.int32) * block_size
    return (blocks, offsets, block_size)


def fold_keys(running, piece, start, queries, query_pos, group_len):
    blocks, offsets, block_size = split_rows(piece)

    def fold_scan_step(inner, scan_item):
        block_rows, offset = scan_item
        for group_id in range(block_rows.shape[2]):
            key_pos = (
                group_id * group_len + start + offset + jnp.arange(block_size, dtype=jnp.int32)
            )
            inner = forward_block(inner, queries, query_pos, block_rows[:, :, group_id], key_pos)
        return (inner, None)

    result, _ = lax.scan(fold_scan_step, running, (blocks, offsets))
    return result


def pair_terms(d_scores, softmax_w, queries, d_attended, block_size):
    d_keys = (
        jnp.einsum("sqhk,sqhe->kshe", d_scores, queries, preferred_element_type=jnp.float32)
        * score_scale
    )
    d_values = jnp.einsum(
        "sqhk,sqhe->kshe",
        softmax_w.astype(jnp.bfloat16),
        d_attended,
        preferred_element_type=jnp.float32,
    )
    shape = (block_size, queries.shape[0], queries.shape[2] * queries.shape[3])
    return jnp.concatenate([d_keys.reshape(shape), d_values.reshape(shape)], axis=-1)


def score_grads(
    queries, query_pos, log_total, row_delta, d_attended, key_rows, value_rows, key_pos
):
    scores = (
        jnp.einsum("sqhe,kshe->sqhk", queries, key_rows, preferred_element_type=jnp.float32)
        * score_scale
    )
    causal = causal_mask(query_pos, key_pos)
    softmax_w = jnp.where(causal, jnp.exp(scores - log_total[..., None]), 0.0)
    d_probs = jnp.einsum(
        "sqhe,kshe->sqhk", d_attended, value_rows, preferred_element_type=jnp.float32
    )
    d_scores = (softmax_w * (d_probs - row_delta[..., None])).astype(jnp.bfloat16)
    return (softmax_w, d_scores)


def backward_keys(whole, queries, query_pos, log_total, row_delta, d_attended, group_len):
    blocks, offsets, block_size = split_rows(whole)

    def backward_scan_step(d_queries, scan_item):
        block_rows, offset = scan_item
        for group_id in range(block_rows.shape[2]):
            key_pos = group_id * group_len + offset + jnp.arange(block_size, dtype=jnp.int32)
            key_rows, value_rows = split_pair(block_rows[:, :, group_id], queries.shape[2])
            softmax_w, d_scores = score_grads(
                queries, query_pos, log_total, row_delta, d_attended, key_rows, value_rows, key_pos
            )
            d_queries = (
                d_queries
                + jnp.einsum(
                    "sqhk,kshe->sqhe", d_scores, key_rows, preferred_element_type=jnp.float32
                )
                * score_scale
            )
        return (d_queries, None)

    d_queries, terms = lax.scan(
        backward_scan_step, jnp.zeros(queries.shape, jnp.float32), (blocks, offsets)
    )
    return (d_queries, None)


def owner_terms(
    own_cache, all_queries, all_d_att, all_totals, all_deltas, micro_index, ctx_id, group_len
):
    block_len, seq_count, group_count, double = own_cache.shape
    head_count = all_queries.shape[2]
    query_rows = all_queries.shape[1]
    query_size = 512
    block_count = query_rows // query_size

    def loop_step(index, total):
        offset = index * query_size
        q_block = lax.dynamic_slice_in_dim(all_queries, offset, query_size, 1)
        d_block = lax.dynamic_slice_in_dim(all_d_att, offset, query_size, 1)
        t_block = lax.dynamic_slice_in_dim(all_totals, offset, query_size, 1)
        r_block = lax.dynamic_slice_in_dim(all_deltas, offset, query_size, 1)
        query_pos = micro_index * group_len + offset + jnp.arange(query_size, dtype=jnp.int32)
        pieces = []
        for group_id in range(group_count):
            key_pos = (
                group_id * group_len + ctx_id * block_len + jnp.arange(block_len, dtype=jnp.int32)
            )
            key_rows, value_rows = split_pair(own_cache[:, :, group_id], head_count)
            softmax_w, d_scores = score_grads(
                q_block, query_pos, t_block, r_block, d_block, key_rows, value_rows, key_pos
            )
            pieces.append(pair_terms(d_scores, softmax_w, q_block, d_block, block_len))
        return total + jnp.stack(pieces, axis=2)

    return lax.fori_loop(0, block_count, loop_step, jnp.zeros(own_cache.shape, jnp.float32))


def store_at(store, value, micro_index, active):
    updated = lax.dynamic_update_index_in_dim(store, value, micro_index, 0)
    return jnp.where(active, updated, store)


def shards(inputs, cotangent, qkv_weight, out_weight, up_weight, down_weight, norm_gain, norm_bias):
    section_id = lax.axis_index("section")
    ctx_count = lax.axis_size("ctx")
    ctx_id = lax.axis_index("ctx")
    seq_count, group_count, block_len, model_width = inputs.shape
    head_count = model_width // HEAD
    group_len = block_len * ctx_count
    row_count = seq_count * block_len
    w_qkv, w_out, w_up, w_down, gains, biases = (
        lax.all_gather(qkv_weight[0], "shard", axis=0, tiled=True),
        lax.all_gather(out_weight[0], "shard", axis=0, tiled=True),
        lax.all_gather(up_weight[0], "shard", axis=0, tiled=True),
        lax.all_gather(down_weight[0], "shard", axis=1, tiled=True),
        lax.all_gather(norm_gain[0], "shard", axis=1, tiled=True),
        lax.all_gather(norm_bias[0], "shard", axis=1, tiled=True),
    )
    gains = gains.astype(jnp.float32)
    biases = biases.astype(jnp.float32)
    ff_width = w_up.shape[1]
    cache = jnp.zeros((block_len, seq_count, group_count, 2 * model_width), jnp.bfloat16)
    in_store = jnp.zeros((group_count, seq_count, block_len, model_width), jnp.bfloat16)
    query_store = jnp.zeros((group_count, seq_count, block_len, head_count, HEAD), jnp.bfloat16)
    att_store = jnp.zeros((group_count, seq_count, block_len, head_count, HEAD), jnp.float32)
    total_store = jnp.zeros((group_count, seq_count, block_len, head_count), jnp.float32)
    middle_store = jnp.zeros((group_count, row_count, model_width), jnp.float32)
    upper_store = jnp.zeros((group_count, row_count, ff_width), jnp.float32)
    out_store = jnp.zeros((group_count, seq_count, block_len, model_width), jnp.bfloat16)
    received = jnp.zeros((seq_count, block_len, model_width), jnp.bfloat16)
    for tick_no in range(group_count + 1):
        micro = tick_no - section_id
        active = (micro >= 0) & (micro < group_count)
        micro_index = jnp.clip(micro, 0, group_count - 1)
        own_input = lax.dynamic_index_in_dim(inputs, micro_index, 1, keepdims=False)
        entering = jnp.where(section_id == 0, own_input, received)
        flat_rows = entering.reshape(row_count, model_width).astype(jnp.float32)
        normed = layer_norm(flat_rows, gains[0], biases[0]).astype(jnp.bfloat16)
        mixed = jnp.dot(normed, w_qkv, preferred_element_type=jnp.float32).astype(jnp.bfloat16)
        queries = mixed[:, :model_width].reshape(seq_count, block_len, head_count, HEAD)
        fresh = jnp.swapaxes(
            mixed[:, model_width:].reshape(seq_count, block_len, 2 * model_width), 0, 1
        )
        updated = lax.dynamic_update_index_in_dim(cache, fresh, micro_index, 2)
        cache = jnp.where(active, updated, cache)
        query_pos = (
            micro_index * group_len + ctx_id * block_len + jnp.arange(block_len, dtype=jnp.int32)
        )
        start_state = (
            jnp.full((seq_count, block_len, head_count), -1e30, jnp.float32),
            jnp.zeros((seq_count, block_len, head_count), jnp.float32),
            jnp.zeros((seq_count, block_len, head_count, HEAD), jnp.float32),
        )
        row_max, row_sum, accum = fold_keys(
            start_state,
            lax.all_gather(cache, "ctx", axis=0, tiled=True),
            jnp.int32(0),
            queries,
            query_pos,
            group_len,
        )
        attended = accum / row_sum[..., None]
        log_total = row_max + jnp.log(row_sum)
        att_low = attended.reshape(row_count, model_width).astype(jnp.bfloat16)
        middle = flat_rows + jnp.dot(att_low, w_out, preferred_element_type=jnp.float32)
        normed2 = layer_norm(middle, gains[1], biases[1]).astype(jnp.bfloat16)
        upper = jnp.dot(normed2, w_up, preferred_element_type=jnp.float32)
        hidden = gelu_tanh(upper).astype(jnp.bfloat16)
        leaving = (middle + jnp.dot(hidden, w_down, preferred_element_type=jnp.float32)).astype(
            jnp.bfloat16
        )
        leaving = leaving.reshape(seq_count, block_len, model_width)
        in_store = store_at(in_store, entering, micro_index, active)
        query_store = store_at(query_store, queries, micro_index, active)
        att_store = store_at(att_store, attended, micro_index, active)
        total_store = store_at(total_store, log_total, micro_index, active)
        middle_store = store_at(middle_store, middle, micro_index, active)
        upper_store = store_at(upper_store, upper, micro_index, active)
        out_store = store_at(out_store, leaving, micro_index, active)
        if tick_no < group_count:
            received = passed_along(leaving, "section", 1)
    key_acc = jnp.zeros((block_len, seq_count, group_count, 2 * model_width), jnp.float32)
    grad_qkv = jnp.zeros((model_width, 3 * model_width), jnp.float32)
    grad_out = jnp.zeros((model_width, model_width), jnp.float32)
    grad_up = jnp.zeros((model_width, ff_width), jnp.float32)
    grad_down = jnp.zeros((ff_width, model_width), jnp.float32)
    grad_gain = jnp.zeros((2, model_width), jnp.float32)
    grad_bias = jnp.zeros((2, model_width), jnp.float32)
    grad_store = jnp.zeros((group_count, seq_count, block_len, model_width), jnp.bfloat16)
    coming = jnp.zeros((seq_count, block_len, model_width), jnp.bfloat16)
    for tick_no in range(group_count + 1):
        micro = group_count - tick_no - section_id
        active = (micro >= 0) & (micro < group_count)
        active_weight = active.astype(jnp.float32)
        micro_index = jnp.clip(micro, 0, group_count - 1)
        own_cot = lax.dynamic_index_in_dim(cotangent, micro_index, 1, keepdims=False)
        d_out = (
            jnp.where(section_id == 1, own_cot, coming)
            .reshape(row_count, model_width)
            .astype(jnp.float32)
        )
        flat_rows = in_store[micro_index].reshape(row_count, model_width).astype(jnp.float32)
        queries = query_store[micro_index]
        attended = att_store[micro_index]
        log_total = total_store[micro_index]
        middle = middle_store[micro_index]
        upper = upper_store[micro_index]
        normed2_full, norm2_back = jax.vjp(
            lambda v, g, b: layer_norm(v, g, b), middle, gains[1], biases[1]
        )
        normed2 = normed2_full.astype(jnp.bfloat16)
        hidden_full, gelu_back = jax.vjp(gelu_tanh, upper)
        hidden = hidden_full.astype(jnp.bfloat16)
        d_branch = d_out.astype(jnp.bfloat16)
        grad_down = grad_down + active_weight * jnp.dot(
            hidden.T, d_branch, preferred_element_type=jnp.float32
        )
        d_hidden = jnp.dot(d_branch, w_down.T, preferred_element_type=jnp.float32)
        d_upper = gelu_back(d_hidden)[0].astype(jnp.bfloat16)
        grad_up = grad_up + active_weight * jnp.dot(
            normed2.T, d_upper, preferred_element_type=jnp.float32
        )
        d_normed2 = jnp.dot(d_upper, w_up.T, preferred_element_type=jnp.float32)
        d_mid_norm, d_gain2, d_bias2 = norm2_back(d_normed2)
        d_middle = d_out + d_mid_norm
        att_low = attended.reshape(row_count, model_width).astype(jnp.bfloat16)
        d_att = d_middle.astype(jnp.bfloat16)
        grad_out = grad_out + active_weight * jnp.dot(
            att_low.T, d_att, preferred_element_type=jnp.float32
        )
        d_attended = jnp.dot(d_att, w_out.T, preferred_element_type=jnp.float32).astype(
            jnp.bfloat16
        )
        d_attended = d_attended.reshape(seq_count, block_len, head_count, HEAD)
        row_delta = jnp.sum(d_attended.astype(jnp.float32) * attended, axis=-1)
        query_pos = (
            micro_index * group_len + ctx_id * block_len + jnp.arange(block_len, dtype=jnp.int32)
        )
        whole = lax.all_gather(cache, "ctx", axis=0, tiled=True)
        d_queries, unused = backward_keys(
            whole, queries, query_pos, log_total, row_delta, d_attended, group_len
        )
        all_queries, all_d_att = (
            lax.all_gather(queries, "ctx", axis=1, tiled=True),
            lax.all_gather(d_attended, "ctx", axis=1, tiled=True),
        )
        all_totals, all_deltas = (
            lax.all_gather(log_total, "ctx", axis=1, tiled=True),
            lax.all_gather(row_delta, "ctx", axis=1, tiled=True),
        )
        shares = owner_terms(
            cache, all_queries, all_d_att, all_totals, all_deltas, micro_index, ctx_id, group_len
        )
        key_acc = key_acc + active_weight * shares
        d_pair = jnp.swapaxes(
            lax.dynamic_index_in_dim(key_acc, micro_index, 2, keepdims=False), 0, 1
        )
        d_mixed = jnp.concatenate(
            [d_queries.reshape(row_count, model_width), d_pair.reshape(row_count, 2 * model_width)],
            axis=-1,
        ).astype(jnp.bfloat16)
        normed_full, norm1_back = jax.vjp(
            lambda v, g, b: layer_norm(v, g, b), flat_rows, gains[0], biases[0]
        )
        normed = normed_full.astype(jnp.bfloat16)
        grad_qkv = grad_qkv + active_weight * jnp.dot(
            normed.T, d_mixed, preferred_element_type=jnp.float32
        )
        d_normed = jnp.dot(d_mixed, w_qkv.T, preferred_element_type=jnp.float32)
        d_flat_norm, d_gain1, d_bias1 = norm1_back(d_normed)
        grad_gain = grad_gain + active_weight * jnp.stack([d_gain1, d_gain2])
        grad_bias = grad_bias + active_weight * jnp.stack([d_bias1, d_bias2])
        d_entering = (
            (d_middle + d_flat_norm).astype(jnp.bfloat16).reshape(seq_count, block_len, model_width)
        )
        grad_store = store_at(grad_store, d_entering, micro_index, active)
        if tick_no < group_count:
            coming = passed_along(d_entering, "section", -1)
    sums = (
        lax.psum_scatter(grad_qkv, ("ctx", "shard"), scatter_dimension=0, tiled=True),
        lax.psum_scatter(grad_out, ("ctx", "shard"), scatter_dimension=0, tiled=True),
        lax.psum_scatter(grad_up, ("ctx", "shard"), scatter_dimension=0, tiled=True),
        lax.psum_scatter(grad_down, ("ctx", "shard"), scatter_dimension=1, tiled=True),
        lax.psum_scatter(grad_gain, ("ctx", "shard"), scatter_dimension=1, tiled=True),
        lax.psum_scatter(grad_bias, ("ctx", "shard"), scatter_dimension=1, tiled=True),
    )
    layer_outputs = jnp.swapaxes(out_store, 0, 1)[None]
    input_grads = jnp.swapaxes(grad_store, 0, 1)[None]
    return (
        layer_outputs,
        input_grads,
        sums[0][None],
        sums[1][None],
        sums[2][None],
        sums[3][None],
        sums[4][None],
        sums[5][None],
    )


def solution(mesh):
    in_specs = (
        P("shard", None, "ctx", None),
        P("shard", None, "ctx", None),
        P("section", "shard", None),
        P("section", "shard", None),
        P("section", "shard", None),
        P("section", None, "shard"),
        P("section", None, "shard"),
        P("section", None, "shard"),
    )
    out_specs = (
        P("section", "shard", None, "ctx", None),
        P("section", "shard", None, "ctx", None),
        P("section", ("ctx", "shard"), None),
        P("section", ("ctx", "shard"), None),
        P("section", ("ctx", "shard"), None),
        P("section", None, ("ctx", "shard")),
        P("section", None, ("ctx", "shard")),
        P("section", None, ("ctx", "shard")),
    )
    return jax.shard_map(shards, mesh=mesh, in_specs=in_specs, out_specs=out_specs, check_vma=False)
```

profile of v0, /device:TPU:24, one launch (start us, length us, event | category | flops | bytes accessed | tf_op | source)
XLA Modules:
  0.0 2666.2 jit_solution(1780912114888641613)
XLA Ops:
  8.9 18.7 all-gather.1
  28.4 24.8 all-gather
  54.1 17.8 slice_reduce_fusion
  71.9 18.0 slice_reduce_fusion.1
  90.0 58.9 %all-gather.41.cloned.1.call-done = bf16[1,1088,3264]{2,1,0:T(8,128)(2,1)} async-done(((bf16[1,272,3264]{2,1,0:T(8,128)(2,1)}), bf16[1,1088,3264]{2,1,0:T(8,128)(2,1)}) %all-gather.41.cloned.1.call-update) | async-done | bytes 7102480 | tf_op jit(solution)/shard_map/all_gather | solution.py:189
  148.8 6.3 fusion.48
  160.6 51.5 %all-gather.29.cloned.1.call-done = bf16[512,1,2,2176]{0,3,2,1:T(8,128)(2,1)} async-done(((bf16[128,1,2,2176]{0,3,2,1:T(8,128)(2,1)}), bf16[512,1,2,2176]{0,3,2,1:T(8,128)(2,1)}) %all-gather.29.cloned.1.call-update) | async-done | bytes 4456464 | tf_op jit(solution)/shard_map/all_gather | solution.py:233
  222.3 41.8 %all-gather.43.cloned.1.call-done = bf16[1,1088,1088]{2,1,0:T(8,128)(2,1)} async-done(((bf16[1,272,1088]{2,1,0:T(8,128)(2,1)}), bf16[1,1088,1088]{2,1,0:T(8,128)(2,1)}) %all-gather.43.cloned.1.call-update) | async-done | bytes 2367504 | tf_op jit(solution)/shard_map/all_gather | solution.py:190
  267.1 163.8 %all-gather.45.cloned.1.call-done = bf16[1,1088,4352]{2,1,0:T(8,128)(2,1)} async-done(((bf16[1,272,4352]{2,1,0:T(8,128)(2,1)}), bf16[1,1088,4352]{2,1,0:T(8,128)(2,1)}) %all-gather.45.cloned.1.call-update) | async-done | bytes 9469968 | tf_op jit(solution)/shard_map/all_gather | solution.py:191
  433.3 7.5 bitcast_dynamic-update-slice_fusion
  440.9 157.0 %all-gather.47.cloned.1.call-done = bf16[1,4352,1088]{1,2,0:T(8,128)(2,1)} async-done(((bf16[1,4352,272]{1,2,0:T(8,128)(2,1)}), bf16[1,4352,1088]{1,2,0:T(8,128)(2,1)}) %all-gather.47.cloned.1.call-update) | async-done | bytes 9469968 | tf_op jit(solution)/shard_map/all_gather | solution.py:192
  597.9 7.4 bitcast_dynamic-update-slice_fusion.4
  608.9 6.4 fusion.51
  618.5 54.9 %all-gather.31.cloned.1.call-done = bf16[512,1,2,2176]{0,3,2,1:T(8,128)(2,1)} async-done(((bf16[128,1,2,2176]{0,3,2,1:T(8,128)(2,1)}), bf16[512,1,2,2176]{0,3,2,1:T(8,128)(2,1)}) %all-gather.31.cloned.1.call-update) | async-done | bytes 4456464 | tf_op jit(solution)/shard_map/all_gather | solution.py:233
  686.0 5.1 fusion.314
  715.0 14.2 all-gather.49.cloned.1.call-done
  736.4 21.6 all-gather.51.cloned.1.call-done
  765.1 21.7 all-gather.53.cloned.1.call-done
  793.9 49.8 %all-gather.33.cloned.1.call-done = bf16[512,1,2,2176]{0,3,2,1:T(8,128)(2,1)} async-done(((bf16[128,1,2,2176]{0,3,2,1:T(8,128)(2,1)}), bf16[512,1,2,2176]{0,3,2,1:T(8,128)(2,1)}) %all-gather.33.cloned.1.call-update) | async-done | bytes 4456464 | tf_op jit(solution)/shard_map/all_gather | solution.py:233
  874.6 5.7 fusion.313
  896.5 9.0 all-gather.7
  905.5 8.9 all-gather.8
  914.4 8.3 all-gather.10
  923.3 8.0 all-gather.13
  931.3 9.5 convolution_multiply_fusion.2
  945.1 5.4 fusion.377
  950.5 5.8 fusion.516
  956.4 9.9 convolution_multiply_fusion.5
  966.3 7.1 fusion.186
  977.0 5.8 fusion.483
  988.4 5.8 fusion.480
  996.7 5.3 fusion.629
  1005.6 7.7 convolution_multiply_fusion.8
  1026.9 8.9 all-gather.11
  1037.6 5.5 fusion.369
  1043.0 5.8 fusion.513
  1048.8 12.8 fusion.5
  1061.6 5.6 fusion.11
  1067.2 11.8 fusion.7
  1083.5 5.8 fusion.495
  1095.9 5.8 fusion.492
  1105.2 6.0 fusion.641
  1113.8 9.9 fusion.9
  1125.7 7.2 fusion.209
  1140.5 7.4 all-gather.14
  1148.0 12.5 fusion.4
  1160.5 410.2 %fusion.3 = f32[4352,72]{0,1:T(8,128)} fusion(f32[4352,1088]{0,1:T(8,128)} %fusion.4), kind=kCustom, calls=%all-reduce-scatter.3 | all-reduce-scatter fusion | flops 5013505 | bytes 20193792
  1573.1 7.1 collective-permute-start.9
  1581.4 5.3 fusion.361
  1586.7 5.8 fusion.510
  1592.6 5.7 fusion.10
  1598.2 12.0 fusion.6
  1610.2 9.4 concatenate.84
  1627.9 5.1 fusion.507
  1638.8 5.4 fusion.504
  1647.1 6.5 fusion.653
  1653.6 9.5 fusion.8
  1663.2 834.1 %fusion.885 = (f32[72,3264]{1,0:T(8,128)S(1)}, f32[80,1088]{1,0:T(8,128)S(1)}, f32[72,4352]{1,0:T(8,128)S(1)}) fusion(f32[1088,3264]{1,0:T(8,128)} %fusion.8, f32[1088,1088]{1,0:T(8,128)} %fusion.10, f32[1088,4352]{1,0:T(8,128)} %fusion.6), kind=kCustom, calls=%all-reduce-scatter.4 | all-reduce-scatter fusion | flops 10166274 | bytes 40421888
  2497.3 5.9 collective-permute-start.6
  2511.4 4.9 collective-permute-start.7
  2517.5 5.2 collective-permute-start.8
  2524.1 105.7 %all-reduce.10 = (f32[2,1088]{1,0:T(2,128)S(1)}, f32[2,1088]{1,0:T(2,128)S(1)}) all-reduce(f32[2,1088]{1,0:T(2,128)S(1)} %fusion.792, f32[2,1088]{1,0:T(2,128)S(1)} %fusion.794), channel_id=21, replica_groups=mesh['section'=2,'ctx'=4,'shard'=4] {'ctx','shard'}, use_global_device_ids=true, to_apply=%region_61.62.clone | all-reduce | flops 4352 | bytes 34816
  2636.5 7.2 concatenate.81
  2646.9 8.6 concatenate.83
  (660 shorter events, 238.9 us)
Async XLA Ops:
  7.2 21.0 copy-start.161
  7.2 141.6 %all-gather.41.cloned.1.call-start = ((), (), s32[]{:S(2)}) async-start(), calls=%async_computation.6 | async-start | bytes 9052160 | tf_op jit(solution)/shard_map/all_gather | solution.py:189
  7.9 45.8 %copy-start.25 = (bf16[1,2,128,1088]{2,3,1,0:T(8,128)(2,1)S(1)}, bf16[1,2,128,1088]{2,3,1,0:T(8,128)(2,1)}, u32[]{:S(2)}) copy-start(bf16[1,2,128,1088]{2,3,1,0:T(8,128)(2,1)} %param.8) | copy-start | bytes 1671172
  7.9 204.2 %all-gather.29.cloned.1.call-start = ((), (), s32[]{:S(2)}) async-start(), calls=%async_computation | async-start | bytes 5570560 | tf_op jit(solution)/shard_map/all_gather | solution.py:233
  156.5 107.7 %all-gather.43.cloned.1.call-start = ((), (), s32[]{:S(2)}) async-start(), calls=%async_computation.7 | async-start | bytes 3133440 | tf_op jit(solution)/shard_map/all_gather | solution.py:190
  157.2 273.7 %all-gather.45.cloned.1.call-start = ((), (), s32[]{:S(2)}) async-start(), calls=%async_computation.8 | async-start | bytes 11837440 | tf_op jit(solution)/shard_map/all_gather | solution.py:191
  157.8 440.1 %all-gather.47.cloned.1.call-start = ((), (), s32[]{:S(2)}) async-start(), calls=%async_computation.9 | async-start | bytes 11837440 | tf_op jit(solution)/shard_map/all_gather | solution.py:192
  158.4 515.1 %all-gather.31.cloned.1.call-start = ((), (), s32[]{:S(2)}) async-start(), calls=%async_computation.1 | async-start | bytes 5570560 | tf_op jit(solution)/shard_map/all_gather | solution.py:233
  159.8 59.4 %copy-start.72 = (pred[128,512]{0,1:T(8,128)(4,1)}, pred[128,512]{0,1:T(8,128)(4,1)S(1)}, u32[]{:S(2)}) copy-start(pred[128,512]{0,1:T(8,128)(4,1)S(1)} %get-tuple-element.378) | copy-start | bytes 196612
  159.8 60.5 %copy-start.74 = (pred[128,512]{0,1:T(8,128)(4,1)}, pred[128,512]{0,1:T(8,128)(4,1)S(1)}, u32[]{:S(2)}) copy-start(pred[128,512]{0,1:T(8,128)(4,1)S(1)} %get-tuple-element.373) | copy-start | bytes 196612
  159.9 521.2 %copy-start.76 = (pred[128,512]{0,1:T(8,128)(4,1)}, pred[128,512]{0,1:T(8,128)(4,1)S(1)}, u32[]{:S(2)}) copy-start(pred[128,512]{0,1:T(8,128)(4,1)S(1)} %get-tuple-element.379) | copy-start | bytes 196612
  605.3 3.1 collective-permute-start
  617.5 111.8 %all-gather.49.cloned.1.call-start = ((), (), s32[]{:S(2)}) async-start(), calls=%async_computation.10 | async-start | bytes 1392640 | tf_op jit(solution)/shard_map/all_gather | solution.py:321
  694.4 2.7 collective-permute-start.1
  702.2 55.8 %all-gather.51.cloned.1.call-start = ((), (), s32[]{:S(2)}) async-start(), calls=%async_computation.11 | async-start | bytes 1392640 | tf_op jit(solution)/shard_map/all_gather | solution.py:321
  702.9 83.9 %all-gather.53.cloned.1.call-start = ((), (), s32[]{:S(2)}) async-start(), calls=%async_computation.12 | async-start | bytes 1392640 | tf_op jit(solution)/shard_map/all_gather | solution.py:321
  703.7 140.0 %all-gather.33.cloned.1.call-start = ((), (), s32[]{:S(2)}) async-start(), calls=%async_computation.2 | async-start | bytes 5570560 | tf_op jit(solution)/shard_map/all_gather | solution.py:233
  705.0 268.4 %all-gather.35.cloned.1.call-start = ((), (), s32[]{:S(2)}) async-start(), calls=%async_computation.3 | async-start | bytes 1392640 | tf_op jit(solution)/shard_map/all_gather | solution.py:322
  846.5 23.8 copy-start.68
  853.2 12.8 copy-start.6
  853.2 15.9 copy-start.69
  874.3 14.3 copy-start.126
  874.5 14.1 copy-start.145
  890.6 188.5 %all-gather.37.cloned.1.call-start = ((), (), s32[]{:S(2)}) async-start(), calls=%async_computation.4 | async-start | bytes 1392640 | tf_op jit(solution)/shard_map/all_gather | solution.py:322
  890.6 32.0 %copy-start.162 = (f32[128]{0:T(128)S(1)}, f32[128]{0:T(128)}, u32[]{:S(2)}) copy-start(f32[128]{0:T(128)} %get-tuple-element.234) | copy-start | bytes 1540
  890.6 40.7 %copy-start.48 = (bf16[1,2,128,1088]{2,3,1,0:T(8,128)(2,1)S(1)}, bf16[1,2,128,1088]{2,3,1,0:T(8,128)(2,1)}, u32[]{:S(2)}) copy-start(bf16[1,2,128,1088]{2,3,1,0:T(8,128)(2,1)} %param.9) | copy-start | bytes 1671172
  894.0 29.2 %copy-start.121 = (f32[128,17]{0,1:T(8,128)}, f32[128,17]{0,1:T(8,128)S(1)}, u32[]{:S(2)}) copy-start(f32[128,17]{0,1:T(8,128)S(1)} %fusion.665) | copy-start | bytes 26116
  896.5 26.8 %copy-start.118 = (f32[1,1,128,17]{2,3,1,0:T(8,128)}, f32[1,1,128,17]{2,3,1,0:T(8,128)S(1)}, u32[]{:S(2)}) copy-start(f32[1,1,128,17]{2,3,1,0:T(8,128)S(1)} %get-tuple-element.347) | copy-start | bytes 26116
  896.5 26.8 %copy-start.119 = (f32[1,1,128,17]{2,3,1,0:T(8,128)}, f32[1,1,128,17]{2,3,1,0:T(8,128)S(1)}, u32[]{:S(2)}) copy-start(f32[1,1,128,17]{2,3,1,0:T(8,128)S(1)} %get-tuple-element.348) | copy-start | bytes 26116
  896.5 44.3 %copy-start.120 = (f32[1,1,128,17]{2,3,1,0:T(8,128)}, f32[1,1,128,17]{2,3,1,0:T(8,128)S(1)}, u32[]{:S(2)}) copy-start(f32[1,1,128,17]{2,3,1,0:T(8,128)S(1)} %get-tuple-element.349) | copy-start | bytes 26116
  956.3 62.9 %copy-start.141 = (f32[128]{0:T(128)}, f32[128]{0:T(128)S(1)}, u32[]{:S(2)}) copy-start(f32[128]{0:T(128)S(1)} %broadcast_multiply_fusion.1) | copy-start | bytes 1540
  1003.1 11.5 slice-start.20
  1003.9 10.7 slice-start.21
  1003.9 10.7 slice-start.22
  1003.9 10.6 collective-permute-start.2
  1005.6 13.7 slice-start.6
  1005.6 13.7 slice-start.7
  1022.1 13.7 copy-start.164
  1024.1 13.5 copy-start.79
  1025.6 597.7 %all-gather.39.cloned.1.call-start = ((), (), s32[]{:S(2)}) async-start(), calls=%async_computation.5 | async-start | bytes 1392640 | tf_op jit(solution)/shard_map/all_gather | solution.py:322
  1026.9 10.6 copy-start.123
  1048.8 12.8 copy-start.61
  1048.8 12.8 copy-start.66
  1067.2 11.8 copy-start.112
  1105.2 27.7 %slice-start.9 = ((s8[9469952]{0:T(1024)(128)(4,1)}), s8[4194304]{0:T(1024)(128)(4,1)S(1)}, s32[]{:S(2)}) async-start(s8[9469952]{0:T(1024)(128)(4,1)} %bitcast.1656), calls=%async_computation.22 | async-start | bytes 8388608
  1112.1 11.5 copy-start.36
  1112.2 13.5 copy-start.50
  1112.2 20.8 slice-start.10
  1112.2 20.8 slice-start.11
  1112.2 13.5 collective-permute-start.3
  1140.5 20.0 copy-start.122
  1570.8 10.6 copy-start.75
  1573.1 37.1 %collective-permute-start.9 = (f32[4352,60]{0,1:T(8,128)}, f32[4352,60]{0,1:T(8,128)}, u32[]{:S(2)}, u32[]{:S(2)}) collective-permute-start(f32[4352,60]{0,1:T(8,128)} %slice.281), channel_id=1, source_target_pairs={{0,1},{1,2},{2,3},{3,4},{4,5},{5,6},{6,7},{7,8},{8,9},{9,10},{10,1... | collective-permute-start | bytes 3133448
  2497.3 20.2 copy-start.59
  2497.3 133.8 %collective-permute-start.6 = (f32[80,1088]{1,0:T(8,128)S(1)}, f32[80,1088]{1,0:T(8,128)}, u32[]{:S(2)}, u32[]{:S(2)}) collective-permute-start(f32[80,1088]{1,0:T(8,128)S(1)} %get-tuple-element.289), channel_id=1, source_target_pairs={{0,2},{1,3},{2,4},{3,5},{4,6},{5,7},{6,8},{7,9},{8,10},{9,11},{10,... | collective-permute-start | bytes 1044488
  2503.2 127.9 %collective-permute-start.5 = (f32[80,1088]{1,0:T(8,128)S(1)}, f32[80,1088]{1,0:T(8,128)}, u32[]{:S(2)}, u32[]{:S(2)}) collective-permute-start(f32[80,1088]{1,0:T(8,128)S(1)} %get-tuple-element.289), channel_id=1, source_target_pairs={{0,1},{1,2},{2,3},{3,4},{4,5},{5,6},{6,7},{7,8},{8,9},{9,10},{10,1... | collective-permute-start | bytes 1044488
  2505.2 17.5 copy-start.29
  2505.2 17.5 copy-start.37
  2505.2 17.5 copy-start.52
  2505.2 17.5 copy-start.84
  2505.2 17.5 copy-start.160
  2507.8 128.7 %collective-permute-start.4 = (f32[60,3264]{1,0:T(8,128)}, f32[60,3264]{1,0:T(8,128)}, u32[]{:S(2)}, u32[]{:S(2)}) collective-permute-start(f32[60,3264]{1,0:T(8,128)} %slice.278), channel_id=1, source_target_pairs={{0,1},{1,2},{2,3},{3,4},{4,5},{5,6},{6,7},{7,8},{8,9},{9,10},{10,1... | collective-permute-start | bytes 2350088
  2511.4 119.7 %collective-permute-start.7 = (f32[20,1088]{1,0:T(8,128)S(1)}, f32[20,1088]{1,0:T(8,128)}, u32[]{:S(2)}, u32[]{:S(2)}) collective-permute-start(f32[20,1088]{1,0:T(8,128)S(1)} %slice.279), channel_id=1, source_target_pairs={{0,3},{1,4},{2,5},{3,6},{4,7},{5,8},{6,9},{7,10},{8,11},{9,12},{10... | collective-permute-start | bytes 261128
  2517.5 129.4 %collective-permute-start.8 = (f32[60,4352]{1,0:T(8,128)}, f32[60,4352]{1,0:T(8,128)}, u32[]{:S(2)}, u32[]{:S(2)}) collective-permute-start(f32[60,4352]{1,0:T(8,128)} %slice.280), channel_id=1, source_target_pairs={{0,1},{1,2},{2,3},{3,4},{4,5},{5,6},{6,7},{7,8},{8,9},{9,10},{10,1... | collective-permute-start | bytes 3133448
  (153 other events, 631.3 us)
Sparse Core Ops, SparseCore 0:
  9.6 139.2 all-gather.40
  156.6 55.4 all-gather.28
  213.7 50.3 all-gather.42
  265.6 165.3 all-gather.44
  432.4 165.4 all-gather.46
  617.6 55.8 all-gather.30
  702.3 26.9 all-gather.48
  731.1 26.8 all-gather.50
  759.9 26.8 all-gather.52
  789.0 54.6 all-gather.32
  890.7 27.5 all-gather.34
  1025.7 27.3 all-gather.36
  1139.4 27.4 all-gather.38
where the time goes:
time: 2690 us; the launch traced here: 2670 us
  blocking collectives  1440 us (54%)
  waiting for transfers between devices  641 us (24%)
  matrix products  361 us (13%)
  local copies, waits for them, and re-layouts  125 us (5%)
  other arithmetic  39.3 us (1%)
  starting transfers between devices  36.2 us (1%)
    unnamed x3, blocking collectives  1350 us
    all_gather x1, waiting for transfers between devices, shards(): lax.all_gather(up_weight[0], 'shard', axis=0, tiled=True)  164 us
    all_gather x1, waiting for transfers between devices, shards(): lax.all_gather(down_weight[0], 'shard', axis=1, tiled=True)  157 us
    all_gather x3, waiting for transfers between devices, shards(): lax.all_gather(cache, 'ctx', axis=0, tiled=True)  156 us
    unnamed x405, local copies, waits for them, and re-layouts  60.3 us
    all_gather x1, waiting for transfers between devices, shards(): lax.all_gather(qkv_weight[0], 'shard', axis=0, tiled=True)  58.9 us
    all_gather x3, waiting for transfers between devices, shards(): lax.all_gather(queries, 'ctx', axis=1, tiled=True)  57.6 us
  transfers between devices with their start and end apart: 23, of which 12 were waited for; matrix products, arithmetic and copies ran while one was open for 26% of the time, Pallas kernels for 0%

commit v1 on v0

--- a/solution.py
+++ b/solution.py
@@ -1,13 +1,353 @@
+import functools
+
 import jax
 import jax.numpy as jnp
 from jax import lax
+from jax.experimental import pallas as pl
+from jax.experimental.pallas import tpu as pltpu
 from jax.sharding import PartitionSpec as P
 
 HEAD = 64
-
+LANES = 128
+ROWS = 8
+NEG = -1e30
 
 eps_norm = 1e-05
 score_scale = 0.125
+f32 = jnp.float32
+bf16 = jnp.bfloat16
+
+
+def up_to(width, step):
+    return -(-width // step) * step
+
+
+def dot(a, b, dims):
+    return lax.dot_general(a, b, (dims, ((), ())), preferred_element_type=f32)
+
+
+def mm(a, b):
+    return dot(a, b, ((1,), (0,)))
+
+
+def mm_t(a, b):
+    return dot(a, b, ((1,), (1,)))
+
+
+def t_mm(a, b):
+    return dot(a, b, ((0,), (0,)))
+
+
+def attention_masks(core, half):
+    row = lax.broadcasted_iota(jnp.int32, (2 * half, 2 * half), 0)
+    col = lax.broadcasted_iota(jnp.int32, (2 * half, 2 * half), 1)
+    row_slice, col_slice = row // half, col // half
+    own = (col_slice < row_slice) | ((col_slice == row_slice) & (col <= row))
+    other = (col_slice < row_slice) | ((col_slice == row_slice) & (core == 1))
+    return jnp.where(jnp.stack([own, other]), 0.0, NEG).astype(f32)
+
+
+def attention_forward_kernel(half, mask_ref, q_ref, k0_ref, k1_ref, v0_ref, v1_ref, o_ref, ob_ref, lse_ref):
+    pair = pl.program_id(0)
+    tokens = q_ref.shape[0]
+    block = 2 * half
+
+    @pl.when(pair == 0)
+    def _():
+        lse_ref[...] = jnp.zeros_like(lse_ref)
+
+    lane = lax.broadcasted_iota(jnp.int32, (block, LANES), 1)
+    for u in range(tokens // block):
+        rows = pl.ds(u * block, block)
+        keys = (u + 1) * block
+        outs = []
+        for h in range(2):
+            cols = pl.ds(h * HEAD, HEAD)
+            q = q_ref[rows, cols]
+            scores = []
+            for part, k_ref in enumerate((k0_ref, k1_ref)):
+                s = mm_t(q, k_ref[pl.ds(0, keys), cols])
+                last = s[:, keys - block :] + mask_ref[part]
+                scores.append(last if u == 0 else jnp.concatenate([s[:, : keys - block], last], axis=1))
+            top = jnp.maximum(
+                jnp.max(scores[0], axis=1, keepdims=True), jnp.max(scores[1], axis=1, keepdims=True)
+            )
+            total, acc = 0.0, 0.0
+            for s, v_ref in zip(scores, (v0_ref, v1_ref)):
+                p = jnp.exp(s - top)
+                total = total + jnp.sum(p, axis=1, keepdims=True)
+                acc = acc + mm(p.astype(bf16), v_ref[pl.ds(0, keys), cols])
+            outs.append(acc / total)
+            lse = top + jnp.log(total)
+            lse_ref[rows, :] = jnp.where(lane == 2 * pair + h, lse, lse_ref[rows, :])
+        out = jnp.concatenate(outs, axis=1)
+        o_ref[rows, :] = out
+        ob_ref[rows, :] = out.astype(bf16)
+
+
+def attention_forward(mask, q, k0, k1, v0, v1, half):
+    tokens, width = q.shape
+    spec = pl.BlockSpec((tokens, LANES), lambda i: (0, i))
+    return pl.pallas_call(
+        functools.partial(attention_forward_kernel, half),
+        grid=(width // LANES,),
+        in_specs=[pl.BlockSpec(mask.shape, lambda i: (0, 0, 0))] + [spec] * 5,
+        out_specs=[spec, spec, pl.BlockSpec((tokens, LANES), lambda i: (0, 0))],
+        out_shape=[
+            jax.ShapeDtypeStruct((tokens, width), f32),
+            jax.ShapeDtypeStruct((tokens, width), bf16),
+            jax.ShapeDtypeStruct((tokens, LANES), f32),
+        ],
+        name="attention_forward",
+    )(mask, q, k0, k1, v0, v1)
+
+
+def attention_backward_kernel(
+    half, mask_ref, q_ref, k0_ref, k1_ref, v0_ref, v1_ref, da_ref, o_ref, lse_ref,
+    dq_ref, dk0_ref, dk1_ref, dv0_ref, dv1_ref, acc_ref,
+):
+    pair = pl.program_id(0)
+    tokens = q_ref.shape[0]
+    block = 2 * half
+    lane = lax.broadcasted_iota(jnp.int32, (block, LANES), 1)
+    acc_ref[...] = jnp.zeros_like(acc_ref)
+    for u in range(tokens // block):
+        rows = pl.ds(u * block, block)
+        keys = (u + 1) * block
+        dqs = []
+        for h in range(2):
+            cols = pl.ds(h * HEAD, HEAD)
+            q, da = q_ref[rows, cols], da_ref[rows, cols]
+            q_t, da_t = q.T, da.T
+            lse = jnp.sum(jnp.where(lane == 2 * pair + h, lse_ref[rows, :], 0.0), axis=1, keepdims=True)
+            delta = jnp.sum(da.astype(f32) * o_ref[rows, cols], axis=1, keepdims=True)
+            dq = 0.0
+            for part, (k_ref, v_ref) in enumerate(((k0_ref, v0_ref), (k1_ref, v1_ref))):
+                k, v = k_ref[pl.ds(0, keys), cols], v_ref[pl.ds(0, keys), cols]
+                s = mm_t(q, k)
+                last = s[:, keys - block :] + mask_ref[part]
+                s = last if u == 0 else jnp.concatenate([s[:, : keys - block], last], axis=1)
+                p = jnp.exp(s - lse)
+                ds = (p * (mm_t(da, v) - delta)).astype(bf16)
+                dq = dq + mm(ds, k)
+                acc_ref[part, 0, h, :, pl.ds(0, keys)] += mm(q_t, ds)
+                acc_ref[part, 1, h, :, pl.ds(0, keys)] += mm(da_t, p.astype(bf16))
+            dqs.append(dq * score_scale)
+        dq_ref[rows, :] = jnp.concatenate(dqs, axis=1).astype(bf16)
+    for part, (dk_ref, dv_ref) in enumerate(((dk0_ref, dv0_ref), (dk1_ref, dv1_ref))):
+        for which, ref in enumerate((dk_ref, dv_ref)):
+            both = jnp.concatenate([acc_ref[part, which, 0], acc_ref[part, which, 1]], axis=0)
+            ref[...] = both.T.astype(ref.dtype)
+
+
+def attention_backward(mask, q, k0, k1, v0, v1, da, o, lse, half):
+    tokens, width = q.shape
+    spec = pl.BlockSpec((tokens, LANES), lambda i: (0, i))
+    whole = pl.BlockSpec((tokens, LANES), lambda i: (0, 0))
+    shape = lambda t: jax.ShapeDtypeStruct((tokens, width), t)
+    return pl.pallas_call(
+        functools.partial(attention_backward_kernel, half),
+        grid=(width // LANES,),
+        in_specs=[pl.BlockSpec(mask.shape, lambda i: (0, 0, 0))] + [spec] * 7 + [whole],
+        out_specs=[spec] * 5,
+        out_shape=[shape(bf16), shape(f32), shape(bf16), shape(f32), shape(bf16)],
+        scratch_shapes=[pltpu.VMEM((2, 2, 2, HEAD, tokens), f32)],
+        name="attention_backward",
+    )(mask, q, k0, k1, v0, v1, da, o, lse)
+
+
+def normalised(values):
+    mean = jnp.mean(values, axis=-1, keepdims=True)
+    centred = values - mean
+    var = jnp.mean(centred * centred, axis=-1, keepdims=True)
+    scale = lax.rsqrt(var + eps_norm)
+    return centred * scale, scale
+
+
+def norm_backward(hat, scale, gain, grad):
+    scaled = grad * gain
+    mean = jnp.mean(scaled, axis=-1, keepdims=True)
+    along = jnp.mean(scaled * hat, axis=-1, keepdims=True)
+    return scale * (scaled - mean - hat * along)
+
+
+def swap_cores(value):
+    return lax.ppermute(value, "section", [(0, 1), (1, 0)])
+
+
+def hop(value, source, target):
+    return lax.ppermute(value, "shard", [(source, target)])
+
+
+def gather_weights(attn_piece, ff_piece):
+    def bring(piece, kind):
+        parts = []
+        for j in range(2):
+            moves = []
+            for layer in range(2):
+                for core in range(2):
+                    moves.append((layer * 4 + 2 * core + j, core * 4 + 2 * layer + kind))
+            parts.append(lax.ppermute(piece, ("section", "shard"), moves))
+        both = jnp.stack(parts)
+        quarters = lax.all_gather(both, "ctx", axis=0)
+        full = lax.all_gather(quarters, "section", axis=1)
+        return full.reshape(4, 4 * piece.shape[0], piece.shape[1])
+
+    return bring(attn_piece, 0), bring(ff_piece, 1)
+
+
+def scatter_grads(grads, kind, section, shard):
+    columns = grads.shape[1]
+    rows = grads.shape[0] // 16
+    terms = grads.reshape(4, 2, 2, rows, columns)
+    terms = lax.psum_scatter(terms, "section", scatter_dimension=1, tiled=False)
+    terms = lax.psum_scatter(terms, "ctx", scatter_dimension=0, tiled=False)
+    total = None
+    for j in range(2):
+        moves = []
+        for layer in range(2):
+            for core in range(2):
+                moves.append((core * 4 + 2 * layer + kind, layer * 4 + 2 * core + j))
+        came = lax.ppermute(terms[j], ("section", "shard"), moves)
+        total = came if total is None else jnp.where(shard % 2 == j, came, total)
+    return total
+
+
+def chain(inputs, cotangent, qkv_weight, out_weight, up_weight, down_weight, norm_gain, norm_bias):
+    section, ctx, shard = lax.axis_index("section"), lax.axis_index("ctx"), lax.axis_index("shard")
+    seq_count, blocks, slice_len, width = inputs.shape
+    half = slice_len // 2
+    tokens = blocks * 4 * half
+    share = width // 4
+    group = share // 4
+    group_pad = up_to(group, ROWS)
+    wide = up_to(width, LANES)
+    ff = up_weight.shape[2]
+    is_attn = shard % 2 == 0
+
+    pad = lambda w: jnp.pad(w, ((0, 0), (0, wide - width)))
+    own_qkv, own_out = qkv_weight[0], out_weight[0]
+    attn_src = jnp.stack([pad(own_qkv[:, i * width : (i + 1) * width]) for i in range(3)] + [pad(own_out)])
+    down_t = down_weight[0].T
+    up0 = up_weight[0]
+    ff_src = jnp.stack([up0[:, : ff // 2], up0[:, ff // 2 :], down_t[:, : ff // 2], down_t[:, ff // 2 :]])
+    w_attn, w_ff = gather_weights(
+        lax.dynamic_index_in_dim(attn_src, ctx, 0, keepdims=False),
+        lax.dynamic_index_in_dim(ff_src, ctx, 0, keepdims=False),
+    )
+    norms = jnp.stack([norm_gain[0], norm_bias[0]])
+    norms = lax.all_gather(lax.all_gather(norms, "shard", axis=2, tiled=True), "section", axis=0)
+    norms = lax.dynamic_index_in_dim(norms, shard // 2, 0, keepdims=False).astype(f32)
+    gain1, gain2, bias1, bias2 = norms[0, 0], norms[0, 1], norms[1, 0], norms[1, 1]
+
+    def bring_tokens(array):
+        own = lax.dynamic_slice_in_dim(array[0], section * half, half, 1)
+        every = lax.all_gather(own, "shard", axis=0)
+        mine = lax.all_to_all(every, "ctx", 0, 0)
+        return jnp.swapaxes(mine, 0, 1).reshape(tokens, width)
+
+    x_first, g_last = bring_tokens(inputs), bring_tokens(cotangent)
+    mask = attention_masks(section, half)
+    feature = lax.broadcasted_iota(jnp.int32, (width, 16 * group_pad), 0)
+    place = lax.broadcasted_iota(jnp.int32, (width, 16 * group_pad), 1)
+    spread = (feature // group * group_pad + feature % group == place).astype(bf16)
+    grouped = lambda v: mm(v, spread).astype(bf16)
+
+    def attn_forward(x):
+        x = x.astype(f32)
+        hat, scale = normalised(x)
+        normed = (hat * gain1 + bias1).astype(bf16)
+        q = (mm(normed, w_attn[0]) * score_scale).astype(bf16)
+        k = mm(normed, w_attn[1]).astype(bf16)
+        v = mm(normed, w_attn[2]).astype(bf16)
+        k1, v1 = swap_cores(k), swap_cores(v)
+        o, ob, lse = attention_forward(mask, q, k, k1, v, v1, half)
+        middle = x + mm(ob[:, :width], w_attn[3])[:, :width]
+        return middle.astype(bf16), (hat, scale, normed, q, k, k1, v, v1, o, ob, lse)
+
+    def ff_forward(middle):
+        middle = middle.astype(f32)
+        hat, scale = normalised(middle)
+        normed = (hat * gain2 + bias2).astype(bf16)
+        upper = [mm(normed, w_ff[i]) for i in range(2)]
+        hidden = [jax.nn.gelu(u, approximate=True).astype(bf16) for u in upper]
+        y = middle + mm_t(hidden[0], w_ff[2]) + mm_t(hidden[1], w_ff[3])
+        return y.astype(bf16), (hat, scale, normed, upper, hidden)
+
+    def ff_backward(g, state):
+        hat, scale, normed, upper, hidden = state
+        d_upper = []
+        for i in range(2):
+            d_hidden = mm(g, w_ff[2 + i])
+            _, back = jax.vjp(lambda u: jax.nn.gelu(u, approximate=True), upper[i])
+            d_upper.append(back(d_hidden)[0].astype(bf16))
+        d_normed = mm_t(d_upper[0], w_ff[0]) + mm_t(d_upper[1], w_ff[1])
+        d_middle = g.astype(f32) + norm_backward(hat, scale, gain2, d_normed)
+        return d_middle.astype(bf16), d_upper, d_normed
+
+    def attn_backward(d_middle, state):
+        hat, scale, normed, q, k, k1, v, v1, o, ob, lse = state
+        d_att = mm_t(jnp.pad(d_middle, ((0, 0), (0, wide - width))), w_attn[3]).astype(bf16)
+        d_att = jnp.pad(d_att, ((0, 0), (0, wide - width)))
+        dq, dk, dk_other, dv, dv_other = attention_backward(mask, q, k, k1, v, v1, d_att, o, lse, half)
+        dk = (dk + swap_cores(dk_other).astype(f32)).astype(bf16)
+        dv = (dv + swap_cores(dv_other).astype(f32)).astype(bf16)
+        d_mixed = (dq, dk, dv)
+        d_normed = mm_t(dq, w_attn[0]) + mm_t(dk, w_attn[1]) + mm_t(dv, w_attn[2])
+        dx = d_middle.astype(f32) + norm_backward(hat, scale, gain1, d_normed)
+        return dx.astype(bf16), d_mixed, d_normed
+
+    middle, _ = attn_forward(x_first)
+    middle0 = hop(middle, 0, 1)
+    y, _ = ff_forward(middle0)
+    x = jnp.where(shard == 0, x_first, hop(y, 1, 2))
+    middle, attn_state = attn_forward(x)
+    middle = jnp.where(shard == 1, middle0, hop(middle, 2, 3))
+    y, ff_state = ff_forward(middle)
+
+    d_middle, _, _ = ff_backward(g_last, ff_state)
+    d_middle1 = hop(d_middle, 3, 2)
+    dx, _, _ = attn_backward(d_middle1, attn_state)
+    g = jnp.where(shard == 3, g_last, hop(dx, 2, 1))
+    d_middle, d_upper, d_normed2 = ff_backward(g, ff_state)
+    hat2, _, normed2, _, hidden = ff_state
+    g_grouped, n2_grouped = grouped(g), grouped(normed2)
+    ff_grads = [t_mm(n2_grouped, d_upper[0]), t_mm(n2_grouped, d_upper[1]), t_mm(g_grouped, hidden[0]), t_mm(g_grouped, hidden[1])]
+    ff_sums = scatter_grads(jnp.concatenate([v.astype(bf16) for v in ff_grads], axis=1), 1, section, shard)
+    d_middle = jnp.where(shard == 2, d_middle1, hop(d_middle, 1, 0))
+    dx, d_mixed, d_normed1 = attn_backward(d_middle, attn_state)
+    hat1, _, normed, _, _, _, _, _, _, ob, _ = attn_state
+    n1_grouped, att_grouped = grouped(normed), grouped(ob[:, :width])
+    attn_grads = [t_mm(n1_grouped, d) for d in d_mixed] + [t_mm(att_grouped, jnp.pad(d_middle, ((0, 0), (0, wide - width))))]
+    attn_sums = scatter_grads(jnp.concatenate([v.astype(bf16) for v in attn_grads], axis=1), 0, section, shard)
+
+    own_hat = jnp.where(is_attn, hat1, hat2)
+    own_grad = jnp.where(is_attn, d_normed1, d_normed2)
+    terms = jnp.stack([jnp.sum(own_grad * own_hat, axis=0), jnp.sum(own_grad, axis=0)])
+    terms = jnp.where(jnp.arange(4)[:, None, None] == shard, terms[None], 0.0)
+    totals = lax.psum(terms, ("section", "ctx", "shard")).reshape(2, 2, 2, width)
+    totals = lax.dynamic_index_in_dim(totals, section, 0, keepdims=False)
+    totals = lax.dynamic_slice_in_dim(totals, (ctx * 4 + shard) * group, group, 2)
+
+    final = jnp.where(is_attn, dx, y).reshape(blocks, 4, half, width)
+    final = lax.all_to_all(jnp.swapaxes(final, 0, 1), "ctx", 0, 0)
+    final = lax.all_to_all(final, "shard", 0, 0).reshape(2, 2, blocks, half, width)
+    final = lax.all_to_all(final, "section", 0, 0)
+    final = jnp.moveaxis(final, 0, 2).reshape(2, blocks, slice_len, width)
+
+    attn_sums = attn_sums[:group].astype(f32)
+    ff_sums = ff_sums[:group].astype(f32)
+    qkv = jnp.concatenate([attn_sums[:, i * wide : i * wide + width] for i in range(3)], axis=1)
+    return (
+        final[1][None, None],
+        final[0][None, None],
+        qkv[None],
+        attn_sums[:, 3 * wide : 3 * wide + width][None],
+        ff_sums[:, :ff][None],
+        ff_sums[:, ff:].T[None],
+        totals[:, 0][None],
+        totals[:, 1][None],
+    )
 
 
 def passed_along(value, axis, steps):
@@ -396,4 +736,5 @@
         P("section", None, ("ctx", "shard")),
         P("section", None, ("ctx", "shard")),
     )
-    return jax.shard_map(shards, mesh=mesh, in_specs=in_specs, out_specs=out_specs, check_vma=False)
+    relay = mesh.shape["section"] == 2 and mesh.shape["shard"] == 4 and mesh.shape["ctx"] == 4
+    return jax.shard_map(chain if relay else shards, mesh=mesh, in_specs=in_specs, out_specs=out_specs, check_vma=False)

time: 2690 us -> 1260 us (0.47)
  blocking collectives: 1440 us -> 100 us
  matrix products: 361 us -> 198 us
  Pallas kernels: 0 us -> 135 us
  waiting for transfers between devices: 641 us -> 591 us
  other arithmetic: 39.3 us -> 67.6 us
    unnamed x3 -> x0, blocking collectives: 1350 us -> none
    all_gather x13 -> x6, waiting for transfers between devices: 635 us -> 200 us  [the longest x2 126 us: bring(): quarters = lax.all_gather(both, 'ctx', axis=0)]
    unnamed x19 -> x11, waiting for transfers between devices: 3.93 us -> 222 us
    dot_general x78 -> x39, matrix products: 361 us -> 198 us  [dot(): return lax.dot_general(a, b, (dims, ((), ())), preferred_element_type=f32)]
    pallas_call x0 -> x4, Pallas kernels: none -> 135 us  [the longest x2 78.4 us: attention_backward(): pl.pallas_call(functools.partial(attention_backward_kernel, half), grid=(...]
    ppermute x4 -> x22, waiting for transfers between devices: 1.79 us -> 113 us  [the longest x4 42.1 us: bring(): parts.append(lax.ppermute(piece, ('section', 'shard'), moves))]
    all_gather x8 -> x2, blocking collectives: 94 us -> 18 us  [the longest x1 15.8 us: chain(): lax.all_gather(norms, 'shard', axis=2, tiled=True)]
    psum x0 -> x1, blocking collectives: none -> 45.5 us  [chain(): lax.psum(terms, ('section', 'ctx', 'shard')).reshape(2, 2, 2, width)]
  transfers between devices with their start and end apart: 23 -> 34, of which waited for: 12 -> 18; matrix products, arithmetic and copies ran while one was open for 26% -> 13% of each run, Pallas kernels for 0% -> 5%
where the time goes in v1:
time: 1260 us; the launch traced here: 1250 us
  waiting for transfers between devices  591 us (47%)
  matrix products  198 us (16%)
  Pallas kernels  135 us (11%)
  local copies, waits for them, and re-layouts  103 us (8%)
  blocking collectives  100 us (8%)
  other arithmetic  67.6 us (5%)
  starting transfers between devices  41.2 us (3%)
  between operations  15.5 us (1%)
    unnamed x11, waiting for transfers between devices  222 us
    dot_general x39, matrix products, dot(): return lax.dot_general(a, b, (dims, ((), ())), preferred_element_type=f32)  198 us
    all_gather x2, waiting for transfers between devices, bring(): quarters = lax.all_gather(both, 'ctx', axis=0)  126 us
    pallas_call x2, Pallas kernels, attention_backward(): pl.pallas_call(functools.partial(attention_backward_kernel, half), grid=(...  78.4 us
    all_gather x2, waiting for transfers between devices, bring_tokens(): every = lax.all_gather(own, 'shard', axis=0)  73.2 us
    pallas_call x2, Pallas kernels, attention_forward(): pl.pallas_call(functools.partial(attention_forward_kernel, half), grid=(w...  56.9 us
    psum x1, blocking collectives, chain(): lax.psum(terms, ('section', 'ctx', 'shard')).reshape(2, 2, 2, width)  45.5 us
    ppermute x4, waiting for transfers between devices, bring(): parts.append(lax.ppermute(piece, ('section', 'shard'), moves))  42.1 us
  transfers between devices with their start and end apart: 34, of which 18 were waited for; matrix products, arithmetic and copies ran while one was open for 13% of the time, Pallas kernels for 5%

profile of v1, /device:TPU:24, one launch (start us, length us, event | category | flops | bytes accessed | tf_op | source)
XLA Modules:
  0.0 1252.8 jit_solution(15979178039356718888)
XLA Ops:
  13.0 13.7 %collective-permute-done.1 = bf16[272,1152]{1,0:T(8,128)(2,1)S(1)} collective-permute-done((bf16[272,1152]{1,0:T(8,128)(2,1)S(1)}, bf16[272,1152]{1,0:T(8,128)(2,1)S(1)}, u32[]{:S(2)}, u32[]{:S(2)}) %collective-permute-start.1) | collective-permute-done | bytes 626720 | tf_op jit(solution)/shard_map/ppermute | solution.py:190
  30.9 3.6 collective-permute-start.6
  35.9 24.1 %collective-permute-done.6 = bf16[272,2176]{1,0:T(8,128)(2,1)S(1)} collective-permute-done((bf16[272,2176]{1,0:T(8,128)(2,1)S(1)}, bf16[272,2176]{1,0:T(8,128)(2,1)S(1)}, u32[]{:S(2)}, u32[]{:S(2)}) %collective-permute-start.6) | collective-permute-done | bytes 1183776 | tf_op jit(solution)/shard_map/ppermute | solution.py:190
  60.0 4.3 collective-permute-done.5
  67.2 28.0 %all-gather.16.cloned.1.call-done = bf16[8,272,1152]{2,1,0:T(8,128)(2,1)} async-done(((bf16[2,272,1152]{2,1,0:T(8,128)(2,1)}), bf16[8,272,1152]{2,1,0:T(8,128)(2,1)}) %all-gather.16.cloned.1.call-update) | async-done | bytes 5013520 | tf_op jit(solution)/shard_map/all_gather | solution.py:192
  95.3 98.3 %all-gather.20.cloned.1.call-done = bf16[8,272,2176]{2,1,0:T(8,128)(2,1)} async-done(((bf16[2,272,2176]{2,1,0:T(8,128)(2,1)}), bf16[8,272,2176]{2,1,0:T(8,128)(2,1)}) %all-gather.20.cloned.1.call-update) | async-done | bytes 9469968 | tf_op jit(solution)/shard_map/all_gather | solution.py:192
  193.7 30.7 %all-gather.14.cloned.1.call-done = bf16[4,2,64,1088]{3,2,1,0:T(8,128)(2,1)} async-done(((bf16[1,2,64,1088]{3,2,1,0:T(8,128)(2,1)}), bf16[4,2,64,1088]{3,2,1,0:T(8,128)(2,1)}) %all-gather.14.cloned.1.call-update) | async-done | bytes 1114128 | tf_op jit(solution)/shard_map/all_gather | solution.py:245
  224.4 3.6 all-to-all-start.1
  228.2 15.8 %all_gather.43 = bf16[2,2,1088]{1,0,2:T(2,128)(2,1)S(1)} all-gather(bf16[2,2,272]{1,0,2:T(2,128)(2,1)S(1)} %copy.114), channel_id=1, replica_groups=mesh['section'=2,'ctx'=4,'shard'=4] {'shard'}, dimensions={2}, use_global_device_ids=true | all-gather | bytes 10880 | tf_op jit(solution)/shard_map/all_gather | solution.py:239
  248.7 6.3 fusion.192
  262.9 6.7 fusion.34.q_ref
  269.6 28.5 %attention_forward.2 = (f32[512,1152]{1,0:T(8,128)}, bf16[512,1152]{1,0:T(8,128)(2,1)}, f32[512,128]{1,0:T(8,128)}) custom-call(f32[2,128,128]{2,1,0:T(8,128)} %add_select_fusion.mask_ref, bf16[512,1152]{1,0:T(8,128)(2,1)} %fusion.34.q_ref, bf16[512,1152]{1,0:T(8,128)(2,1)} %convolution_convert_fusion.17.k0_ref, ...), custom_call_target="tpu_custom_call" | custom-call | tf_op jit(solution)/shard_map/attention_forward/pallas_call | solution.py:91
  298.1 3.7 fusion.33
  303.2 13.1 %fusion.191 = (bf16[1,4,272,2176]{3,2,1,0:T(8,128)(2,1)}, bf16[1,4,272,2176]{3,2,1,0:T(8,128)(2,1)}, bf16[1,4,272,2176]{3,2,1,0:T(8,128)(2,1)}, bf16[1,4,272,2176]{3,2,1,0:T(8,128)(2,1)}) fusion(bf16[4,4,272,2176]{3,2,1,0:T(8,128)(2,1)} %all-gather.22.cloned.1.call-done), kind=kLoop, calls=%fused_computation.306 | loop fusion | bytes 37879808 | tf_op jit(solution)/shard_map/slice | solution.py:272
  316.4 11.4 fusion.91
  327.8 10.7 fusion.32
  343.2 3.1 convolution_convert_fusion.14.v0_ref
  348.0 4.7 fusion.35.q_ref
  352.7 28.3 %attention_forward.3 = (f32[512,1152]{1,0:T(8,128)}, bf16[512,1152]{1,0:T(8,128)(2,1)}, f32[512,128]{1,0:T(8,128)}) custom-call(f32[2,128,128]{2,1,0:T(8,128)} %add_select_fusion.mask_ref, bf16[512,1152]{1,0:T(8,128)(2,1)} %fusion.35.q_ref, bf16[512,1152]{1,0:T(8,128)(2,1)} %copy-done.2, bf16[512,1152]{1,0:T(8,128)(2,1)} %collective-permute-done.8.k1_ref, ...), custom_call_target="tpu_custom_call" | custom-call | tf_op jit(solution)/shard_map/attention_forward/pallas_call | solution.py:91
  381.0 4.8 fusion.30
  387.1 42.5 %all-gather.12.cloned.1.call-done = bf16[4,2,64,1088]{3,2,1,0:T(8,128)(2,1)} async-done(((bf16[1,2,64,1088]{3,2,1,0:T(8,128)(2,1)}), bf16[4,2,64,1088]{3,2,1,0:T(8,128)(2,1)}) %all-gather.12.cloned.1.call-update) | async-done | bytes 1114128 | tf_op jit(solution)/shard_map/all_gather | solution.py:245
  429.6 3.6 all-to-all-start
  433.3 15.1 %all-to-all-done = bf16[4,2,64,1088]{3,2,1,0:T(8,128)(2,1)S(1)} async-done(((bf16[4,2,64,1088]{3,2,1,0:T(8,128)(2,1)}), bf16[4,2,64,1088]{3,2,1,0:T(8,128)(2,1)S(1)}, u32[]{:S(2)}, u32[]{:S(2)}) %all-to-all-start) | async-done | bytes 1114144 | tf_op jit(solution)/shard_map/all_to_all | solution.py:246
  452.4 12.9 %collective-permute-done.10 = bf16[512,1088]{0,1:T(8,128)(2,1)} collective-permute-done((bf16[512,1088]{0,1:T(8,128)(2,1)}, bf16[512,1088]{0,1:T(8,128)(2,1)}, u32[]{:S(2)}, u32[]{:S(2)}) %collective-permute-start.10) | collective-permute-done | bytes 1114144 | tf_op jit(solution)/shard_map/ppermute | solution.py:179
  467.4 7.5 fusion.183
  475.0 5.7 fusion.181
  480.7 12.7 %fusion.107 = f32[512,1088]{0,1:T(8,128)} fusion(bf16[1088,2176]{1,0:T(8,128)(2,1)} %bitcast.172, f32[512,2176]{1,0:T(8,128)} %fusion.183, bf16[512,1088]{1,0:T(8,128)(2,1)} %bitcast.178, bf16[1088,2176]{1,0:T(8,128)(2,1)} %bitcast.153), kind=kOutput, calls=%fused_computation.174 | convolution fusion | flops 4870897664 | bytes 17268736 | tf_op jit(solution)/shard_map/dot_general | solution.py:26
  493.3 13.5 %fusion.190 = (f32[512]{0:T(512)S(1)}, f32[512]{0:T(512)S(1)}, f32[512,1088]{0,1:T(8,128)}) fusion(f32[512]{0:T(512)S(1)} %add_rsqrt_fusion.1, f32[512]{0:T(512)S(1)} %broadcast_multiply_fusion.9, bf16[512,1088]{0,1:T(8,128)(2,1)S(1)} %get-tuple-element.93, f32[1088]{0:T(1024)S(1)} %get-tuple-element.86, f32[512,1088]{0,1:T(8,128)} %fusion.107, ...), kind=kOutput, calls=%fused_computation.305 | convolution fusion | flops 4875353088 | bytes 20623616 | tf_op jit(solution)/shard_map/dot_general | solution.py:26
  511.3 23.3 %collective-permute-done.11 = bf16[512,1088]{0,1:T(8,128)(2,1)S(1)} collective-permute-done((bf16[512,1088]{0,1:T(8,128)(2,1)S(1)}, bf16[512,1088]{0,1:T(8,128)(2,1)S(1)}, u32[]{:S(2)}, u32[]{:S(2)}) %collective-permute-start.11) | collective-permute-done | bytes 1114144 | tf_op jit(solution)/shard_map/ppermute | solution.py:179
  543.0 39.0 %attention_backward.2 = (bf16[512,1152]{1,0:T(8,128)(2,1)}, f32[512,1152]{1,0:T(8,128)}, bf16[512,1152]{1,0:T(8,128)(2,1)}, f32[512,1152]{1,0:T(8,128)}, bf16[512,1152]{1,0:T(8,128)(2,1)}) custom-call(f32[2,128,128]{2,1,0:T(8,128)} %add_select_fusion.mask_ref, bf16[512,1152]{1,0:T(8,128)(2,1)} %fusion.35.q_ref, bf16[512,1152]{1,0:T(8,128)(2,1)} %copy-done.2, ...), custom_call_target="tpu_custom_call" | custom-call | tf_op jit(solution)/shard_map/attention_backward/pallas_call | solution.py:148
  585.1 4.3 fusion.116
  598.7 9.4 add_convert_fusion.1
  608.2 9.1 add_convert_fusion
  620.2 3.1 multiply_reduce_fusion.1
  636.8 39.4 %attention_backward.3 = (bf16[512,1152]{1,0:T(8,128)(2,1)}, f32[512,1152]{1,0:T(8,128)}, bf16[512,1152]{1,0:T(8,128)(2,1)}, f32[512,1152]{1,0:T(8,128)}, bf16[512,1152]{1,0:T(8,128)(2,1)}) custom-call(f32[2,128,128]{2,1,0:T(8,128)} %add_select_fusion.mask_ref, bf16[512,1152]{1,0:T(8,128)(2,1)} %fusion.35.q_ref, bf16[512,1152]{1,0:T(8,128)(2,1)} %copy-done.2, ...), custom_call_target="tpu_custom_call" | custom-call | tf_op jit(solution)/shard_map/attention_backward/pallas_call | solution.py:148
  680.0 3.3 convolution_convert_fusion.7
  683.3 7.0 convolution_convert_fusion.4
  690.3 4.2 convolution_convert_fusion.5
  694.6 3.2 convolution_convert_fusion.6
  697.8 28.2 %pad_maximum_fusion.1 = bf16[1152,4608]{0,1:T(8,128)(2,1)} fusion(bf16[1152,1152]{0,1:T(8,128)(2,1)S(1)} %copy-done.12, bf16[1152,1152]{0,1:T(8,128)(2,1)S(1)} %convolution_convert_fusion.5, bf16[1152,1152]{0,1:T(8,128)(2,1)S(1)} %convolution_convert_fusion.6, bf16[1152,1152]{0,1:T(8,128)(2,1)S(1)} %copy-done.11), kind=kLoop, calls=%fused_computation.5 | loop fusion | flops 42467328 | bytes 21233664 | tf_op jit(solution)/shard_map/concatenate | solution.py:322
  726.0 15.3 %copy.125 = bf16[1152,4608]{1,0:T(8,128)(2,1)} copy(bf16[1152,4608]{0,1:T(8,128)(2,1)} %pad_maximum_fusion.1) | data formatting | bytes 21233664 | tf_op jit(solution)/shard_map/concatenate | solution.py:322
  746.3 5.3 convolution_convert_fusion.2
  751.6 5.2 convolution_convert_fusion.3
  756.7 5.9 convolution_convert_fusion
  762.6 5.4 convolution_convert_fusion.1
  768.0 16.8 %pad_maximum_fusion = bf16[1152,8704]{1,0:T(8,128)(2,1)} fusion(bf16[1152,2176]{1,0:T(8,128)(2,1)} %convolution_convert_fusion, bf16[1152,2176]{1,0:T(8,128)(2,1)} %convolution_convert_fusion.1, bf16[1152,2176]{1,0:T(8,128)(2,1)} %convolution_convert_fusion.2, bf16[1152,2176]{1,0:T(8,128)(2,1)} %convolution_convert_fusion.3), kind=kLoop, calls=%fused_computation | loop fusion | flops 80216064 | bytes 40108032 | tf_op jit(solution)/shard_map/concatenate | solution.py:316
  784.8 17.2 %copy.126 = bf16[4,2,2,72,8704]{4,3,2,0,1:T(8,128)(2,1)} copy(bf16[4,2,2,72,8704]{4,3,2,1,0:T(8,128)(2,1)} %bitcast.146) | data formatting | bytes 40108032 | tf_op jit(solution)/shard_map/reshape | solution.py:202
  803.3 33.8 %all-reduce.14.cloned.1.call-done = bf16[4,2,2,72,4608]{4,3,2,1,0:T(8,128)(2,1)} async-done(((bf16[4,2,2,72,4608]{4,3,2,1,0:T(8,128)(2,1)}), bf16[4,2,2,72,4608]{4,3,2,1,0:T(8,128)(2,1)}) %all-reduce.14.cloned.1.call-update) | async-done | bytes 10616848
  837.0 5.8 dynamic-slice_bitcast_fusion
  842.9 41.3 %reduce-scatter.5.cloned.1.call-done = bf16[4,1,2,72,8704]{4,3,2,0,1:T(8,128)(2,1)} async-done(((bf16[4,2,2,72,8704]{4,3,2,0,1:T(8,128)(2,1)}), bf16[4,1,2,72,8704]{4,3,2,0,1:T(8,128)(2,1)}) %reduce-scatter.5.cloned.1.call-update) | async-done | bytes 10027024 | tf_op jit(solution)/shard_map/reduce_scatter | solution.py:203
  884.2 7.0 fusion.179
  891.3 3.1 fusion.166
  894.4 3.5 fusion.165
  900.9 4.8 fusion.119
  907.5 32.4 %all_to_all.25 = bf16[4,2,64,1088]{3,2,1,0:T(8,128)(2,1)} all-to-all(bf16[4,2,64,1088]{3,2,1,0:T(8,128)(2,1)S(1)} %copy.122), channel_id=1, replica_groups=mesh['section'=2,'ctx'=4,'shard'=4] {'ctx'}, dimensions={0} | all-to-all | bytes 2228224 | tf_op jit(solution)/shard_map/all_to_all | solution.py:333
  939.9 5.1 all-to-all-start.3
  945.7 45.5 %psum.7 = f32[2,2,2,1088]{3,2,1,0:T(2,128)S(1)} all-reduce(f32[2,2,2,1088]{3,2,1,0:T(2,128)S(1)} %bitcast.215), channel_id=1, replica_groups=mesh['section'=2,'ctx'=4,'shard'=4] {'section','ctx','shard'}, use_global_device_ids=true, to_apply=%region_22.23 | all-reduce | flops 8704 | bytes 69632 | tf_op jit(solution)/shard_map/psum | solution.py:328
  991.8 4.7 all_to_all.26
  998.8 188.2 %all-reduce.16.cloned.1.call-done = (bf16[4,2,72,4608]{3,2,1,0:T(8,128)(2,1)}, bf16[4,2,72,8704]{3,2,1,0:T(8,128)(2,1)}) async-done(((bf16[4,2,72,4608]{3,2,1,0:T(8,128)(2,1)}, bf16[4,2,72,8704]{3,2,1,0:T(8,128)(2,1)}), (bf16[4,2,72,4608]{3,2,1,0:T(8,128)(2,1)}, bf16[4,2,72,8704]{3,2,1,0:T(8,128)(2,1)})) %all-reduce.16.cloned.1.call-update) | async-done | bytes 15335440
  1191.0 3.9 dynamic-slice_bitcast_fusion.2
  1194.9 7.2 collective-permute-start.21
  1204.0 12.2 collective-permute-done.18
  1219.5 6.7 collective-permute-done.21
  1226.2 13.4 %collective-permute-done.20 = bf16[72,8704]{1,0:T(8,128)(2,1)} collective-permute-done((bf16[72,8704]{1,0:T(8,128)(2,1)}, bf16[72,8704]{1,0:T(8,128)(2,1)}, u32[]{:S(2)}, u32[]{:S(2)}) %collective-permute-start.20) | collective-permute-done | bytes 1253408 | tf_op jit(solution)/shard_map/ppermute | solution.py:211
  (298 shorter events, 117.4 us)
Async XLA Ops:
  7.2 58.8 %copy-start = (bf16[1,2,128,1088]{2,3,1,0:T(8,128)(2,1)S(1)}, bf16[1,2,128,1088]{2,3,1,0:T(8,128)(2,1)}, u32[]{:S(2)}) copy-start(bf16[1,2,128,1088]{2,3,1,0:T(8,128)(2,1)} %param.8) | copy-start | bytes 1671172
  7.2 88.1 %all-gather.16.cloned.1.call-start = ((), (), s32[]{:S(2)}) async-start(), calls=%async_computation.9 | async-start | bytes 6266880 | tf_op jit(solution)/shard_map/all_gather | solution.py:192
  10.8 17.1 %copy-start.24 = (bf16[1,4352,272]{1,2,0:T(8,128)(2,1)S(1)}, bf16[1,4352,272]{1,2,0:T(8,128)(2,1)}, u32[]{:S(2)}) copy-start(bf16[1,4352,272]{1,2,0:T(8,128)(2,1)} %param.13) | copy-start | bytes 7102468
  10.8 15.9 %collective-permute-start.1 = (bf16[272,1152]{1,0:T(8,128)(2,1)S(1)}, bf16[272,1152]{1,0:T(8,128)(2,1)S(1)}, u32[]{:S(2)}, u32[]{:S(2)}) collective-permute-start(bf16[272,1152]{1,0:T(8,128)(2,1)S(1)} %fusion.131), channel_id=1, source_target_pairs={{1,0},{3,16},{17,2},{19,18},{5,4},{7,20},{21,6},{23,22},{9,8},{11,... | collective-permute-start | bytes 1880072 | tf_op jit(solution)/shard_map/ppermute | solution.py:190
  12.3 14.4 %collective-permute-start = (bf16[272,1152]{1,0:T(8,128)(2,1)S(1)}, bf16[272,1152]{1,0:T(8,128)(2,1)S(1)}, u32[]{:S(2)}, u32[]{:S(2)}) collective-permute-start(bf16[272,1152]{1,0:T(8,128)(2,1)S(1)} %fusion.131), channel_id=1, source_target_pairs={{0,0},{2,16},{16,2},{18,18},{4,4},{6,20},{20,6},{22,22},{8,8},{10,... | collective-permute-start | bytes 1880072 | tf_op jit(solution)/shard_map/ppermute | solution.py:190
  27.9 165.7 %all-gather.20.cloned.1.call-start = ((), (), s32[]{:S(2)}) async-start(), calls=%async_computation.11 | async-start | bytes 11837440 | tf_op jit(solution)/shard_map/all_gather | solution.py:192
  30.9 29.1 %collective-permute-start.6 = (bf16[272,2176]{1,0:T(8,128)(2,1)S(1)}, bf16[272,2176]{1,0:T(8,128)(2,1)S(1)}, u32[]{:S(2)}, u32[]{:S(2)}) collective-permute-start(bf16[272,2176]{1,0:T(8,128)(2,1)S(1)} %fusion.114), channel_id=1, source_target_pairs={{1,1},{3,17},{17,3},{19,19},{5,5},{7,21},{21,7},{23,23},{9,9},{11,... | collective-permute-start | bytes 3551240 | tf_op jit(solution)/shard_map/ppermute | solution.py:190
  34.6 29.7 %collective-permute-start.5 = (bf16[272,2176]{1,0:T(8,128)(2,1)S(1)}, bf16[272,2176]{1,0:T(8,128)(2,1)S(1)}, u32[]{:S(2)}, u32[]{:S(2)}) collective-permute-start(bf16[272,2176]{1,0:T(8,128)(2,1)S(1)} %fusion.114), channel_id=1, source_target_pairs={{0,1},{2,17},{16,3},{18,19},{4,5},{6,21},{20,7},{22,23},{8,9},{10,... | collective-permute-start | bytes 3551240 | tf_op jit(solution)/shard_map/ppermute | solution.py:190
  65.9 158.4 %all-gather.14.cloned.1.call-start = ((), (), s32[]{:S(2)}) async-start(), calls=%async_computation.7 | async-start | bytes 1474560 | tf_op jit(solution)/shard_map/all_gather | solution.py:245
  67.2 181.5 %all-gather.18.cloned.1.call-start = ((), (), s32[]{:S(2)}) async-start(), calls=%async_computation.10 | async-start | bytes 15040512 | tf_op jit(solution)/shard_map/all_gather | solution.py:193
  95.3 207.9 %all-gather.22.cloned.1.call-start = ((), (), s32[]{:S(2)}) async-start(), calls=%async_computation.12 | async-start | bytes 28409856 | tf_op jit(solution)/shard_map/all_gather | solution.py:193
  193.6 34.4 %copy-start.33 = (bf16[1,2,272]{2,1,0:T(2,128)(2,1)S(1)}, bf16[1,2,272]{2,1,0:T(2,128)(2,1)}, u32[]{:S(2)}) copy-start(bf16[1,2,272]{2,1,0:T(2,128)(2,1)} %param.15) | copy-start | bytes 3268
  193.6 34.4 %copy-start.34 = (bf16[1,2,272]{2,1,0:T(2,128)(2,1)S(1)}, bf16[1,2,272]{2,1,0:T(2,128)(2,1)}, u32[]{:S(2)}) copy-start(bf16[1,2,272]{2,1,0:T(2,128)(2,1)} %param.14) | copy-start | bytes 3268
  224.4 22.8 %all-to-all-start.1 = ((bf16[4,2,64,1088]{3,2,1,0:T(8,128)(2,1)}), bf16[4,2,64,1088]{3,2,1,0:T(8,128)(2,1)S(1)}, u32[]{:S(2)}, u32[]{:S(2)}) async-start(bf16[4,2,64,1088]{3,2,1,0:T(8,128)(2,1)} %all-gather.14.cloned.1.call-done), calls=%async_computation.1 | async-start | bytes 2359296 | tf_op jit(solution)/shard_map/all_to_all | solution.py:246
  228.0 201.6 %all-gather.12.cloned.1.call-start = ((), (), s32[]{:S(2)}) async-start(), calls=%async_computation.6 | async-start | bytes 1474560 | tf_op jit(solution)/shard_map/all_gather | solution.py:245
  248.5 9.5 copy-start.27
  257.9 11.7 collective-permute-start.2
  261.0 8.6 collective-permute-start.3
  262.9 35.3 %copy-start.6 = (bf16[512,1088]{0,1:T(8,128)(2,1)}, bf16[512,1088]{0,1:T(8,128)(2,1)S(1)}, u32[]{:S(2)}) copy-start(bf16[512,1088]{0,1:T(8,128)(2,1)S(1)} %copy.113) | copy-start | bytes 3342340
  301.9 0.7 collective-permute-start.4
  302.6 25.2 %copy-start.3 = (bf16[512,1088]{0,1:T(8,128)(2,1)}, bf16[512,1088]{0,1:T(8,128)(2,1)S(1)}, u32[]{:S(2)}) copy-start(bf16[512,1088]{0,1:T(8,128)(2,1)S(1)} %collective-permute-done.4) | copy-start | bytes 3342340
  338.4 0.9 collective-permute-start.7
  346.3 6.5 collective-permute-start.8
  346.4 6.4 collective-permute-start.9
  385.8 79.4 %collective-permute-start.10 = (bf16[512,1088]{0,1:T(8,128)(2,1)}, bf16[512,1088]{0,1:T(8,128)(2,1)}, u32[]{:S(2)}, u32[]{:S(2)}) collective-permute-start(bf16[512,1088]{0,1:T(8,128)(2,1)} %fusion.30), channel_id=1, source_target_pairs={{2,3},{6,7},{10,11},{14,15},{18,19},{22,23},{26,27},{30,31}} | collective-permute-start | bytes 3342344 | tf_op jit(solution)/shard_map/ppermute | solution.py:179
  429.6 18.8 %all-to-all-start = ((bf16[4,2,64,1088]{3,2,1,0:T(8,128)(2,1)}), bf16[4,2,64,1088]{3,2,1,0:T(8,128)(2,1)S(1)}, u32[]{:S(2)}, u32[]{:S(2)}) async-start(bf16[4,2,64,1088]{3,2,1,0:T(8,128)(2,1)} %all-gather.12.cloned.1.call-done), calls=%async_computation | async-start | bytes 2359296 | tf_op jit(solution)/shard_map/all_to_all | solution.py:246
  433.3 403.8 %all-reduce.14.cloned.1.call-start = ((), (), s32[]{:S(2)}) async-start(), calls=%async_computation.13 | async-start | bytes 21233664
  465.3 9.7 slice-start.2
  467.4 7.6 slice-start.3
  506.9 28.7 %copy-start.22 = (bf16[1,4,272,1152]{3,2,1,0:T(8,128)(2,1)S(1)}, bf16[1,4,272,1152]{3,2,1,0:T(8,128)(2,1)}, u32[]{:S(2)}) copy-start(bf16[1,4,272,1152]{3,2,1,0:T(8,128)(2,1)} %get-tuple-element.105) | copy-start | bytes 7520260
  509.6 25.0 %collective-permute-start.11 = (bf16[512,1088]{0,1:T(8,128)(2,1)S(1)}, bf16[512,1088]{0,1:T(8,128)(2,1)S(1)}, u32[]{:S(2)}, u32[]{:S(2)}) collective-permute-start(bf16[512,1088]{0,1:T(8,128)(2,1)S(1)} %fusion.65), channel_id=1, source_target_pairs={{3,2},{7,6},{11,10},{15,14},{19,18},{23,22},{27,26},{31,30}} | collective-permute-start | bytes 3342344 | tf_op jit(solution)/shard_map/ppermute | solution.py:179
  581.9 3.1 collective-permute-start.13
  582.0 7.3 collective-permute-start.12
  595.3 1.9 collective-permute-start.14
  597.2 11.0 slice-start.12
  598.7 24.6 %copy-start.7 = (bf16[512,1088]{0,1:T(8,128)(2,1)}, bf16[512,1088]{0,1:T(8,128)(2,1)S(1)}, u32[]{:S(2)}) copy-start(bf16[512,1088]{0,1:T(8,128)(2,1)S(1)} %broadcast_select_fusion) | copy-start | bytes 3342340
  598.7 9.4 slice-start.13
  598.7 18.6 %slice-start.6 = ((s8[4734976]{0:T(1024)(128)(4,1)}), s8[4194304]{0:T(1024)(128)(4,1)S(1)}, s32[]{:S(2)}) async-start(s8[4734976]{0:T(1024)(128)(4,1)} %bitcast.173), calls=%async_computation.21 | async-start | bytes 8388608
  598.7 21.4 %slice-start.4 = ((s8[4734976]{0:T(1024)(128)(4,1)}), s8[4194304]{0:T(1024)(128)(4,1)S(1)}, s32[]{:S(2)}) async-start(s8[4734976]{0:T(1024)(128)(4,1)} %bitcast.167), calls=%async_computation.19 | async-start | bytes 8388608
  608.2 9.1 copy-start.46
  608.2 9.1 slice-start.7
  608.2 12.0 slice-start.5
  625.2 1.7 collective-permute-start.15
  676.2 14.1 %collective-permute-start.17 = (bf16[512,1152]{1,0:T(8,128)(2,1)}, bf16[512,1152]{1,0:T(8,128)(2,1)}, u32[]{:S(2)}, u32[]{:S(2)}) collective-permute-start(bf16[512,1152]{1,0:T(8,128)(2,1)} %get-tuple-element.35), channel_id=1, source_target_pairs={{0,16},{16,0},{1,17},{17,1},{2,18},{18,2},{3,19},{19,3},{4,20},{20... | collective-permute-start | bytes 3538952 | tf_op jit(solution)/shard_map/ppermute | solution.py:175
  679.0 15.6 %collective-permute-start.16 = (bf16[512,1152]{1,0:T(8,128)(2,1)}, bf16[512,1152]{1,0:T(8,128)(2,1)}, u32[]{:S(2)}, u32[]{:S(2)}) collective-permute-start(bf16[512,1152]{1,0:T(8,128)(2,1)} %get-tuple-element.33), channel_id=1, source_target_pairs={{0,16},{16,0},{1,17},{17,1},{2,18},{18,2},{3,19},{19,3},{4,20},{20... | collective-permute-start | bytes 3538952 | tf_op jit(solution)/shard_map/ppermute | solution.py:175
  741.3 142.9 %reduce-scatter.5.cloned.1.call-start = ((), (), s32[]{:S(2)}) async-start(), calls=%async_computation.8 | async-start | bytes 30081024 | tf_op jit(solution)/shard_map/reduce_scatter | solution.py:203
  746.3 5.3 copy-start.47
  746.3 10.5 slice-start.14
  746.3 16.3 %slice-start.8 = ((s8[4456448]{0:T(1024)(128)(4,1)}), s8[4194304]{0:T(1024)(128)(4,1)S(1)}, s32[]{:S(2)}) async-start(s8[4456448]{0:T(1024)(128)(4,1)} %bitcast.219), calls=%async_computation.23 | async-start | bytes 8388608
  751.5 5.2 slice-start.15
  751.6 11.1 slice-start.9
  802.1 384.9 %all-reduce.16.cloned.1.call-start = ((), (), s32[]{:S(2)}) async-start(), calls=%async_computation.14 | async-start | bytes 30670848
  884.2 7.0 copy-start.21
  884.2 7.0 copy-start.37
  891.3 6.6 copy-start.40
  894.4 6.5 slice-start
  894.4 6.5 slice-start.10
  907.5 37.5 %copy-start.42 = (u32[32]{0:T(128)S(1)}, u32[32]{0:T(128)}, u32[]{:S(2)}) copy-start(u32[32]{0:T(128)} %constant.211) | copy-start | bytes 388
  939.9 51.9 %all-to-all-start.3 = ((bf16[4,2,64,1088]{3,2,1,0:T(8,128)(2,1)}), bf16[4,2,64,1088]{3,2,1,0:T(8,128)(2,1)S(1)}, u32[]{:S(2)}, u32[]{:S(2)}) async-start(bf16[4,2,64,1088]{3,2,1,0:T(8,128)(2,1)} %all_to_all.25), calls=%async_computation.3 | async-start | bytes 2359296 | tf_op jit(solution)/shard_map/all_to_all | solution.py:334
  1189.0 15.0 %collective-permute-start.19 = (bf16[72,4608]{1,0:T(8,128)(2,1)S(1)}, bf16[72,4608]{1,0:T(8,128)(2,1)S(1)}, u32[]{:S(2)}, u32[]{:S(2)}) collective-permute-start(bf16[72,4608]{1,0:T(8,128)(2,1)S(1)} %get-tuple-element.107), channel_id=1, source_target_pairs={{0,0},{16,2},{2,16},{18,18},{4,4},{20,6},{6,20},{22,22},{8,8},{24,... | collective-permute-start | bytes 1990664 | tf_op jit(solution)/shard_map/ppermute | solution.py:211
  1189.7 26.5 %collective-permute-start.18 = (bf16[72,4608]{1,0:T(8,128)(2,1)S(1)}, bf16[72,4608]{1,0:T(8,128)(2,1)S(1)}, u32[]{:S(2)}, u32[]{:S(2)}) collective-permute-start(bf16[72,4608]{1,0:T(8,128)(2,1)S(1)} %get-tuple-element.106), channel_id=1, source_target_pairs={{0,1},{16,3},{2,17},{18,19},{4,5},{20,7},{6,21},{22,23},{8,9},{24,... | collective-permute-start | bytes 1990664 | tf_op jit(solution)/shard_map/ppermute | solution.py:211
  1194.9 31.2 %collective-permute-start.21 = (bf16[72,8704]{1,0:T(8,128)(2,1)}, bf16[72,8704]{1,0:T(8,128)(2,1)}, u32[]{:S(2)}, u32[]{:S(2)}) collective-permute-start(bf16[72,8704]{1,0:T(8,128)(2,1)} %get-tuple-element.101), channel_id=1, source_target_pairs={{1,0},{17,2},{3,16},{19,18},{5,4},{21,6},{7,20},{23,22},{9,8},{25,... | collective-permute-start | bytes 3760136 | tf_op jit(solution)/shard_map/ppermute | solution.py:211
  1202.1 37.5 %collective-permute-start.20 = (bf16[72,8704]{1,0:T(8,128)(2,1)}, bf16[72,8704]{1,0:T(8,128)(2,1)}, u32[]{:S(2)}, u32[]{:S(2)}) collective-permute-start(bf16[72,8704]{1,0:T(8,128)(2,1)} %get-tuple-element.100), channel_id=1, source_target_pairs={{1,1},{17,3},{3,17},{19,19},{5,5},{21,7},{7,21},{23,23},{9,9},{25,... | collective-permute-start | bytes 3760136 | tf_op jit(solution)/shard_map/ppermute | solution.py:211
  1241.6 4.5 copy-start.1
  (36 other events, 93.5 us)
Sparse Core Ops, SparseCore 0:
  28.0 67.1 all-gather.15
  97.1 96.4 all-gather.19
  195.8 28.5 all-gather.13
  225.8 22.8 all-gather.17
  250.1 33.2 all-gather.21
  348.1 81.5 all-gather.11
  741.4 95.5 all-reduce.13
  839.3 44.7 reduce-scatter.4
  887.9 298.9 all-reduce.15

commit v2 on v1

--- a/solution.py
+++ b/solution.py
@@ -179,38 +179,299 @@
     return lax.ppermute(value, "shard", [(source, target)])
 
 
-def gather_weights(attn_piece, ff_piece):
-    def bring(piece, kind):
-        parts = []
-        for j in range(2):
-            moves = []
-            for layer in range(2):
-                for core in range(2):
-                    moves.append((layer * 4 + 2 * core + j, core * 4 + 2 * layer + kind))
-            parts.append(lax.ppermute(piece, ("section", "shard"), moves))
-        both = jnp.stack(parts)
-        quarters = lax.all_gather(both, "ctx", axis=0)
-        full = lax.all_gather(quarters, "section", axis=1)
-        return full.reshape(4, 4 * piece.shape[0], piece.shape[1])
-
-    return bring(attn_piece, 0), bring(ff_piece, 1)
-
-
-def scatter_grads(grads, kind, section, shard):
-    columns = grads.shape[1]
-    rows = grads.shape[0] // 16
-    terms = grads.reshape(4, 2, 2, rows, columns)
-    terms = lax.psum_scatter(terms, "section", scatter_dimension=1, tiled=False)
-    terms = lax.psum_scatter(terms, "ctx", scatter_dimension=0, tiled=False)
-    total = None
-    for j in range(2):
-        moves = []
-        for layer in range(2):
-            for core in range(2):
-                moves.append((core * 4 + 2 * layer + kind, layer * 4 + 2 * core + j))
-        came = lax.ppermute(terms[j], ("section", "shard"), moves)
-        total = came if total is None else jnp.where(shard % 2 == j, came, total)
-    return total
+ANY = pl.BlockSpec(memory_space=pl.ANY)
+
+
+def remote(src, dst, send, recv, section, ctx, shard):
+    return pltpu.make_async_remote_copy(
+        src_ref=src,
+        dst_ref=dst,
+        send_sem=send,
+        recv_sem=recv,
+        device_id=(section, ctx, shard),
+        device_id_type=pl.DeviceIdType.MESH,
+    )
+
+
+def gather_kernel(
+    attn_ref, ff_ref, x_ref, g_ref, norm_ref,
+    w_attn_ref, w_ff_ref, x_all_ref, g_all_ref, norm_all_ref,
+    send, recv, token_send, token_recv, norm_send, norm_recv, far_send, far_recv,
+):
+    section, ctx, shard = lax.axis_index("section"), lax.axis_index("ctx"), lax.axis_index("shard")
+    kind = lax.rem(shard, 2)
+    x_near, y_near = 1, 2
+    near = lambda c, step: c + step - 2 * step * lax.rem(c // step, 2)
+    far_core = 1 - shard // 2
+
+    x_copy = remote(x_ref, x_all_ref.at[ctx], token_send.at[0], token_recv.at[ctx], section, shard, 0)
+    g_copy = remote(g_ref, g_all_ref.at[ctx], token_send.at[1], token_recv.at[ctx], section, shard, 3)
+    x_stays = (shard == 0) & (ctx == 0)
+    g_stays = (shard == 3) & (ctx == 3)
+    attn_copy = remote(
+        attn_ref, w_attn_ref.at[ctx, shard], far_send.at[0], recv.at[ctx, shard], far_core, ctx, 2 * section
+    )
+    ff_copy = remote(
+        ff_ref, w_ff_ref.at[ctx, shard], far_send.at[1], recv.at[ctx, shard], far_core, ctx, 2 * section + 1
+    )
+
+    @pl.when(jnp.logical_not(x_stays))
+    def _():
+        x_copy.start()
+
+    attn_copy.start()
+    norm_copies = []
+    for core in range(2):
+        for stage in range(2):
+            index = core * 2 + stage
+            copy = remote(
+                norm_ref, norm_all_ref.at[shard], norm_send.at[index], norm_recv.at[shard],
+                core, ctx, 2 * section + stage,
+            )
+            stays = (section == core) & (shard == 2 * section + stage)
+            norm_copies.append((copy, stays))
+
+            @pl.when(jnp.logical_not(stays))
+            def _():
+                copy.start()
+
+    ff_copy.start()
+
+    @pl.when(jnp.logical_not(g_stays))
+    def _():
+        g_copy.start()
+
+    def spread(out_ref):
+        def piece(c, s, which, core, to_ctx):
+            return remote(
+                out_ref.at[c, s], out_ref.at[c, s], send.at[which], recv.at[c, s], core, to_ctx, shard
+            )
+
+        mine = [2 * (1 - section) + j for j in range(2)]
+        x_ctx, y_ctx = near(ctx, x_near), near(ctx, y_near)
+        d_ctx = near(x_ctx, y_near)
+        started = []
+
+        def go(c, s, core, to_ctx):
+            copy = piece(c, s, len(started), core, to_ctx)
+            copy.start()
+            started.append(copy)
+
+        def arrived(c, s):
+            piece(c, s, 0, section, ctx).wait_recv()
+
+        for s in mine:
+            arrived(ctx, s)
+            go(ctx, s, section, x_ctx)
+            go(ctx, s, section, y_ctx)
+            go(ctx, s, 1 - section, ctx)
+        arrived(x_ctx, mine[0])
+        go(x_ctx, mine[0], section, y_ctx)
+        go(x_ctx, mine[0], 1 - section, ctx)
+        arrived(y_ctx, mine[0])
+        go(y_ctx, mine[0], 1 - section, ctx)
+        arrived(y_ctx, mine[1])
+        go(y_ctx, mine[1], section, x_ctx)
+        go(y_ctx, mine[1], 1 - section, ctx)
+        arrived(x_ctx, mine[1])
+        go(x_ctx, mine[1], 1 - section, ctx)
+        for s in mine:
+            arrived(d_ctx, s)
+            go(d_ctx, s, 1 - section, ctx)
+        for c in (ctx, x_ctx, y_ctx, d_ctx):
+            for j in range(2):
+                arrived(c, 2 * section + j)
+        for copy in started:
+            copy.wait_send()
+
+    @pl.when(kind == 0)
+    def _():
+        spread(w_attn_ref)
+
+    @pl.when(kind == 1)
+    def _():
+        spread(w_ff_ref)
+
+    for s in range(4):
+
+        @pl.when(jnp.logical_not((section == shard // 2) & (shard == s)))
+        def _():
+            remote(norm_ref, norm_all_ref.at[s], norm_send.at[0], norm_recv.at[s], section, ctx, shard).wait_recv()
+
+    for c in range(4):
+
+        @pl.when((shard == 0) & jnp.logical_not((ctx == 0) & (c == 0)))
+        def _():
+            remote(x_ref, x_all_ref.at[c], token_send.at[0], token_recv.at[c], section, ctx, shard).wait_recv()
+
+        @pl.when((shard == 3) & jnp.logical_not((ctx == 3) & (c == 3)))
+        def _():
+            remote(g_ref, g_all_ref.at[c], token_send.at[1], token_recv.at[c], section, ctx, shard).wait_recv()
+
+    @pl.when(jnp.logical_not(x_stays))
+    def _():
+        x_copy.wait_send()
+
+    @pl.when(jnp.logical_not(g_stays))
+    def _():
+        g_copy.wait_send()
+
+    attn_copy.wait_send()
+    ff_copy.wait_send()
+    for copy, stays in norm_copies:
+
+        @pl.when(jnp.logical_not(stays))
+        def _():
+            copy.wait_send()
+
+
+def gather_all(attn_piece, ff_piece, x_own, g_own, norm_own):
+    like = lambda lead, v: jax.ShapeDtypeStruct(lead + v.shape, v.dtype)
+    dma = pltpu.SemaphoreType.DMA
+    return pl.pallas_call(
+        gather_kernel,
+        in_specs=[ANY] * 5,
+        out_specs=[ANY] * 5,
+        out_shape=[
+            like((4, 4), attn_piece), like((4, 4), ff_piece), like((4,), x_own), like((4,), g_own), like((4,), norm_own),
+        ],
+        scratch_shapes=[dma((14,)), dma((4, 4)), dma((2,)), dma((4,)), dma((4,)), dma((4,)), dma((2,)), dma((2,))],
+        compiler_params=pltpu.CompilerParams(has_side_effects=True),
+        name="gather_all",
+    )(attn_piece, ff_piece, x_own, g_own, norm_own)
+
+
+def add_into(total, term):
+    total[...] = (total[...].astype(f32) + term[...].astype(f32)).astype(bf16)
+
+
+def reduce_kernel(*refs):
+    attn_terms, ff_terms = refs[0:4], refs[4:8]
+    attn_out, ff_out = refs[8:10]
+    held, first, second, third = refs[10:14]
+    load, first_send, first_recv, second_send, second_recv, third_send, third_recv, last_send, last_recv = refs[14:]
+    section, ctx, shard = lax.axis_index("section"), lax.axis_index("ctx"), lax.axis_index("shard")
+    kind = lax.rem(shard, 2)
+    near = lambda c, step: c + step - 2 * step * lax.rem(c // step, 2)
+    x_ctx, y_ctx = near(ctx, 1), near(ctx, 2)
+    d_ctx = near(x_ctx, 2)
+    count = len(attn_terms)
+
+    def reduce(terms, out_ref, which):
+        width = terms[0].shape[-1]
+        cols = pl.ds(0, width)
+        own = lambda i, c, j: held.at[i, c, j, :, cols]
+
+        def give(i):
+            return remote(
+                terms[i].at[:, section], first.at[i, :, :, :, cols], first_send.at[i], first_recv.at[i],
+                1 - section, ctx, shard,
+            )
+
+        def take(i):
+            return pltpu.make_async_copy(terms[i].at[:, 1 - section], held.at[i, :, :, :, cols], load.at[i])
+
+        def second_copy(i, j, part):
+            to = (x_ctx, y_ctx)[j]
+            return remote(
+                own(i, (to, d_ctx)[part], j), second.at[i, j, part, :, cols],
+                second_send.at[i, j, part], second_recv.at[i, j, part], section, to, shard,
+            )
+
+        def third_copy(i, j):
+            to = (y_ctx, x_ctx)[j]
+            return remote(
+                own(i, to, j), third.at[i, j, :, cols], third_send.at[i, j], third_recv.at[i, j], section, to, shard
+            )
+
+        def last_copy(i, j):
+            return remote(
+                own(i, ctx, j), out_ref.at[i], last_send.at[i, j], last_recv.at[which, i],
+                shard // 2, ctx, 2 * (1 - section) + j,
+            )
+
+        for i in range(count):
+            give(i).start()
+            take(i).start()
+        for step in range(count + 2):
+            i = step
+            if i < count:
+                take(i).wait()
+                give(i).wait_recv()
+
+                @pl.loop(0, 4)
+                def _(c):
+                    for j in range(2):
+                        add_into(own(i, c, j), first.at[i, c, j, :, cols])
+
+                for part in (1, 0):
+                    for j in range(2):
+                        second_copy(i, j, part).start()
+            i = step - 1
+            if 0 <= i < count:
+                for j in range(2):
+                    second_copy(i, j, 1).wait_recv()
+                    add_into(own(i, (y_ctx, x_ctx)[j], j), second.at[i, j, 1, :, cols])
+                    third_copy(i, j).start()
+                for j in range(2):
+                    second_copy(i, j, 0).wait_recv()
+                    add_into(own(i, ctx, j), second.at[i, j, 0, :, cols])
+            i = step - 2
+            if 0 <= i < count:
+                for j in range(2):
+                    third_copy(i, j).wait_recv()
+                    add_into(own(i, ctx, j), third.at[i, j, :, cols])
+                    last_copy(i, j).start()
+        for i in range(count):
+            give(i).wait_send()
+            for j in range(2):
+                for part in range(2):
+                    second_copy(i, j, part).wait_send()
+                third_copy(i, j).wait_send()
+                last_copy(i, j).wait_send()
+
+    @pl.when(kind == 0)
+    def _():
+        reduce(attn_terms, attn_out, 0)
+
+    @pl.when(kind == 1)
+    def _():
+        reduce(ff_terms, ff_out, 1)
+
+    for i in range(count):
+        for which, out_ref in enumerate((attn_out, ff_out)):
+            remote(
+                out_ref.at[i], out_ref.at[i], last_send.at[i, 0], last_recv.at[which, i], section, ctx, shard
+            ).wait_recv()
+
+
+def reduce_all(attn_terms, ff_terms):
+    rows = attn_terms[0].shape[0] // 16
+    count = len(attn_terms)
+    split = lambda v: v.reshape(4, 2, 2, rows, v.shape[1])
+    width = ff_terms[0].shape[1]
+    dma = pltpu.SemaphoreType.DMA
+    return pl.pallas_call(
+        reduce_kernel,
+        in_specs=[ANY] * (2 * count),
+        out_specs=[ANY] * 2,
+        out_shape=[
+            jax.ShapeDtypeStruct((count, rows, attn_terms[0].shape[1]), bf16),
+            jax.ShapeDtypeStruct((count, rows, width), bf16),
+        ],
+        scratch_shapes=[
+            pltpu.VMEM((count, 4, 2, rows, width), bf16),
+            pltpu.VMEM((count, 4, 2, rows, width), bf16),
+            pltpu.VMEM((count, 2, 2, rows, width), bf16),
+            pltpu.VMEM((count, 2, rows, width), bf16),
+            dma((count,)), dma((count,)), dma((count,)),
+            dma((count, 2, 2)), dma((count, 2, 2)),
+            dma((count, 2)), dma((count, 2)),
+            dma((count, 2)), dma((2, count)),
+        ],
+        compiler_params=pltpu.CompilerParams(has_side_effects=True, vmem_limit_bytes=48 * 2**20),
+        name="reduce_all",
+    )(*[split(v) for v in attn_terms], *[split(v) for v in ff_terms])
 
 
 def chain(inputs, cotangent, qkv_weight, out_weight, up_weight, down_weight, norm_gain, norm_bias):
@@ -231,22 +492,26 @@
     down_t = down_weight[0].T
     up0 = up_weight[0]
     ff_src = jnp.stack([up0[:, : ff // 2], up0[:, ff // 2 :], down_t[:, : ff // 2], down_t[:, ff // 2 :]])
-    w_attn, w_ff = gather_weights(
+    norm_own = jnp.concatenate([norm_gain[0], norm_bias[0], jnp.zeros((4, share), bf16)], axis=0)
+    x_own = lax.dynamic_slice_in_dim(inputs[0], section * half, half, 1)
+    g_own = lax.dynamic_slice_in_dim(cotangent[0], section * half, half, 1)
+    w_attn, w_ff, x_all, g_all, norm_all = gather_all(
         lax.dynamic_index_in_dim(attn_src, ctx, 0, keepdims=False),
         lax.dynamic_index_in_dim(ff_src, ctx, 0, keepdims=False),
-    )
-    norms = jnp.stack([norm_gain[0], norm_bias[0]])
-    norms = lax.all_gather(lax.all_gather(norms, "shard", axis=2, tiled=True), "section", axis=0)
-    norms = lax.dynamic_index_in_dim(norms, shard // 2, 0, keepdims=False).astype(f32)
-    gain1, gain2, bias1, bias2 = norms[0, 0], norms[0, 1], norms[1, 0], norms[1, 1]
-
-    def bring_tokens(array):
-        own = lax.dynamic_slice_in_dim(array[0], section * half, half, 1)
-        every = lax.all_gather(own, "shard", axis=0)
-        mine = lax.all_to_all(every, "ctx", 0, 0)
+        x_own, g_own, norm_own,
+    )
+    w_attn = w_attn.reshape(4, width, wide)
+    w_ff = w_ff.reshape(4, width, ff // 2)
+    own_place = jnp.arange(4)[:, None, None]
+    norm_all = jnp.where((own_place == shard) & (section == shard // 2), norm_own, norm_all)
+    norms = jnp.swapaxes(norm_all[:, :4], 0, 1).reshape(4, width).astype(f32)
+    gain1, gain2, bias1, bias2 = norms[0], norms[1], norms[2], norms[3]
+
+    def bring_tokens(every, own):
+        mine = jnp.where((own_place[..., None] == ctx) & (shard == ctx), own, every)
         return jnp.swapaxes(mine, 0, 1).reshape(tokens, width)
 
-    x_first, g_last = bring_tokens(inputs), bring_tokens(cotangent)
+    x_first, g_last = bring_tokens(x_all, x_own), bring_tokens(g_all, g_own)
     mask = attention_masks(section, half)
     feature = lax.broadcasted_iota(jnp.int32, (width, 16 * group_pad), 0)
     place = lax.broadcasted_iota(jnp.int32, (width, 16 * group_pad), 1)
@@ -313,13 +578,12 @@
     hat2, _, normed2, _, hidden = ff_state
     g_grouped, n2_grouped = grouped(g), grouped(normed2)
     ff_grads = [t_mm(n2_grouped, d_upper[0]), t_mm(n2_grouped, d_upper[1]), t_mm(g_grouped, hidden[0]), t_mm(g_grouped, hidden[1])]
-    ff_sums = scatter_grads(jnp.concatenate([v.astype(bf16) for v in ff_grads], axis=1), 1, section, shard)
     d_middle = jnp.where(shard == 2, d_middle1, hop(d_middle, 1, 0))
     dx, d_mixed, d_normed1 = attn_backward(d_middle, attn_state)
     hat1, _, normed, _, _, _, _, _, _, ob, _ = attn_state
     n1_grouped, att_grouped = grouped(normed), grouped(ob[:, :width])
     attn_grads = [t_mm(n1_grouped, d) for d in d_mixed] + [t_mm(att_grouped, jnp.pad(d_middle, ((0, 0), (0, wide - width))))]
-    attn_sums = scatter_grads(jnp.concatenate([v.astype(bf16) for v in attn_grads], axis=1), 0, section, shard)
+    attn_sums, ff_sums = reduce_all([v.astype(bf16) for v in attn_grads], [v.astype(bf16) for v in ff_grads])
 
     own_hat = jnp.where(is_attn, hat1, hat2)
     own_grad = jnp.where(is_attn, d_normed1, d_normed2)
@@ -335,16 +599,15 @@
     final = lax.all_to_all(final, "section", 0, 0)
     final = jnp.moveaxis(final, 0, 2).reshape(2, blocks, slice_len, width)
 
-    attn_sums = attn_sums[:group].astype(f32)
-    ff_sums = ff_sums[:group].astype(f32)
-    qkv = jnp.concatenate([attn_sums[:, i * wide : i * wide + width] for i in range(3)], axis=1)
+    attn_sums = attn_sums[:, :group, :width].astype(f32)
+    ff_sums = ff_sums[:, :group].astype(f32)
     return (
         final[1][None, None],
         final[0][None, None],
-        qkv[None],
-        attn_sums[:, 3 * wide : 3 * wide + width][None],
-        ff_sums[:, :ff][None],
-        ff_sums[:, ff:].T[None],
+        jnp.concatenate([attn_sums[0], attn_sums[1], attn_sums[2]], axis=1)[None],
+        attn_sums[3][None],
+        jnp.concatenate([ff_sums[0], ff_sums[1]], axis=1)[None],
+        jnp.concatenate([ff_sums[2].T, ff_sums[3].T], axis=0)[None],
         totals[:, 0][None],
         totals[:, 1][None],
     )

time: 1260 us -> 814 us (0.65)
  waiting for transfers between devices: 591 us -> 70 us
  Pallas kernels: 135 us -> 402 us
  blocking collectives: 100 us -> 49.4 us
  other arithmetic: 67.6 us -> 18.2 us
  local copies, waits for them, and re-layouts: 103 us -> 60.5 us
  starting transfers between devices: 41.2 us -> 18.4 us
  between operations: 15.5 us -> 2.3 us
  matrix products: 198 us -> 185 us
    pallas_call x0 -> x2, Pallas kernels: none -> 268 us  [the longest x1 135 us: gather_all(): pl.pallas_call(gather_kernel, in_specs=[ANY] * 5, out_specs=[ANY] * 5, ou...]
    unnamed x11 -> x0, waiting for transfers between devices: 222 us -> none
    all_gather x6 -> x0, waiting for transfers between devices: 200 us -> none  [the longest x2 126 us: bring(): quarters = lax.all_gather(both, 'ctx', axis=0)]
    ppermute x8 -> x0, waiting for transfers between devices: 74.4 us -> none  [the longest x4 42.1 us: bring(): parts.append(lax.ppermute(piece, ('section', 'shard'), moves))]
    concatenate x2 -> x1, other arithmetic: 45 us -> 0.77 us  [chain(): jnp.concatenate([norm_gain[0], norm_bias[0], jnp.zeros((4, share), bf16)]...]
    reduce_scatter x1 -> x0, waiting for transfers between devices: 41.3 us -> none  [scatter_grads(): terms = lax.psum_scatter(terms, 'section', scatter_dimension=1, tiled=False)]
    ppermute x6, waiting for transfers between devices: 36.2 us -> 69.9 us  [hop(): return lax.ppermute(value, 'shard', [(source, target)])]
    all_to_all x1 -> x0, blocking collectives: 32.4 us -> none  [chain(): final = lax.all_to_all(jnp.swapaxes(final, 0, 1), 'ctx', 0, 0)]
  transfers between devices with their start and end apart: 34 -> 16, of which waited for: 18 -> 3; matrix products, arithmetic and copies ran while one was open for 13% -> 12% of each run, Pallas kernels for 5% -> 16%
where the time goes in v2:
time: 814 us; the launch traced here: 806 us
  Pallas kernels  402 us (49%)
  matrix products  185 us (23%)
  waiting for transfers between devices  70 us (9%)
  local copies, waits for them, and re-layouts  60.5 us (7%)
  blocking collectives  49.4 us (6%)
  starting transfers between devices  18.4 us (2%)
  other arithmetic  18.2 us (2%)
    dot_general x39, matrix products, dot(): return lax.dot_general(a, b, (dims, ((), ())), preferred_element_type=f32)  185 us
    pallas_call x1, Pallas kernels, gather_all(): pl.pallas_call(gather_kernel, in_specs=[ANY] * 5, out_specs=[ANY] * 5, ou...  135 us
    pallas_call x1, Pallas kernels, reduce_all(): pl.pallas_call(reduce_kernel, in_specs=[ANY] * (2 * count), out_specs=[AN...  133 us
    pallas_call x2, Pallas kernels, attention_backward(): pl.pallas_call(functools.partial(attention_backward_kernel, half), grid=(...  78.2 us
    ppermute x6, waiting for transfers between devices, hop(): return lax.ppermute(value, 'shard', [(source, target)])  69.9 us
    pallas_call x2, Pallas kernels, attention_forward(): pl.pallas_call(functools.partial(attention_forward_kernel, half), grid=(w...  56.6 us
    psum x1, blocking collectives, chain(): lax.psum(terms, ('section', 'ctx', 'shard')).reshape(2, 2, 2, width)  43.6 us
    unnamed x156, local copies, waits for them, and re-layouts  17 us
  transfers between devices with their start and end apart: 16, of which 3 were waited for; matrix products, arithmetic and copies ran while one was open for 12% of the time, Pallas kernels for 16%

profile of v2, /device:TPU:24, one launch (start us, length us, event | category | flops | bytes accessed | tf_op | source)
XLA Modules:
  0.0 806.2 jit_solution(18024431064962295280)
XLA Ops:
  0.7 1.6 fusion.191
  10.9 2.0 fusion.113.ff_ref
  12.9 135.0 %gather_all.1 = (bf16[4,4,272,1152]{3,2,1,0:T(8,128)(2,1)}, bf16[4,4,272,2176]{3,2,1,0:T(8,128)(2,1)}, bf16[4,2,64,1088]{3,2,1,0:T(8,128)(2,1)}, bf16[4,2,64,1088]{3,2,1,0:T(8,128)(2,1)}, bf16[4,8,272]{2,1,0:T(8,128)(2,1)}) custom-call(bf16[272,1152]{1,0:T(8,128)(2,1)} %fusion.129.attn_ref, bf16[272,2176]{1,0:T(8,128)(2,1)} %fusion.113.ff_ref, ...), custom_call_target="tpu_custom_call" | custom-call | tf_op jit(solution)/shard_map/gather_all/pallas_call | solution.py:331
  148.0 6.9 fusion.190
  155.7 1.8 convert_reduce_fusion.3
  158.6 2.9 convolution_convert_fusion.17.k0_ref
  161.9 2.9 convolution_convert_fusion.16.v0_ref
  166.6 4.6 fusion.34.q_ref
  171.2 28.3 %attention_forward.2 = (f32[512,1152]{1,0:T(8,128)}, bf16[512,1152]{1,0:T(8,128)(2,1)}, f32[512,128]{1,0:T(8,128)}) custom-call(f32[2,128,128]{2,1,0:T(8,128)} %add_select_fusion.mask_ref, bf16[512,1152]{1,0:T(8,128)(2,1)} %fusion.34.q_ref, bf16[512,1152]{1,0:T(8,128)(2,1)} %convolution_convert_fusion.17.k0_ref, ...), custom_call_target="tpu_custom_call" | custom-call | tf_op jit(solution)/shard_map/attention_forward/pallas_call | solution.py:91
  199.6 3.7 fusion.33
  204.0 13.0 %fusion.189 = (bf16[1,4,272,2176]{3,2,1,0:T(8,128)(2,1)}, bf16[1,4,272,2176]{3,2,1,0:T(8,128)(2,1)}, bf16[1,4,272,2176]{3,2,1,0:T(8,128)(2,1)}, bf16[1,4,272,2176]{3,2,1,0:T(8,128)(2,1)}) fusion(bf16[4,4,272,2176]{3,2,1,0:T(8,128)(2,1)} %get-tuple-element.34), kind=kLoop, calls=%fused_computation.306 | loop fusion | bytes 37879808 | tf_op jit(solution)/shard_map/slice | solution.py:537
  217.7 11.4 %fusion.91 = f32[512,1088]{0,1:T(8,128)} fusion(bf16[1088,2176]{1,0:T(8,128)(2,1)} %bitcast.170, bf16[1088,2176]{1,0:T(8,128)(2,1)} %bitcast.156, bf16[512,1088]{0,1:T(8,128)(2,1)S(1)} %collective-permute-done.2, f32[1088]{0:T(1024)S(1)} %add.247, f32[1088]{0:T(1024)S(1)} %mul.381, f32[512]{0:T(512)S(1)} %add_rsqrt_fusion.3, ...), kind=kOutput, calls=%fused_computation.156 | convolution fusion | flops 4861984768 | bytes 12825088 | tf_op jit(solution)/shard_map/dot_general | solution.py:26
  229.1 11.7 %fusion.32 = bf16[512,1088]{0,1:T(8,128)(2,1)} fusion(f32[512,1088]{0,1:T(8,128)} %fusion.91, bf16[1088,2176]{1,0:T(8,128)(2,1)} %bitcast.148, bf16[512,1088]{0,1:T(8,128)(2,1)S(1)} %collective-permute-done.2, bf16[1088,2176]{1,0:T(8,128)(2,1)} %bitcast.164, f32[1088]{0:T(1024)S(1)} %add.247, f32[1088]{0:T(1024)S(1)} %mul.381, f32[512]{0:T(512)S(1)} %add_rsqrt_fusion.3, ...), kind=kOutput, calls=%fused_computation.77 | convolution fusion | flops 4864212992 | bytes 13939200 | tf_op jit(solution)/shard_map/dot_general | solution.py:26
  243.7 2.1 convolution_convert_fusion.15.k0_ref
  245.8 2.1 convolution_convert_fusion.14.v0_ref
  248.5 3.1 fusion.35.q_ref
  252.7 28.3 %attention_forward.3 = (f32[512,1152]{1,0:T(8,128)}, bf16[512,1152]{1,0:T(8,128)(2,1)}, f32[512,128]{1,0:T(8,128)}) custom-call(f32[2,128,128]{2,1,0:T(8,128)} %add_select_fusion.mask_ref, bf16[512,1152]{1,0:T(8,128)(2,1)} %fusion.35.q_ref, bf16[512,1152]{1,0:T(8,128)(2,1)} %copy-done.2, bf16[512,1152]{1,0:T(8,128)(2,1)} %copy-done.4, ...), custom_call_target="tpu_custom_call" | custom-call | tf_op jit(solution)/shard_map/attention_forward/pallas_call | solution.py:91
  281.0 4.8 fusion.30
  290.1 46.4 %collective-permute-done.6 = bf16[512,1088]{0,1:T(8,128)(2,1)} collective-permute-done((bf16[512,1088]{0,1:T(8,128)(2,1)}, bf16[512,1088]{0,1:T(8,128)(2,1)}, u32[]{:S(2)}, u32[]{:S(2)}) %collective-permute-start.6) | collective-permute-done | bytes 1114144 | tf_op jit(solution)/shard_map/ppermute | solution.py:179
  336.5 1.8 convert_reduce_fusion
  338.7 7.5 fusion.181
  346.2 5.5 fusion.179
  351.7 12.3 %fusion.107 = f32[512,1088]{0,1:T(8,128)} fusion(bf16[1088,2176]{1,0:T(8,128)(2,1)} %bitcast.166, f32[512,2176]{1,0:T(8,128)} %fusion.181, bf16[512,1088]{1,0:T(8,128)(2,1)S(1)} %bitcast.177, bf16[1088,2176]{1,0:T(8,128)(2,1)} %bitcast.149), kind=kOutput, calls=%fused_computation.170 | convolution fusion | flops 4870897664 | bytes 17268736 | tf_op jit(solution)/shard_map/dot_general | solution.py:26
  364.0 13.1 %fusion.188 = (f32[512]{0:T(512)S(1)}, f32[512]{0:T(512)S(1)}, f32[512,1088]{0,1:T(8,128)}) fusion(f32[512]{0:T(512)S(1)} %add_rsqrt_fusion.1, f32[512]{0:T(512)S(1)} %broadcast_multiply_fusion.9, bf16[512,1088]{0,1:T(8,128)(2,1)S(1)} %get-tuple-element.105, f32[1088]{0:T(1024)S(1)} %mul.381, f32[512,1088]{0,1:T(8,128)} %fusion.107, ...), kind=kOutput, calls=%fused_computation.305 | convolution fusion | flops 4875353088 | bytes 20623616 | tf_op jit(solution)/shard_map/dot_general | solution.py:26
  377.1 2.5 fusion.65
  379.6 1.7 collective-permute-start.7
  381.3 23.4 %collective-permute-done.7 = bf16[512,1088]{0,1:T(8,128)(2,1)S(1)} collective-permute-done((bf16[512,1088]{0,1:T(8,128)(2,1)S(1)}, bf16[512,1088]{0,1:T(8,128)(2,1)S(1)}, u32[]{:S(2)}, u32[]{:S(2)}) %collective-permute-start.7) | collective-permute-done | bytes 1114144 | tf_op jit(solution)/shard_map/ppermute | solution.py:179
  405.7 2.7 convolution_convert_fusion.9
  408.4 1.7 copy.92
  411.2 39.1 %attention_backward.2 = (bf16[512,1152]{1,0:T(8,128)(2,1)}, f32[512,1152]{1,0:T(8,128)}, bf16[512,1152]{1,0:T(8,128)(2,1)}, f32[512,1152]{1,0:T(8,128)}, bf16[512,1152]{1,0:T(8,128)(2,1)}) custom-call(f32[2,128,128]{2,1,0:T(8,128)} %add_select_fusion.mask_ref, bf16[512,1152]{1,0:T(8,128)(2,1)} %fusion.35.q_ref, bf16[512,1152]{1,0:T(8,128)(2,1)} %copy-done.2, ...), custom_call_target="tpu_custom_call" | custom-call | tf_op jit(solution)/shard_map/attention_backward/pallas_call | solution.py:148
  451.0 3.6 convolution_convert_fusion.13
  454.6 3.1 fusion.115
  457.8 1.7 fusion.114
  459.8 2.1 fusion.187
  464.1 2.5 convolution_convert_fusion.11
  466.7 4.3 fusion.177
  471.2 5.9 add_convert_fusion.1
  477.1 5.9 add_convert_fusion
  483.0 2.3 convolution_convert_fusion.10
  485.4 2.8 fusion.199
  488.2 3.1 multiply_reduce_fusion.1
  493.6 5.3 convolution_convert_fusion.1
  498.9 5.1 convolution_convert_fusion.3
  504.1 5.3 convolution_convert_fusion
  515.3 39.1 %attention_backward.3 = (bf16[512,1152]{1,0:T(8,128)(2,1)}, f32[512,1152]{1,0:T(8,128)}, bf16[512,1152]{1,0:T(8,128)(2,1)}, f32[512,1152]{1,0:T(8,128)}, bf16[512,1152]{1,0:T(8,128)(2,1)}) custom-call(f32[2,128,128]{2,1,0:T(8,128)} %add_select_fusion.mask_ref, bf16[512,1152]{1,0:T(8,128)(2,1)} %fusion.35.q_ref, bf16[512,1152]{1,0:T(8,128)(2,1)} %copy-done.2, ...), custom_call_target="tpu_custom_call" | custom-call | tf_op jit(solution)/shard_map/attention_backward/pallas_call | solution.py:148
  554.6 5.2 convolution_convert_fusion.2
  560.3 1.7 convolution_convert_fusion.7
  562.0 7.4 convolution_convert_fusion.4
  569.4 4.6 fusion.164
  574.1 3.1 fusion.163
  577.3 3.1 fusion.85
  580.6 4.7 fusion.118
  585.3 2.4 copy.95
  587.7 2.4 copy.96
  590.1 4.3 all-to-all-start
  594.4 5.7 convolution_convert_fusion.6
  600.1 4.5 convolution_convert_fusion.5
  604.6 132.5 %reduce_all.1 = (bf16[4,72,1152]{2,1,0:T(8,128)(2,1)S(1)}, bf16[4,72,2176]{2,1,0:T(8,128)(2,1)S(1)}) custom-call(bf16[4,2,2,72,1152]{4,3,2,1,0:T(8,128)(2,1)S(1)} %bitcast.143, bf16[4,2,2,72,1152]{4,3,2,1,0:T(8,128)(2,1)} %bitcast.188, bf16[4,2,2,72,1152]{4,3,2,1,0:T(8,128)(2,1)} %bitcast.189, bf16[4,2,2,72,1152]{4,3,2,1,0:T(8,128)(2,1)} %bitcast.187, ...), custom_call_target="tpu_custom_call" | custom-call | tf_op jit(solution)/shard_map/reduce_all/pallas_call | solution.py:454
  738.5 5.1 all-to-all-start.1
  746.0 1.9 copy.101
  748.9 2.2 copy.103
  751.2 2.2 copy.104
  753.6 43.6 %psum.7 = f32[2,2,2,1088]{3,2,1,0:T(2,128)S(1)} all-reduce(f32[2,2,2,1088]{3,2,1,0:T(2,128)S(1)} %bitcast.216), channel_id=1, replica_groups=mesh['section'=2,'ctx'=4,'shard'=4] {'section','ctx','shard'}, use_global_device_ids=true, to_apply=%region_18.19 | all-reduce | flops 8704 | bytes 69632 | tf_op jit(solution)/shard_map/psum | solution.py:592
  797.9 5.8 all_to_all.15
  (269 shorter events, 45.4 us)
Async XLA Ops:
  2.3 4.3 copy-start.37
  2.3 4.3 copy-start.42
  147.9 7.5 slice-start.12
  147.9 7.5 copy-start.40
  148.0 7.8 copy-start.13
  154.9 3.8 copy-start.18
  158.6 3.3 copy-start.33
  158.6 3.3 copy-start.22
  161.5 9.7 %collective-permute-start = (bf16[512,1152]{1,0:T(8,128)(2,1)}, bf16[512,1152]{1,0:T(8,128)(2,1)}, u32[]{:S(2)}, u32[]{:S(2)}) collective-permute-start(bf16[512,1152]{1,0:T(8,128)(2,1)} %convolution_convert_fusion.17.k0_ref), channel_id=1, source_target_pairs={{0,16},{16,0},{1,17},{17,1},{2,18},{18,2},{3,19},{19,3},{4,20},{20... | collective-permute-start | bytes 3538952 | tf_op jit(solution)/shard_map/ppermute | solution.py:175
  164.9 6.3 collective-permute-start.1
  203.3 13.8 %collective-permute-start.2 = (bf16[512,1088]{0,1:T(8,128)(2,1)S(1)}, bf16[512,1088]{0,1:T(8,128)(2,1)S(1)}, u32[]{:S(2)}, u32[]{:S(2)}) collective-permute-start(bf16[512,1088]{0,1:T(8,128)(2,1)S(1)} %fusion.33), channel_id=1, source_target_pairs={{0,1},{4,5},{8,9},{12,13},{16,17},{20,21},{24,25},{28,29}} | collective-permute-start | bytes 3342344 | tf_op jit(solution)/shard_map/ppermute | solution.py:179
  217.1 12.0 %copy-start.8 = (bf16[512,1088]{0,1:T(8,128)(2,1)}, bf16[512,1088]{0,1:T(8,128)(2,1)S(1)}, u32[]{:S(2)}) copy-start(bf16[512,1088]{0,1:T(8,128)(2,1)S(1)} %collective-permute-done.2) | copy-start | bytes 3342340
  240.7 0.9 collective-permute-start.3
  242.0 39.0 %copy-start.5 = (bf16[512,1088]{0,1:T(8,128)(2,1)}, bf16[512,1088]{0,1:T(8,128)(2,1)S(1)}, u32[]{:S(2)}) copy-start(bf16[512,1088]{0,1:T(8,128)(2,1)S(1)} %get-tuple-element.107) | copy-start | bytes 3342340
  247.9 3.7 copy-start.3
  247.9 3.7 collective-permute-start.4
  248.4 4.3 collective-permute-start.5
  281.0 6.1 copy-start.14
  281.0 6.1 copy-start.32
  285.9 50.7 %collective-permute-start.6 = (bf16[512,1088]{0,1:T(8,128)(2,1)}, bf16[512,1088]{0,1:T(8,128)(2,1)}, u32[]{:S(2)}, u32[]{:S(2)}) collective-permute-start(bf16[512,1088]{0,1:T(8,128)(2,1)} %fusion.30), channel_id=1, source_target_pairs={{2,3},{6,7},{10,11},{14,15},{18,19},{22,23},{26,27},{30,31}} | collective-permute-start | bytes 3342344 | tf_op jit(solution)/shard_map/ppermute | solution.py:179
  287.4 49.2 %copy-start.9 = (bf16[512,1088]{0,1:T(8,128)(2,1)S(1)}, bf16[512,1088]{0,1:T(8,128)(2,1)}, u32[]{:S(2)}) copy-start(bf16[512,1088]{0,1:T(8,128)(2,1)} %copy-done.8) | copy-start | bytes 3342340
  336.5 9.7 %slice-start.4 = ((s8[4734976]{0:T(1024)(128)(4,1)}), s8[4194304]{0:T(1024)(128)(4,1)S(1)}, s32[]{:S(2)}) async-start(s8[4734976]{0:T(1024)(128)(4,1)} %bitcast.158), calls=%async_computation.7 | async-start | bytes 8388608
  338.3 153.1 %copy-start = (bf16[512,1088]{0,1:T(8,128)(2,1)}, bf16[512,1088]{0,1:T(8,128)(2,1)S(1)}, u32[]{:S(2)}) copy-start(bf16[512,1088]{0,1:T(8,128)(2,1)S(1)} %get-tuple-element.105) | copy-start | bytes 3342340
  338.7 7.5 slice-start.5
  346.2 5.5 copy-start.10
  377.1 28.6 %copy-start.25 = (bf16[1,4,272,1152]{3,2,1,0:T(8,128)(2,1)S(1)}, bf16[1,4,272,1152]{3,2,1,0:T(8,128)(2,1)}, u32[]{:S(2)}) copy-start(bf16[1,4,272,1152]{3,2,1,0:T(8,128)(2,1)} %get-tuple-element.115) | copy-start | bytes 7520260
  379.6 25.1 %collective-permute-start.7 = (bf16[512,1088]{0,1:T(8,128)(2,1)S(1)}, bf16[512,1088]{0,1:T(8,128)(2,1)S(1)}, u32[]{:S(2)}, u32[]{:S(2)}) collective-permute-start(bf16[512,1088]{0,1:T(8,128)(2,1)S(1)} %fusion.65), channel_id=1, source_target_pairs={{3,2},{7,6},{11,10},{15,14},{19,18},{23,22},{27,26},{31,30}} | collective-permute-start | bytes 3342344 | tf_op jit(solution)/shard_map/ppermute | solution.py:179
  411.2 39.8 %copy-start.6 = (bf16[512,1088]{0,1:T(8,128)(2,1)S(1)}, bf16[512,1088]{0,1:T(8,128)(2,1)}, u32[]{:S(2)}) copy-start(bf16[512,1088]{0,1:T(8,128)(2,1)} %copy-done.5) | copy-start | bytes 3342340
  450.3 4.3 collective-permute-start.9
  450.4 7.3 collective-permute-start.8
  451.0 3.6 copy-start.24
  451.0 3.6 copy-start.46
  462.0 4.6 slice-start.10
  462.0 4.6 slice-start.17
  462.7 3.9 slice-start.11
  462.7 3.9 slice-start.18
  462.8 8.3 %collective-permute-start.10 = (bf16[512,1088]{0,1:T(8,128)(2,1)S(1)}, bf16[512,1088]{0,1:T(8,128)(2,1)S(1)}, u32[]{:S(2)}, u32[]{:S(2)}) collective-permute-start(bf16[512,1088]{0,1:T(8,128)(2,1)S(1)} %fusion.78), channel_id=1, source_target_pairs={{2,1},{6,5},{10,9},{14,13},{18,17},{22,21},{26,25},{30,29}} | collective-permute-start | bytes 3342344 | tf_op jit(solution)/shard_map/ppermute | solution.py:179
  464.0 7.1 slice-start
  464.0 7.1 slice-start.13
  466.7 32.2 %copy-start.54 = (bf16[512,1152]{1,0:T(8,128)(2,1)}, bf16[512,1152]{1,0:T(8,128)(2,1)S(1)}, u32[]{:S(2)}) copy-start(bf16[512,1152]{1,0:T(8,128)(2,1)S(1)} %convolution_convert_fusion.11) | copy-start | bytes 3538948
  466.7 4.5 slice-start.1
  466.7 4.5 slice-start.14
  471.2 14.2 %slice-start.8 = ((s8[4734976]{0:T(1024)(128)(4,1)}), s8[540672]{0:T(1024)(128)(4,1)S(1)}, s32[]{:S(2)}) async-start(s8[4734976]{0:T(1024)(128)(4,1)} %bitcast.167), calls=%async_computation.11 | async-start | bytes 1081344
  477.1 8.2 %slice-start.9 = ((s8[4734976]{0:T(1024)(128)(4,1)}), s8[4194304]{0:T(1024)(128)(4,1)S(1)}, s32[]{:S(2)}) async-start(s8[4734976]{0:T(1024)(128)(4,1)} %bitcast.167), calls=%async_computation.12 | async-start | bytes 8388608
  483.0 5.2 copy-start.52
  483.0 5.2 slice-start.6
  492.7 16.7 %collective-permute-start.11 = (bf16[512,1088]{0,1:T(8,128)(2,1)S(1)}, bf16[512,1088]{0,1:T(8,128)(2,1)S(1)}, u32[]{:S(2)}, u32[]{:S(2)}) collective-permute-start(bf16[512,1088]{0,1:T(8,128)(2,1)S(1)} %fusion.70), channel_id=1, source_target_pairs={{1,0},{5,4},{9,8},{13,12},{17,16},{21,20},{25,24},{29,28}} | collective-permute-start | bytes 3342344 | tf_op jit(solution)/shard_map/ppermute | solution.py:179
  515.3 39.3 %copy-start.53 = (bf16[512,2176]{1,0:T(8,128)(2,1)S(1)}, bf16[512,2176]{1,0:T(8,128)(2,1)}, u32[]{:S(2)}) copy-start(bf16[512,2176]{1,0:T(8,128)(2,1)} %copy-done.52) | copy-start | bytes 6684676
  515.3 39.3 %copy-start.55 = (bf16[512,1152]{1,0:T(8,128)(2,1)S(1)}, bf16[512,1152]{1,0:T(8,128)(2,1)}, u32[]{:S(2)}) copy-start(bf16[512,1152]{1,0:T(8,128)(2,1)} %copy-done.54) | copy-start | bytes 3538948
  554.4 5.8 copy-start.48
  554.4 5.8 copy-start.50
  554.4 15.0 %collective-permute-start.13 = (bf16[512,1152]{1,0:T(8,128)(2,1)}, bf16[512,1152]{1,0:T(8,128)(2,1)}, u32[]{:S(2)}, u32[]{:S(2)}) collective-permute-start(bf16[512,1152]{1,0:T(8,128)(2,1)} %get-tuple-element.47), channel_id=1, source_target_pairs={{0,16},{16,0},{1,17},{17,1},{2,18},{18,2},{3,19},{19,3},{4,20},{20... | collective-permute-start | bytes 3538952 | tf_op jit(solution)/shard_map/ppermute | solution.py:175
  559.8 14.2 %collective-permute-start.12 = (bf16[512,1152]{1,0:T(8,128)(2,1)}, bf16[512,1152]{1,0:T(8,128)(2,1)}, u32[]{:S(2)}, u32[]{:S(2)}) collective-permute-start(bf16[512,1152]{1,0:T(8,128)(2,1)} %get-tuple-element.45), channel_id=1, source_target_pairs={{0,16},{16,0},{1,17},{17,1},{2,18},{18,2},{3,19},{19,3},{4,20},{20... | collective-permute-start | bytes 3538952 | tf_op jit(solution)/shard_map/ppermute | solution.py:175
  569.4 4.6 copy-start.21
  569.4 4.6 copy-start.44
  569.4 7.8 copy-start.31
  569.4 7.8 copy-start.49
  574.1 6.4 slice-start.2
  574.1 6.4 slice-start.15
  590.1 148.5 %all-to-all-start = ((bf16[4,2,64,1088]{3,2,1,0:T(8,128)(2,1)}), bf16[4,2,64,1088]{3,2,1,0:T(8,128)(2,1)}, u32[]{:S(2)}, u32[]{:S(2)}) async-start(bf16[4,2,64,1088]{3,2,1,0:T(8,128)(2,1)} %copy.96), calls=%async_computation | async-start | bytes 2359296 | tf_op jit(solution)/shard_map/all_to_all | solution.py:597
  594.4 5.7 copy-start.43
  594.4 5.7 copy-start.51
  738.5 59.4 %all-to-all-start.1 = ((bf16[4,2,64,1088]{3,2,1,0:T(8,128)(2,1)}), bf16[4,2,64,1088]{3,2,1,0:T(8,128)(2,1)}, u32[]{:S(2)}, u32[]{:S(2)}) async-start(bf16[4,2,64,1088]{3,2,1,0:T(8,128)(2,1)} %all-to-all-done), calls=%async_computation.1 | async-start | bytes 2359296 | tf_op jit(solution)/shard_map/all_to_all | solution.py:598
  746.0 5.1 copy-start.27
  (28 other events, 64.7 us)

commit v3 on v2

--- a/solution.py
+++ b/solution.py
@@ -156,14 +156,6 @@
     )(mask, q, k0, k1, v0, v1, da, o, lse)
 
 
-def normalised(values):
-    mean = jnp.mean(values, axis=-1, keepdims=True)
-    centred = values - mean
-    var = jnp.mean(centred * centred, axis=-1, keepdims=True)
-    scale = lax.rsqrt(var + eps_norm)
-    return centred * scale, scale
-
-
 def norm_backward(hat, scale, gain, grad):
     scaled = grad * gain
     mean = jnp.mean(scaled, axis=-1, keepdims=True)
@@ -193,27 +185,98 @@
     )
 
 
-def gather_kernel(
-    attn_ref, ff_ref, x_ref, g_ref, norm_ref,
-    w_attn_ref, w_ff_ref, x_all_ref, g_all_ref, norm_all_ref,
-    send, recv, token_send, token_recv, norm_send, norm_recv, far_send, far_recv,
+def normalised(values):
+    mean = jnp.mean(values, axis=-1, keepdims=True)
+    centred = values - mean
+    var = jnp.mean(centred * centred, axis=-1, keepdims=True)
+    scale = lax.rsqrt(var + eps_norm)
+    return centred * scale, scale
+
+
+def stack_heads(value, low):
+    zero = jnp.zeros_like(value)
+    return jnp.concatenate([jnp.where(low, value, zero), jnp.where(low, zero, value)], axis=0)
+
+
+def unstack_heads(value, low):
+    rows = value.shape[0] // 2
+    return jnp.where(low, value[:rows], value[rows:])
+
+
+def mask_last(scores, mask):
+    width = mask.shape[1]
+    last = scores[:, scores.shape[1] - width :] + mask
+    if scores.shape[1] == width:
+        return last
+    return jnp.concatenate([scores[:, : scores.shape[1] - width], last], axis=1)
+
+
+def attend_chunk(u, rows, mask_ref, q, k, k1, v, v1, o, lse):
+    size = rows.size
+    keys = pl.ds(0, (u + 1) * size)
+    lane = lax.broadcasted_iota(jnp.int32, (size, LANES), 1)
+    low = lane < HEAD
+
+    @pl.loop(0, q.shape[1] // LANES)
+    def _(pair):
+        cols = pl.ds(pl.multiple_of(pair * LANES, LANES), LANES)
+        q2 = stack_heads(q[rows, cols], low)
+        scores = [mask_last(mm_t(q2, ref[keys, cols]), mask_ref[part]) for part, ref in enumerate((k, k1))]
+        top = jnp.maximum(
+            jnp.max(scores[0], axis=1, keepdims=True), jnp.max(scores[1], axis=1, keepdims=True)
+        )
+        total, acc = 0.0, 0.0
+        for s, ref in zip(scores, (v, v1)):
+            p = jnp.exp(s - top)
+            total = total + jnp.sum(p, axis=1, keepdims=True)
+            acc = acc + mm(p.astype(bf16), ref[keys, cols])
+        o[rows, cols] = unstack_heads(acc / total, low)
+        level = top + jnp.log(total)
+        lse[rows, :] = jnp.where(
+            lane == 2 * pair, level[:size], jnp.where(lane == 2 * pair + 1, level[size:], lse[rows, :])
+        )
+
+
+def near_ctx(c, step):
+    return c + step - 2 * step * lax.rem(c // step, 2)
+
+
+def forward_kernel(
+    attn_ref, ff_ref, x_ref, g_ref, norm_ref, mask_ref,
+    w_attn_out, w_ff_out, g_all_ref, norm_out,
+    ent_out, nrm_out, q_out, k_out, k1_out, v_out, v1_out, o_out, lse_out, up_out, hid_out, lea_out,
+    w, x_all, norm_all, norms, ent, nrm, q, k, k1, v, v1, o, lse, up, hid, lea,
+    send, recv, token_send, token_recv, norm_send, norm_recv, far_send,
+    hop_send, hop_recv, swap_send, swap_recv, save, keep,
 ):
     section, ctx, shard = lax.axis_index("section"), lax.axis_index("ctx"), lax.axis_index("shard")
     kind = lax.rem(shard, 2)
-    x_near, y_near = 1, 2
-    near = lambda c, step: c + step - 2 * step * lax.rem(c // step, 2)
     far_core = 1 - shard // 2
-
-    x_copy = remote(x_ref, x_all_ref.at[ctx], token_send.at[0], token_recv.at[ctx], section, shard, 0)
+    x_ctx, y_ctx = near_ctx(ctx, 1), near_ctx(ctx, 2)
+    d_ctx = near_ctx(x_ctx, 2)
+    width = ent.shape[1]
+    wide = q.shape[1]
+    size = 2 * x_ref.shape[1]
+    chunks = ent.shape[0] // size
+    attn_cols = pl.ds(0, attn_ref.shape[1])
+    ff_cols = pl.ds(0, ff_ref.shape[1])
+
+    x_copy = remote(x_ref, x_all.at[ctx], token_send.at[0], token_recv.at[ctx], section, shard, 0)
     g_copy = remote(g_ref, g_all_ref.at[ctx], token_send.at[1], token_recv.at[ctx], section, shard, 3)
     x_stays = (shard == 0) & (ctx == 0)
     g_stays = (shard == 3) & (ctx == 3)
     attn_copy = remote(
-        attn_ref, w_attn_ref.at[ctx, shard], far_send.at[0], recv.at[ctx, shard], far_core, ctx, 2 * section
+        attn_ref, w.at[ctx, shard, :, attn_cols], far_send.at[0], recv.at[ctx, shard], far_core, ctx, 2 * section
     )
     ff_copy = remote(
-        ff_ref, w_ff_ref.at[ctx, shard], far_send.at[1], recv.at[ctx, shard], far_core, ctx, 2 * section + 1
-    )
+        ff_ref, w.at[ctx, shard, :, ff_cols], far_send.at[1], recv.at[ctx, shard], far_core, ctx, 2 * section + 1
+    )
+    x_local = pltpu.make_async_copy(x_ref, x_all.at[ctx], token_recv.at[ctx])
+    norm_local = pltpu.make_async_copy(norm_ref, norm_all.at[shard], norm_recv.at[shard])
+
+    @pl.when(x_stays)
+    def _():
+        x_local.start()
 
     @pl.when(jnp.logical_not(x_stays))
     def _():
@@ -223,14 +286,17 @@
     norm_copies = []
     for core in range(2):
         for stage in range(2):
-            index = core * 2 + stage
             copy = remote(
-                norm_ref, norm_all_ref.at[shard], norm_send.at[index], norm_recv.at[shard],
+                norm_ref, norm_all.at[shard], norm_send.at[core * 2 + stage], norm_recv.at[shard],
                 core, ctx, 2 * section + stage,
             )
             stays = (section == core) & (shard == 2 * section + stage)
             norm_copies.append((copy, stays))
 
+            @pl.when(stays)
+            def _():
+                norm_local.start()
+
             @pl.when(jnp.logical_not(stays))
             def _():
                 copy.start()
@@ -241,24 +307,21 @@
     def _():
         g_copy.start()
 
-    def spread(out_ref):
-        def piece(c, s, which, core, to_ctx):
-            return remote(
-                out_ref.at[c, s], out_ref.at[c, s], send.at[which], recv.at[c, s], core, to_ctx, shard
-            )
-
+    def piece(cols, c, s, which, core, to_ctx):
+        ref = w.at[c, s, :, cols]
+        return remote(ref, ref, send.at[which], recv.at[c, s], core, to_ctx, shard)
+
+    def collect(cols):
         mine = [2 * (1 - section) + j for j in range(2)]
-        x_ctx, y_ctx = near(ctx, x_near), near(ctx, y_near)
-        d_ctx = near(x_ctx, y_near)
         started = []
 
         def go(c, s, core, to_ctx):
-            copy = piece(c, s, len(started), core, to_ctx)
+            copy = piece(cols, c, s, len(started), core, to_ctx)
             copy.start()
             started.append(copy)
 
         def arrived(c, s):
-            piece(c, s, 0, section, ctx).wait_recv()
+            piece(cols, c, s, 0, section, ctx).wait_recv()
 
         for s in mine:
             arrived(ctx, s)
@@ -281,28 +344,139 @@
         for c in (ctx, x_ctx, y_ctx, d_ctx):
             for j in range(2):
                 arrived(c, 2 * section + j)
+        for s in range(4):
+            pltpu.make_async_copy(norm_ref, norm_all.at[s], norm_recv.at[s]).wait()
+        norms[...] = (norm_all[0] + norm_all[1]) + (norm_all[2] + norm_all[3])
+        return started
+
+    def hop_copy(u):
+        rows = pl.ds(u * size, size)
+        return remote(lea.at[rows], ent.at[rows], hop_send.at[u], hop_recv.at[u], section, ctx, shard + 1)
+
+    def hop_wait(u):
+        rows = pl.ds(u * size, size)
+        remote(lea.at[rows], ent.at[rows], hop_send.at[u], hop_recv.at[u], section, ctx, shard).wait_recv()
+
+    def weight(c, columns):
+        value = w[c, :, :, pl.ds(0, columns)]
+        return value.reshape(value.shape[0] * value.shape[1], columns)
+
+    def saves(u, pairs):
+        rows = pl.ds(u * size, size)
+        copies = []
+        for index, (src, dst) in enumerate(pairs):
+            if len(src.shape) == 3:
+                copies.append(pltpu.make_async_copy(src.at[:, rows], dst.at[:, rows], save.at[index, u]))
+            else:
+                copies.append(pltpu.make_async_copy(src.at[rows], dst.at[rows], save.at[index, u]))
+        return copies
+
+    norm_save = pltpu.make_async_copy(norms, norm_out, keep.at[1])
+
+    @pl.when(kind == 0)
+    def _():
+        started = collect(attn_cols)
+        norm_save.start()
+        w_save = pltpu.make_async_copy(w.at[:, :, :, attn_cols], w_attn_out, keep.at[0])
+        w_save.start()
+
+        @pl.when(shard == 0)
+        def _():
+            for c in range(4):
+                pltpu.make_async_copy(x_ref, x_all.at[c], token_recv.at[c]).wait()
+
+        lse[...] = jnp.zeros_like(lse)
+        gain, bias = norms[0:1, :width], norms[2:3, :width]
+        pairs = ((ent, ent_out), (nrm, nrm_out), (q, q_out), (k, k_out), (k1, k1_out), (v, v_out), (v1, v1_out), (o, o_out), (lse, lse_out))
+        for u in range(chunks):
+            rows = pl.ds(u * size, size)
+
+            @pl.when(shard == 0)
+            def _():
+                first = 2 * (u % 2)
+                ent[rows] = x_all[first : first + 2, u // 2].reshape(size, width)
+
+            @pl.when(shard > 0)
+            def _():
+                hop_wait(u)
+
+            hat, _ = normalised(ent[rows].astype(f32))
+            normed = (hat * gain + bias).astype(bf16)
+            nrm[rows] = normed
+            k[rows] = mm(normed, weight(1, wide)).astype(bf16)
+            v[rows] = mm(normed, weight(2, wide)).astype(bf16)
+            swaps = [
+                remote(src.at[rows], dst.at[rows], swap_send.at[which, u], swap_recv.at[which, u], 1 - section, ctx, shard)
+                for which, (src, dst) in enumerate(((k, k1), (v, v1)))
+            ]
+            for copy in swaps:
+                copy.start()
+            q[rows] = (mm(normed, weight(0, wide)) * score_scale).astype(bf16)
+            for copy in swaps:
+                copy.wait_recv()
+            attend_chunk(u, rows, mask_ref, q, k, k1, v, v1, o, lse)
+            out = mm(o[rows, :width].astype(bf16), weight(3, wide))[:, :width]
+            lea[rows] = (ent[rows].astype(f32) + out).astype(bf16)
+            hop_copy(u).start()
+            for copy in saves(u, pairs):
+                copy.start()
+        for u in range(chunks):
+            rows = pl.ds(u * size, size)
+            for which, (src, dst) in enumerate(((k, k1), (v, v1))):
+                remote(
+                    src.at[rows], dst.at[rows], swap_send.at[which, u], swap_recv.at[which, u], 1 - section, ctx, shard
+                ).wait_send()
+            hop_copy(u).wait_send()
+            for copy in saves(u, pairs):
+                copy.wait()
+        w_save.wait()
+        norm_save.wait()
         for copy in started:
             copy.wait_send()
 
-    @pl.when(kind == 0)
-    def _():
-        spread(w_attn_ref)
-
     @pl.when(kind == 1)
     def _():
-        spread(w_ff_ref)
-
-    for s in range(4):
-
-        @pl.when(jnp.logical_not((section == shard // 2) & (shard == s)))
-        def _():
-            remote(norm_ref, norm_all_ref.at[s], norm_send.at[0], norm_recv.at[s], section, ctx, shard).wait_recv()
+        started = collect(ff_cols)
+        norm_save.start()
+        w_save = pltpu.make_async_copy(w, w_ff_out, keep.at[0])
+        w_save.start()
+        gain, bias = norms[1:2, :width], norms[3:4, :width]
+        pairs = ((ent, ent_out), (nrm, nrm_out), (lea, lea_out), (up, up_out), (hid, hid_out))
+        for u in range(chunks):
+            rows = pl.ds(u * size, size)
+            hop_wait(u)
+            hat, _ = normalised(ent[rows].astype(f32))
+            normed = (hat * gain + bias).astype(bf16)
+            nrm[rows] = normed
+            total = ent[rows].astype(f32)
+            for i in range(2):
+                upper = mm(normed, weight(i, ff_ref.shape[1]))
+                up[i, rows] = upper
+                hidden = jax.nn.gelu(upper, approximate=True).astype(bf16)
+                hid[i, rows] = hidden
+                total = total + mm_t(hidden, weight(2 + i, ff_ref.shape[1]))
+            lea[rows] = total.astype(bf16)
+
+            @pl.when(shard < 3)
+            def _():
+                hop_copy(u).start()
+
+            for copy in saves(u, pairs):
+                copy.start()
+        for u in range(chunks):
+
+            @pl.when(shard < 3)
+            def _():
+                hop_copy(u).wait_send()
+
+            for copy in saves(u, pairs):
+                copy.wait()
+        w_save.wait()
+        norm_save.wait()
+        for copy in started:
+            copy.wait_send()
 
     for c in range(4):
-
-        @pl.when((shard == 0) & jnp.logical_not((ctx == 0) & (c == 0)))
-        def _():
-            remote(x_ref, x_all_ref.at[c], token_send.at[0], token_recv.at[c], section, ctx, shard).wait_recv()
 
         @pl.when((shard == 3) & jnp.logical_not((ctx == 3) & (c == 3)))
         def _():
@@ -325,20 +499,42 @@
             copy.wait_send()
 
 
-def gather_all(attn_piece, ff_piece, x_own, g_own, norm_own):
-    like = lambda lead, v: jax.ShapeDtypeStruct(lead + v.shape, v.dtype)
+def forward_relay(attn_piece, ff_piece, x_own, g_own, norm_own, mask):
+    share, ff_half = ff_piece.shape
+    wide = attn_piece.shape[1]
+    blocks, half, width = x_own.shape
+    tokens = blocks * 4 * half
+    chunks = tokens // (2 * half)
     dma = pltpu.SemaphoreType.DMA
+    vmem = pl.BlockSpec(memory_space=pltpu.VMEM)
+    state = [
+        ((tokens, width), bf16), ((tokens, width), bf16),
+        ((tokens, wide), bf16), ((tokens, wide), bf16), ((tokens, wide), bf16), ((tokens, wide), bf16), ((tokens, wide), bf16),
+        ((tokens, wide), f32), ((tokens, LANES), f32),
+        ((2, tokens, ff_half), f32), ((2, tokens, ff_half), bf16), ((tokens, width), bf16),
+    ]
+    outs = [
+        ((4, 4, share, wide), bf16), ((4, 4, share, ff_half), bf16), ((4,) + g_own.shape, bf16), (norm_own.shape, f32),
+    ] + state
     return pl.pallas_call(
-        gather_kernel,
-        in_specs=[ANY] * 5,
-        out_specs=[ANY] * 5,
-        out_shape=[
-            like((4, 4), attn_piece), like((4, 4), ff_piece), like((4,), x_own), like((4,), g_own), like((4,), norm_own),
+        forward_kernel,
+        in_specs=[ANY] * 5 + [vmem],
+        out_specs=[ANY] * len(outs),
+        out_shape=[jax.ShapeDtypeStruct(s, t) for s, t in outs],
+        scratch_shapes=[
+            pltpu.VMEM((4, 4, share, ff_half), bf16),
+            pltpu.VMEM((4,) + x_own.shape, bf16),
+            pltpu.VMEM((4,) + norm_own.shape, f32),
+            pltpu.VMEM(norm_own.shape, f32),
+        ]
+        + [pltpu.VMEM(s, t) for s, t in state]
+        + [
+            dma((14,)), dma((4, 4)), dma((2,)), dma((4,)), dma((4,)), dma((4,)), dma((2,)),
+            dma((chunks,)), dma((chunks,)), dma((2, chunks)), dma((2, chunks)), dma((9, chunks)), dma((2,)),
         ],
-        scratch_shapes=[dma((14,)), dma((4, 4)), dma((2,)), dma((4,)), dma((4,)), dma((4,)), dma((2,)), dma((2,))],
-        compiler_params=pltpu.CompilerParams(has_side_effects=True),
-        name="gather_all",
-    )(attn_piece, ff_piece, x_own, g_own, norm_own)
+        compiler_params=pltpu.CompilerParams(has_side_effects=True, vmem_limit_bytes=62 * 2**20),
+        name="forward_relay",
+    )(attn_piece, ff_piece, x_own, g_own, norm_own, mask)
 
 
 def add_into(total, term):
@@ -492,52 +688,32 @@
     down_t = down_weight[0].T
     up0 = up_weight[0]
     ff_src = jnp.stack([up0[:, : ff // 2], up0[:, ff // 2 :], down_t[:, : ff // 2], down_t[:, ff // 2 :]])
-    norm_own = jnp.concatenate([norm_gain[0], norm_bias[0], jnp.zeros((4, share), bf16)], axis=0)
+    norm_own = jnp.concatenate([norm_gain[0], norm_bias[0]], axis=0).astype(f32)
+    norm_own = lax.dynamic_update_slice(
+        jnp.zeros((ROWS, wide), f32), jnp.pad(norm_own, ((0, ROWS - 4), (0, 0))), (0, shard * share)
+    )
     x_own = lax.dynamic_slice_in_dim(inputs[0], section * half, half, 1)
     g_own = lax.dynamic_slice_in_dim(cotangent[0], section * half, half, 1)
-    w_attn, w_ff, x_all, g_all, norm_all = gather_all(
+    mask = attention_masks(section, half)
+    w_attn, w_ff, g_all, norms, ent, nrm, q, k, k1, v, v1, o, lse, up, hid, y = forward_relay(
         lax.dynamic_index_in_dim(attn_src, ctx, 0, keepdims=False),
         lax.dynamic_index_in_dim(ff_src, ctx, 0, keepdims=False),
-        x_own, g_own, norm_own,
+        x_own, g_own, norm_own, jnp.concatenate([mask, mask], axis=1),
     )
     w_attn = w_attn.reshape(4, width, wide)
     w_ff = w_ff.reshape(4, width, ff // 2)
     own_place = jnp.arange(4)[:, None, None]
-    norm_all = jnp.where((own_place == shard) & (section == shard // 2), norm_own, norm_all)
-    norms = jnp.swapaxes(norm_all[:, :4], 0, 1).reshape(4, width).astype(f32)
-    gain1, gain2, bias1, bias2 = norms[0], norms[1], norms[2], norms[3]
+    gain1, gain2 = norms[0, :width], norms[1, :width]
 
     def bring_tokens(every, own):
         mine = jnp.where((own_place[..., None] == ctx) & (shard == ctx), own, every)
         return jnp.swapaxes(mine, 0, 1).reshape(tokens, width)
 
-    x_first, g_last = bring_tokens(x_all, x_own), bring_tokens(g_all, g_own)
-    mask = attention_masks(section, half)
+    g_last = bring_tokens(g_all, g_own)
     feature = lax.broadcasted_iota(jnp.int32, (width, 16 * group_pad), 0)
     place = lax.broadcasted_iota(jnp.int32, (width, 16 * group_pad), 1)
     spread = (feature // group * group_pad + feature % group == place).astype(bf16)
     grouped = lambda v: mm(v, spread).astype(bf16)
-
-    def attn_forward(x):
-        x = x.astype(f32)
-        hat, scale = normalised(x)
-        normed = (hat * gain1 + bias1).astype(bf16)
-        q = (mm(normed, w_attn[0]) * score_scale).astype(bf16)
-        k = mm(normed, w_attn[1]).astype(bf16)
-        v = mm(normed, w_attn[2]).astype(bf16)
-        k1, v1 = swap_cores(k), swap_cores(v)
-        o, ob, lse = attention_forward(mask, q, k, k1, v, v1, half)
-        middle = x + mm(ob[:, :width], w_attn[3])[:, :width]
-        return middle.astype(bf16), (hat, scale, normed, q, k, k1, v, v1, o, ob, lse)
-
-    def ff_forward(middle):
-        middle = middle.astype(f32)
-        hat, scale = normalised(middle)
-        normed = (hat * gain2 + bias2).astype(bf16)
-        upper = [mm(normed, w_ff[i]) for i in range(2)]
-        hidden = [jax.nn.gelu(u, approximate=True).astype(bf16) for u in upper]
-        y = middle + mm_t(hidden[0], w_ff[2]) + mm_t(hidden[1], w_ff[3])
-        return y.astype(bf16), (hat, scale, normed, upper, hidden)
 
     def ff_backward(g, state):
         hat, scale, normed, upper, hidden = state
@@ -562,13 +738,9 @@
         dx = d_middle.astype(f32) + norm_backward(hat, scale, gain1, d_normed)
         return dx.astype(bf16), d_mixed, d_normed
 
-    middle, _ = attn_forward(x_first)
-    middle0 = hop(middle, 0, 1)
-    y, _ = ff_forward(middle0)
-    x = jnp.where(shard == 0, x_first, hop(y, 1, 2))
-    middle, attn_state = attn_forward(x)
-    middle = jnp.where(shard == 1, middle0, hop(middle, 2, 3))
-    y, ff_state = ff_forward(middle)
+    hat, scale = normalised(ent.astype(f32))
+    attn_state = (hat, scale, nrm, q, k, k1, v, v1, o, o.astype(bf16), lse)
+    ff_state = (hat, scale, nrm, (up[0], up[1]), (hid[0], hid[1]))
 
     d_middle, _, _ = ff_backward(g_last, ff_state)
     d_middle1 = hop(d_middle, 3, 2)

time: 814 us -> 726 us (0.89)
  matrix products: 185 us -> 132 us
  waiting for transfers between devices: 70 us -> 32.2 us
    dot_general x39 -> x24, matrix products: 185 us -> 132 us  [dot(): return lax.dot_general(a, b, (dims, ((), ())), preferred_element_type=f32)]
    ppermute x6 -> x3, waiting for transfers between devices: 69.9 us -> 18.1 us  [hop(): return lax.ppermute(value, 'shard', [(source, target)])]
    all_to_all x1, waiting for transfers between devices: 0.01 us -> 14.1 us  [chain(): final = lax.all_to_all(jnp.swapaxes(final, 0, 1), 'ctx', 0, 0)]
    pallas_call x3 -> x1, Pallas kernels: 192 us -> 185 us  [forward_relay(): pl.pallas_call(forward_kernel, in_specs=[ANY] * 5 + [vmem], out_specs=[AN...]
    unnamed x156 -> x144, local copies, waits for them, and re-layouts: 17 us -> 18 us
    slice x5 -> x3, local copies, waits for them, and re-layouts: 20 us -> 20.5 us  [the longest x1 12.6 us: ff_backward(): d_hidden = mm(g, w_ff[2 + i])]
  transfers between devices with their start and end apart: 16 -> 9, of which waited for: 3 -> 2; matrix products, arithmetic and copies ran while one was open for 12% -> 9% of each run, Pallas kernels for 16% -> 0%
where the time goes in v3:
time: 726 us; the launch traced here: 714 us
  Pallas kernels  400 us (55%)
  matrix products  132 us (18%)
  local copies, waits for them, and re-layouts  66.5 us (9%)
  blocking collectives  45.4 us (6%)
  waiting for transfers between devices  32.2 us (4%)
  other arithmetic  18.7 us (3%)
  starting transfers between devices  16.3 us (2%)
    pallas_call x1, Pallas kernels, forward_relay(): pl.pallas_call(forward_kernel, in_specs=[ANY] * 5 + [vmem], out_specs=[AN...  185 us
    pallas_call x1, Pallas kernels, reduce_all(): pl.pallas_call(reduce_kernel, in_specs=[ANY] * (2 * count), out_specs=[AN...  137 us
    dot_general x24, matrix products, dot(): return lax.dot_general(a, b, (dims, ((), ())), preferred_element_type=f32)  132 us
    pallas_call x2, Pallas kernels, attention_backward(): pl.pallas_call(functools.partial(attention_backward_kernel, half), grid=(...  78.1 us
    psum x1, blocking collectives, chain(): lax.psum(terms, ('section', 'ctx', 'shard')).reshape(2, 2, 2, width)  39.6 us
    ppermute x3, waiting for transfers between devices, hop(): return lax.ppermute(value, 'shard', [(source, target)])  18.1 us
    unnamed x144, local copies, waits for them, and re-layouts  18 us
  transfers between devices with their start and end apart: 9, of which 2 were waited for; matrix products, arithmetic and copies ran while one was open for 9% of the time, Pallas kernels for 0%

profile of v3, /device:TPU:24, one launch (start us, length us, event | category | flops | bytes accessed | tf_op | source)
XLA Modules:
  0.0 714.0 jit_solution(2593473601749891578)
XLA Ops:
  0.7 1.6 fusion.107
  6.2 1.2 pad_bitcast_fusion.1
  7.4 2.2 fusion.74
  10.2 3.7 slice_bitcast_fusion
  14.5 1.4 dynamic_update_slice.3.norm_ref
  15.9 2.5 fusion.73.attn_ref
  18.5 2.0 fusion.64.ff_ref
  20.4 185.0 %forward_relay.1 = (bf16[4,4,272,1152]{3,2,1,0:T(8,128)(2,1)}, bf16[4,4,272,2176]{3,2,1,0:T(8,128)(2,1)}, bf16[4,2,64,1088]{3,2,1,0:T(8,128)(2,1)}, f32[8,1152]{...) custom-call(bf16[272,1152]{1,0:T(8,128)(2,1)} %fusion.73.attn_ref, ...), custom_call_target="tpu_custom_call" | custom-call | tf_op jit(solution)/shard_map/forward_relay/pallas_call | solution.py:519
  205.5 1.5 select_bitcast_fusion
  207.0 12.6 %fusion.105 = (bf16[1,4,272,2176]{3,2,1,0:T(8,128)(2,1)}, bf16[1,4,272,2176]{3,2,1,0:T(8,128)(2,1)}, bf16[1,4,272,2176]{3,2,1,0:T(8,128)(2,1)}, bf16[1,4,272,2176]{3,2,1,0:T(8,128)(2,1)}) fusion(bf16[4,4,272,2176]{3,2,1,0:T(8,128)(2,1)} %get-tuple-element.38), kind=kLoop, calls=%fused_computation.215 | loop fusion | bytes 37879808 | tf_op jit(solution)/shard_map/slice | solution.py:722
  221.3 13.5 %fusion.60 = f32[512,1088]{1,0:T(8,128)} fusion(bf16[1088,2176]{1,0:T(8,128)(2,1)} %bitcast.194, f32[2,512,2176]{2,1,0:T(8,128)} %get-tuple-element.39, bf16[512,1088]{1,0:T(8,128)(2,1)S(1)} %bitcast.184, bf16[1088,2176]{1,0:T(8,128)(2,1)} %bitcast.202), kind=kOutput, calls=%fused_computation.109 | convolution fusion | flops 4870897664 | bytes 17268736 | tf_op jit(solution)/shard_map/dot_general | solution.py:26
  234.8 14.6 %fusion.104 = (f32[512]{0:T(512)S(1)}, f32[512]{0:T(512)S(1)}, f32[512,1088]{1,0:T(8,128)}) fusion(f32[512]{0:T(512)S(1)} %add_rsqrt_fusion, f32[512]{0:T(512)S(1)} %broadcast_multiply_fusion.8, bf16[512,1088]{1,0:T(8,128)(2,1)S(1)} %copy-done, f32[1088]{0:T(1024)S(1)} %get-tuple-element.115, f32[512,1088]{1,0:T(8,128)} %fusion.60, ...), kind=kOutput, calls=%fused_computation.214 | convolution fusion | flops 4875353088 | bytes 20754688 | tf_op jit(solution)/shard_map/dot_general | solution.py:26
  249.4 2.5 fusion.33
  252.0 1.4 copy.117
  253.3 2.8 collective-permute-start
  256.2 6.9 fusion.106
  263.1 18.1 %collective-permute-done = bf16[512,1088]{0,1:T(8,128)(2,1)S(1)} collective-permute-done((bf16[512,1088]{0,1:T(8,128)(2,1)}, bf16[512,1088]{0,1:T(8,128)(2,1)S(1)}, u32[]{:S(2)}, u32[]{:S(2)}) %collective-permute-start) | collective-permute-done | bytes 1114144 | tf_op jit(solution)/shard_map/ppermute | solution.py:171
  282.2 2.6 convolution_convert_fusion.8
  284.8 1.7 copy.119
  286.5 1.1 pad.41.da_ref
  287.6 38.9 %attention_backward.2 = (bf16[512,1152]{1,0:T(8,128)(2,1)}, f32[512,1152]{1,0:T(8,128)}, bf16[512,1152]{1,0:T(8,128)(2,1)}, f32[512,1152]{1,0:T(8,128)}, bf16[512,1152]{1,0:T(8,128)(2,1)}) custom-call(f32[2,128,128]{2,1,0:T(8,128)} %copy-done.17, bf16[512,1152]{1,0:T(8,128)(2,1)} %get-tuple-element.41.q_ref, bf16[512,1152]{1,0:T(8,128)(2,1)} %get-tuple-element.42.k0_ref, ...), custom_call_target="tpu_custom_call" | custom-call | tf_op jit(solution)/shard_map/attention_backward/pallas_call | solution.py:148
  327.1 1.7 copy.128
  328.8 4.1 fusion.115
  332.9 3.4 convolution_add_fusion.4
  336.4 3.6 fusion.103
  340.0 2.0 fusion.38
  342.0 2.3 copy.123
  344.3 1.8 collective-permute-start.3
  346.8 4.9 convolution_convert_fusion.11
  351.7 2.4 copy.124
  354.4 7.3 %fusion.116 = f32[512,2176]{1,0:T(8,128)} fusion(bf16[512,1088]{1,0:T(8,128)(2,1)S(1)} %broadcast_select_fusion, bf16[1088,2176]{1,0:T(8,128)(2,1)} %bitcast.203), kind=kOutput, calls=%fused_computation.224 | convolution fusion | flops 2424307712 | bytes 10305536 | tf_op jit(solution)/shard_map/dot_general | solution.py:26
  361.7 2.6 convolution_convert_fusion.9
  364.3 5.2 convolution_convert_fusion.1
  369.6 5.3 convolution_convert_fusion
  374.9 10.6 %add_convert_fusion = (bf16[512,2176]{1,0:T(8,128)(2,1)}, bf16[512,2176]{1,0:T(8,128)(2,1)}) fusion(f32[2,512,2176]{2,1,0:T(8,128)S(1)} %bitcast.234, f32[512,2176]{1,0:T(8,128)} %fusion.116, bf16[512,1088]{1,0:T(8,128)(2,1)S(1)} %broadcast_select_fusion, bf16[1088,2176]{1,0:T(8,128)(2,1)S(1)} %bitcast.201), kind=kOutput, calls=%fused_computation.37 | convolution fusion | flops 2468872192 | bytes 23674880 | tf_op jit(solution)/shard_map/dot_general | solution.py:26
  385.6 5.0 fusion.117
  390.6 3.6 multiply_reduce_fusion.1
  394.3 1.4 copy-done.15
  398.2 7.3 %convolution_convert_fusion.2 = bf16[1152,2176]{1,0:T(8,128)(2,1)} fusion(bf16[512,1152]{1,0:T(8,128)(2,1)} %convolution_convert_fusion.11, bf16[512,2176]{1,0:T(8,128)(2,1)} %get-tuple-element.124), kind=kOutput, calls=%fused_computation.2 | convolution fusion | flops 2569420800 | bytes 8421376 | tf_op jit(solution)/shard_map/dot_general | solution.py:26
  405.5 5.2 convolution_convert_fusion.3
  413.5 1.6 convolution_convert_fusion.12
  415.9 1.1 pad.43.da_ref
  417.0 39.2 %attention_backward.3 = (bf16[512,1152]{1,0:T(8,128)(2,1)}, f32[512,1152]{1,0:T(8,128)}, bf16[512,1152]{1,0:T(8,128)(2,1)}, f32[512,1152]{1,0:T(8,128)}, bf16[512,1152]{1,0:T(8,128)(2,1)}) custom-call(f32[2,128,128]{2,1,0:T(8,128)} %copy-done.17, bf16[512,1152]{1,0:T(8,128)(2,1)} %get-tuple-element.41.q_ref, bf16[512,1152]{1,0:T(8,128)(2,1)} %get-tuple-element.42.k0_ref, ...), custom_call_target="tpu_custom_call" | custom-call | tf_op jit(solution)/shard_map/attention_backward/pallas_call | solution.py:148
  456.4 4.7 fusion.118
  461.7 1.7 convolution_convert_fusion.7
  463.5 7.9 %convolution_convert_fusion.4 = bf16[1152,1152]{1,0:T(8,128)(2,1)} fusion(bf16[512,1088]{1,0:T(8,128)(2,1)} %copy-done.3, f32[512,1152]{1,0:T(8,128)} %get-tuple-element.47.o_ref, s32[1088]{0:T(1024)S(1)} %copy-done.30, s32[1088]{0:T(1024)S(1)} %copy-done.33, s32[1088]{0:T(1024)S(1)} %copy-done.27, s32[1088]{0:T(1024)S(1)} %copy-done.36, ...), kind=kOutput, calls=%fused_computation.4 | convolution fusion | flops 2650595328 | bytes 5033088 | tf_op jit(solution)/shard_map/dot_general | solution.py:26
  471.3 5.8 convolution_convert_fusion.5
  477.1 4.5 convolution_convert_fusion.6
  481.7 137.0 %reduce_all.1 = (bf16[4,72,1152]{2,1,0:T(8,128)(2,1)S(1)}, bf16[4,72,2176]{2,1,0:T(8,128)(2,1)S(1)}) custom-call(bf16[4,2,2,72,1152]{4,3,2,1,0:T(8,128)(2,1)S(1)} %bitcast.183, bf16[4,2,2,72,1152]{4,3,2,1,0:T(8,128)(2,1)} %bitcast.211, bf16[4,2,2,72,1152]{4,3,2,1,0:T(8,128)(2,1)} %bitcast.210, bf16[4,2,2,72,1152]{4,3,2,1,0:T(8,128)(2,1)} %bitcast.209, ...), custom_call_target="tpu_custom_call" | custom-call | tf_op jit(solution)/shard_map/reduce_all/pallas_call | solution.py:650
  618.9 1.2 slice_bitcast_fusion.5
  621.7 3.4 convolution_add_fusion.1
  625.6 4.0 fusion.49
  629.6 1.4 fusion.65
  631.1 1.1 copy.154
  632.2 4.3 all-to-all-start
  637.8 14.1 %all-to-all-done = bf16[4,2,64,1088]{3,2,1,0:T(8,128)(2,1)} async-done(((bf16[4,2,64,1088]{3,2,1,0:T(8,128)(2,1)}), bf16[4,2,64,1088]{3,2,1,0:T(8,128)(2,1)}, u32[]{:S(2)}, u32[]{:S(2)}) %all-to-all-start) | async-done | bytes 1114144 | tf_op jit(solution)/shard_map/all_to_all | solution.py:769
  651.9 5.4 all-to-all-start.1
  657.4 2.2 copy.142
  659.6 2.2 copy.141
  662.2 1.9 copy.139
  665.2 39.6 %psum.7 = f32[2,2,2,1088]{3,2,1,0:T(2,128)S(1)} all-reduce(f32[2,2,2,1088]{3,2,1,0:T(2,128)S(1)} %bitcast.228), channel_id=1, replica_groups=mesh['section'=2,'ctx'=4,'shard'=4] {'section','ctx','shard'}, use_global_device_ids=true, to_apply=%region_12.13 | all-reduce | flops 8704 | bytes 69632 | tf_op jit(solution)/shard_map/psum | solution.py:764
  705.5 5.8 all_to_all.15
  711.4 1.1 copy.137
  712.5 1.1 copy.138
  (205 shorter events, 21.9 us)
Async XLA Ops:
  2.7 4.6 copy-start.20
  2.7 4.6 copy-start.43
  6.2 3.4 copy-start.44
  6.2 3.4 copy-start.45
  15.9 2.5 copy-start.2
  20.4 185.0 %copy-start.5 = (bf16[1,2,64,1088]{3,2,1,0:T(8,128)(2,1)S(1)}, bf16[1,2,64,1088]{3,2,1,0:T(8,128)(2,1)}, u32[]{:S(2)}) copy-start(bf16[1,2,64,1088]{3,2,1,0:T(8,128)(2,1)} %copy.112) | copy-start | bytes 835588
  207.0 12.7 %copy-start = (bf16[512,1088]{1,0:T(8,128)(2,1)S(1)}, bf16[512,1088]{1,0:T(8,128)(2,1)}, u32[]{:S(2)}) copy-start(bf16[512,1088]{1,0:T(8,128)(2,1)} %get-tuple-element.37) | copy-start | bytes 3342340
  221.3 13.5 %copy-start.23 = (f32[1088]{0:T(1024)}, f32[1088]{0:T(1024)S(1)}, u32[]{:S(2)}) copy-start(f32[1088]{0:T(1024)S(1)} %get-tuple-element.115) | copy-start | bytes 13060
  253.3 27.8 %collective-permute-start = (bf16[512,1088]{0,1:T(8,128)(2,1)}, bf16[512,1088]{0,1:T(8,128)(2,1)S(1)}, u32[]{:S(2)}, u32[]{:S(2)}) collective-permute-start(bf16[512,1088]{0,1:T(8,128)(2,1)} %copy.117), channel_id=1, source_target_pairs={{3,2},{7,6},{11,10},{15,14},{19,18},{23,22},{27,26},{31,30}} | collective-permute-start | bytes 3342344 | tf_op jit(solution)/shard_map/ppermute | solution.py:171
  263.1 18.1 %copy-start.11 = (bf16[1,4,272,1152]{3,2,1,0:T(8,128)(2,1)}, bf16[1,4,272,1152]{3,2,1,0:T(8,128)(2,1)S(1)}, u32[]{:S(2)}) copy-start(bf16[1,4,272,1152]{3,2,1,0:T(8,128)(2,1)S(1)} %get-tuple-element.123) | copy-start | bytes 7520260
  326.5 6.4 collective-permute-start.1
  326.6 9.7 %collective-permute-start.2 = (bf16[512,1152]{1,0:T(8,128)(2,1)}, bf16[512,1152]{1,0:T(8,128)(2,1)}, u32[]{:S(2)}, u32[]{:S(2)}) collective-permute-start(bf16[512,1152]{1,0:T(8,128)(2,1)} %get-tuple-element.53), channel_id=1, source_target_pairs={{0,16},{16,0},{1,17},{17,1},{2,18},{18,2},{3,19},{19,3},{4,20},{20... | collective-permute-start | bytes 3538952 | tf_op jit(solution)/shard_map/ppermute | solution.py:167
  328.8 4.1 copy-start.8
  328.8 4.1 copy-start.50
  332.9 3.4 copy-start.6
  332.9 3.4 copy-start.49
  344.3 7.4 %collective-permute-start.3 = (bf16[512,1088]{0,1:T(8,128)(2,1)}, bf16[512,1088]{0,1:T(8,128)(2,1)}, u32[]{:S(2)}, u32[]{:S(2)}) collective-permute-start(bf16[512,1088]{0,1:T(8,128)(2,1)} %copy.123), channel_id=1, source_target_pairs={{2,1},{6,5},{10,9},{14,13},{18,17},{22,21},{26,25},{30,29}} | collective-permute-start | bytes 3342344 | tf_op jit(solution)/shard_map/ppermute | solution.py:171
  346.7 4.9 copy-start.37
  346.7 4.9 copy-start.40
  346.7 4.9 copy-start.25
  346.7 4.9 copy-start.28
  346.7 4.9 copy-start.31
  346.7 4.9 copy-start.34
  354.0 10.2 %slice-start.9 = ((s8[4456448]{0:T(1024)(128)(4,1)}), s8[4194304]{0:T(1024)(128)(4,1)S(1)}, s32[]{:S(2)}) async-start(s8[4456448]{0:T(1024)(128)(4,1)} %bitcast.235), calls=%async_computation.12 | async-start | bytes 8388608
  354.3 7.4 %copy-start.26 = (s32[1088]{0:T(1024)S(1)}, s32[1088]{0:T(1024)}, u32[]{:S(2)}) copy-start(s32[1088]{0:T(1024)} %copy-done.25) | copy-start | bytes 13060
  354.3 7.3 %copy-start.29 = (s32[1088]{0:T(1024)S(1)}, s32[1088]{0:T(1024)}, u32[]{:S(2)}) copy-start(s32[1088]{0:T(1024)} %copy-done.28) | copy-start | bytes 13060
  354.3 7.3 %copy-start.32 = (s32[1088]{0:T(1024)S(1)}, s32[1088]{0:T(1024)}, u32[]{:S(2)}) copy-start(s32[1088]{0:T(1024)} %copy-done.31) | copy-start | bytes 13060
  354.3 7.3 %copy-start.35 = (s32[1088]{0:T(1024)S(1)}, s32[1088]{0:T(1024)}, u32[]{:S(2)}) copy-start(s32[1088]{0:T(1024)} %copy-done.34) | copy-start | bytes 13060
  354.3 7.3 %copy-start.38 = (pred[1088]{0:T(1024)(128)(4,1)S(1)}, pred[1088]{0:T(1024)(128)(4,1)}, u32[]{:S(2)}) copy-start(pred[1088]{0:T(1024)(128)(4,1)} %copy-done.37) | copy-start | bytes 3268
  354.3 7.3 %copy-start.41 = (pred[1088]{0:T(1024)(128)(4,1)S(1)}, pred[1088]{0:T(1024)(128)(4,1)}, u32[]{:S(2)}) copy-start(pred[1088]{0:T(1024)(128)(4,1)} %copy-done.40) | copy-start | bytes 3268
  354.3 9.9 %slice-start.10 = ((s8[4456448]{0:T(1024)(128)(4,1)}), s8[262144]{0:T(1024)(128)(4,1)S(1)}, s32[]{:S(2)}) async-start(s8[4456448]{0:T(1024)(128)(4,1)} %bitcast.235), calls=%async_computation.13 | async-start | bytes 524288
  354.3 20.5 %slice-start.6 = ((s8[8912896]{0:T(1024)(128)(4,1)}), s8[4194304]{0:T(1024)(128)(4,1)S(1)}, s32[]{:S(2)}) async-start(s8[8912896]{0:T(1024)(128)(4,1)} %bitcast.233), calls=%async_computation.9 | async-start | bytes 8388608
  361.7 13.2 %slice-start.4 = ((s8[4734976]{0:T(1024)(128)(4,1)}), s8[4194304]{0:T(1024)(128)(4,1)S(1)}, s32[]{:S(2)}) async-start(s8[4734976]{0:T(1024)(128)(4,1)} %bitcast.199), calls=%async_computation.7 | async-start | bytes 8388608
  361.7 13.2 %slice-start.7 = ((s8[8912896]{0:T(1024)(128)(4,1)}), s8[4194304]{0:T(1024)(128)(4,1)S(1)}, s32[]{:S(2)}) async-start(s8[8912896]{0:T(1024)(128)(4,1)} %bitcast.233), calls=%async_computation.10 | async-start | bytes 8388608
  364.3 10.6 %slice-start.5 = ((s8[4734976]{0:T(1024)(128)(4,1)}), s8[540672]{0:T(1024)(128)(4,1)S(1)}, s32[]{:S(2)}) async-start(s8[4734976]{0:T(1024)(128)(4,1)} %bitcast.199), calls=%async_computation.8 | async-start | bytes 1081344
  364.3 10.6 %slice-start.8 = ((s8[8912896]{0:T(1024)(128)(4,1)}), s8[524288]{0:T(1024)(128)(4,1)S(1)}, s32[]{:S(2)}) async-start(s8[8912896]{0:T(1024)(128)(4,1)} %bitcast.233), calls=%async_computation.11 | async-start | bytes 1048576
  369.6 16.0 %slice-start.2 = ((s8[4734976]{0:T(1024)(128)(4,1)}), s8[4194304]{0:T(1024)(128)(4,1)S(1)}, s32[]{:S(2)}) async-start(s8[4734976]{0:T(1024)(128)(4,1)} %bitcast.195), calls=%async_computation.5 | async-start | bytes 8388608
  369.6 21.0 %slice-start = ((s8[4734976]{0:T(1024)(128)(4,1)}), s8[4194304]{0:T(1024)(128)(4,1)S(1)}, s32[]{:S(2)}) async-start(s8[4734976]{0:T(1024)(128)(4,1)} %bitcast.191), calls=%async_computation.3 | async-start | bytes 8388608
  374.9 10.6 %slice-start.3 = ((s8[4734976]{0:T(1024)(128)(4,1)}), s8[540672]{0:T(1024)(128)(4,1)S(1)}, s32[]{:S(2)}) async-start(s8[4734976]{0:T(1024)(128)(4,1)} %bitcast.195), calls=%async_computation.6 | async-start | bytes 1081344
  374.9 15.7 %slice-start.1 = ((s8[4734976]{0:T(1024)(128)(4,1)}), s8[540672]{0:T(1024)(128)(4,1)S(1)}, s32[]{:S(2)}) async-start(s8[4734976]{0:T(1024)(128)(4,1)} %bitcast.191), calls=%async_computation.4 | async-start | bytes 1081344
  385.6 5.1 copy-start.24
  385.6 5.1 copy-start.57
  397.3 8.2 %copy-start.53 = (bf16[512,1152]{1,0:T(8,128)(2,1)S(1)}, bf16[512,1152]{1,0:T(8,128)(2,1)}, u32[]{:S(2)}) copy-start(bf16[512,1152]{1,0:T(8,128)(2,1)} %convolution_convert_fusion.11) | copy-start | bytes 3538948
  397.3 8.2 %copy-start.56 = (bf16[512,2176]{1,0:T(8,128)(2,1)S(1)}, bf16[512,2176]{1,0:T(8,128)(2,1)}, u32[]{:S(2)}) copy-start(bf16[512,2176]{1,0:T(8,128)(2,1)} %get-tuple-element.125) | copy-start | bytes 6684676
  397.3 13.4 %collective-permute-start.4 = (bf16[512,1088]{0,1:T(8,128)(2,1)S(1)}, bf16[512,1088]{0,1:T(8,128)(2,1)S(1)}, u32[]{:S(2)}, u32[]{:S(2)}) collective-permute-start(bf16[512,1088]{0,1:T(8,128)(2,1)S(1)} %copy.127), channel_id=1, source_target_pairs={{1,0},{5,4},{9,8},{13,12},{17,16},{21,20},{25,24},{29,28}} | collective-permute-start | bytes 3342344 | tf_op jit(solution)/shard_map/ppermute | solution.py:171
  417.0 39.3 %copy-start.10 = (bf16[1,4,272,1152]{3,2,1,0:T(8,128)(2,1)S(1)}, bf16[1,4,272,1152]{3,2,1,0:T(8,128)(2,1)}, u32[]{:S(2)}) copy-start(bf16[1,4,272,1152]{3,2,1,0:T(8,128)(2,1)} %get-tuple-element.122) | copy-start | bytes 7520260
  456.2 15.1 %collective-permute-start.6 = (bf16[512,1152]{1,0:T(8,128)(2,1)}, bf16[512,1152]{1,0:T(8,128)(2,1)}, u32[]{:S(2)}, u32[]{:S(2)}) collective-permute-start(bf16[512,1152]{1,0:T(8,128)(2,1)} %get-tuple-element.58), channel_id=1, source_target_pairs={{0,16},{16,0},{1,17},{17,1},{2,18},{18,2},{3,19},{19,3},{4,20},{20... | collective-permute-start | bytes 3538952 | tf_op jit(solution)/shard_map/ppermute | solution.py:167
  456.4 5.3 copy-start.51
  456.4 5.3 copy-start.54
  461.1 2.3 copy-start.39
  461.1 2.3 copy-start.42
  461.1 16.0 %collective-permute-start.5 = (bf16[512,1152]{1,0:T(8,128)(2,1)}, bf16[512,1152]{1,0:T(8,128)(2,1)}, u32[]{:S(2)}, u32[]{:S(2)}) collective-permute-start(bf16[512,1152]{1,0:T(8,128)(2,1)} %get-tuple-element.56), channel_id=1, source_target_pairs={{0,16},{16,0},{1,17},{17,1},{2,18},{18,2},{3,19},{19,3},{4,20},{20... | collective-permute-start | bytes 3538952 | tf_op jit(solution)/shard_map/ppermute | solution.py:167
  471.3 5.8 copy-start.48
  471.3 5.8 copy-start.55
  618.9 2.9 copy-start.52
  621.7 3.4 copy-start.1
  621.7 3.4 copy-start.7
  621.7 3.4 copy-start.16
  621.7 3.8 copy-start.47
  625.6 4.0 copy-start.4
  625.6 4.0 copy-start.18
  632.2 19.7 %all-to-all-start = ((bf16[4,2,64,1088]{3,2,1,0:T(8,128)(2,1)}), bf16[4,2,64,1088]{3,2,1,0:T(8,128)(2,1)}, u32[]{:S(2)}, u32[]{:S(2)}) async-start(bf16[4,2,64,1088]{3,2,1,0:T(8,128)(2,1)} %bitcast.182), calls=%async_computation | async-start | bytes 2359296 | tf_op jit(solution)/shard_map/all_to_all | solution.py:769
  651.9 53.6 %all-to-all-start.1 = ((bf16[4,2,64,1088]{3,2,1,0:T(8,128)(2,1)}), bf16[4,2,64,1088]{3,2,1,0:T(8,128)(2,1)}, u32[]{:S(2)}, u32[]{:S(2)}) async-start(bf16[4,2,64,1088]{3,2,1,0:T(8,128)(2,1)} %all-to-all-done), calls=%async_computation.1 | async-start | bytes 2359296 | tf_op jit(solution)/shard_map/all_to_all | solution.py:770
  662.0 3.2 copy-start.46
  (14 other events, 23.5 us)

commit v4 on v3

--- a/solution.py
+++ b/solution.py
@@ -47,128 +47,11 @@
     return jnp.where(jnp.stack([own, other]), 0.0, NEG).astype(f32)
 
 
-def attention_forward_kernel(half, mask_ref, q_ref, k0_ref, k1_ref, v0_ref, v1_ref, o_ref, ob_ref, lse_ref):
-    pair = pl.program_id(0)
-    tokens = q_ref.shape[0]
-    block = 2 * half
-
-    @pl.when(pair == 0)
-    def _():
-        lse_ref[...] = jnp.zeros_like(lse_ref)
-
-    lane = lax.broadcasted_iota(jnp.int32, (block, LANES), 1)
-    for u in range(tokens // block):
-        rows = pl.ds(u * block, block)
-        keys = (u + 1) * block
-        outs = []
-        for h in range(2):
-            cols = pl.ds(h * HEAD, HEAD)
-            q = q_ref[rows, cols]
-            scores = []
-            for part, k_ref in enumerate((k0_ref, k1_ref)):
-                s = mm_t(q, k_ref[pl.ds(0, keys), cols])
-                last = s[:, keys - block :] + mask_ref[part]
-                scores.append(last if u == 0 else jnp.concatenate([s[:, : keys - block], last], axis=1))
-            top = jnp.maximum(
-                jnp.max(scores[0], axis=1, keepdims=True), jnp.max(scores[1], axis=1, keepdims=True)
-            )
-            total, acc = 0.0, 0.0
-            for s, v_ref in zip(scores, (v0_ref, v1_ref)):
-                p = jnp.exp(s - top)
-                total = total + jnp.sum(p, axis=1, keepdims=True)
-                acc = acc + mm(p.astype(bf16), v_ref[pl.ds(0, keys), cols])
-            outs.append(acc / total)
-            lse = top + jnp.log(total)
-            lse_ref[rows, :] = jnp.where(lane == 2 * pair + h, lse, lse_ref[rows, :])
-        out = jnp.concatenate(outs, axis=1)
-        o_ref[rows, :] = out
-        ob_ref[rows, :] = out.astype(bf16)
-
-
-def attention_forward(mask, q, k0, k1, v0, v1, half):
-    tokens, width = q.shape
-    spec = pl.BlockSpec((tokens, LANES), lambda i: (0, i))
-    return pl.pallas_call(
-        functools.partial(attention_forward_kernel, half),
-        grid=(width // LANES,),
-        in_specs=[pl.BlockSpec(mask.shape, lambda i: (0, 0, 0))] + [spec] * 5,
-        out_specs=[spec, spec, pl.BlockSpec((tokens, LANES), lambda i: (0, 0))],
-        out_shape=[
-            jax.ShapeDtypeStruct((tokens, width), f32),
-            jax.ShapeDtypeStruct((tokens, width), bf16),
-            jax.ShapeDtypeStruct((tokens, LANES), f32),
-        ],
-        name="attention_forward",
-    )(mask, q, k0, k1, v0, v1)
-
-
-def attention_backward_kernel(
-    half, mask_ref, q_ref, k0_ref, k1_ref, v0_ref, v1_ref, da_ref, o_ref, lse_ref,
-    dq_ref, dk0_ref, dk1_ref, dv0_ref, dv1_ref, acc_ref,
-):
-    pair = pl.program_id(0)
-    tokens = q_ref.shape[0]
-    block = 2 * half
-    lane = lax.broadcasted_iota(jnp.int32, (block, LANES), 1)
-    acc_ref[...] = jnp.zeros_like(acc_ref)
-    for u in range(tokens // block):
-        rows = pl.ds(u * block, block)
-        keys = (u + 1) * block
-        dqs = []
-        for h in range(2):
-            cols = pl.ds(h * HEAD, HEAD)
-            q, da = q_ref[rows, cols], da_ref[rows, cols]
-            q_t, da_t = q.T, da.T
-            lse = jnp.sum(jnp.where(lane == 2 * pair + h, lse_ref[rows, :], 0.0), axis=1, keepdims=True)
-            delta = jnp.sum(da.astype(f32) * o_ref[rows, cols], axis=1, keepdims=True)
-            dq = 0.0
-            for part, (k_ref, v_ref) in enumerate(((k0_ref, v0_ref), (k1_ref, v1_ref))):
-                k, v = k_ref[pl.ds(0, keys), cols], v_ref[pl.ds(0, keys), cols]
-                s = mm_t(q, k)
-                last = s[:, keys - block :] + mask_ref[part]
-                s = last if u == 0 else jnp.concatenate([s[:, : keys - block], last], axis=1)
-                p = jnp.exp(s - lse)
-                ds = (p * (mm_t(da, v) - delta)).astype(bf16)
-                dq = dq + mm(ds, k)
-                acc_ref[part, 0, h, :, pl.ds(0, keys)] += mm(q_t, ds)
-                acc_ref[part, 1, h, :, pl.ds(0, keys)] += mm(da_t, p.astype(bf16))
-            dqs.append(dq * score_scale)
-        dq_ref[rows, :] = jnp.concatenate(dqs, axis=1).astype(bf16)
-    for part, (dk_ref, dv_ref) in enumerate(((dk0_ref, dv0_ref), (dk1_ref, dv1_ref))):
-        for which, ref in enumerate((dk_ref, dv_ref)):
-            both = jnp.concatenate([acc_ref[part, which, 0], acc_ref[part, which, 1]], axis=0)
-            ref[...] = both.T.astype(ref.dtype)
-
-
-def attention_backward(mask, q, k0, k1, v0, v1, da, o, lse, half):
-    tokens, width = q.shape
-    spec = pl.BlockSpec((tokens, LANES), lambda i: (0, i))
-    whole = pl.BlockSpec((tokens, LANES), lambda i: (0, 0))
-    shape = lambda t: jax.ShapeDtypeStruct((tokens, width), t)
-    return pl.pallas_call(
-        functools.partial(attention_backward_kernel, half),
-        grid=(width // LANES,),
-        in_specs=[pl.BlockSpec(mask.shape, lambda i: (0, 0, 0))] + [spec] * 7 + [whole],
-        out_specs=[spec] * 5,
-        out_shape=[shape(bf16), shape(f32), shape(bf16), shape(f32), shape(bf16)],
-        scratch_shapes=[pltpu.VMEM((2, 2, 2, HEAD, tokens), f32)],
-        name="attention_backward",
-    )(mask, q, k0, k1, v0, v1, da, o, lse)
-
-
 def norm_backward(hat, scale, gain, grad):
     scaled = grad * gain
     mean = jnp.mean(scaled, axis=-1, keepdims=True)
     along = jnp.mean(scaled * hat, axis=-1, keepdims=True)
     return scale * (scaled - mean - hat * along)
-
-
-def swap_cores(value):
-    return lax.ppermute(value, "section", [(0, 1), (1, 0)])
-
-
-def hop(value, source, target):
-    return lax.ppermute(value, "shard", [(source, target)])
 
 
 ANY = pl.BlockSpec(memory_space=pl.ANY)
@@ -537,6 +420,234 @@
     )(attn_piece, ff_piece, x_own, g_own, norm_own, mask)
 
 
+def backward_kernel(
+    w_attn_ref, w_ff_ref, g_ref, norm_ref, mask_ref,
+    ent_ref, q_ref, k_ref, k1_ref, v_ref, v1_ref, o_ref, lse_ref, up_ref,
+    coming_out, leaving_out, dq_out, dk_out, dv_out, d_up_out, sums_out,
+    w, coming, leaving, ent, slots, o, lse, da, dq, dk, dv, give, take, big, sums,
+    load, hop_send, hop_recv, swap_send, swap_recv, save, keep,
+):
+    section, ctx, shard = lax.axis_index("section"), lax.axis_index("ctx"), lax.axis_index("shard")
+    kind = lax.rem(shard, 2)
+    width = ent.shape[1]
+    wide = dq.shape[1]
+    size = da.shape[0]
+    chunks = ent.shape[0] // size
+    ff_half = w_ff_ref.shape[3]
+    parts = ((0, wide), (wide, ff_half - wide))
+    order = range(chunks - 1, -1, -1)
+
+    def weight(c, start, columns):
+        value = w[c, :, :, pl.ds(start, columns)]
+        return value.reshape(value.shape[0] * value.shape[1], columns)
+
+    def hop_copy(u):
+        rows = pl.ds(u * size, size)
+        return remote(leaving.at[rows], coming.at[rows], hop_send.at[u], hop_recv.at[u], section, ctx, shard - 1)
+
+    def hop_wait(u):
+        rows = pl.ds(u * size, size)
+        remote(leaving.at[rows], coming.at[rows], hop_send.at[u], hop_recv.at[u], section, ctx, shard).wait_recv()
+
+    def saves(u, pairs):
+        rows = pl.ds(u * size, size)
+        return [
+            pltpu.make_async_copy(src.at[rows], dst.at[rows], save.at[index, u])
+            for index, (src, dst) in enumerate(pairs)
+        ]
+
+    def finish_chunk(rows, d_normed, gain):
+        hat, scale = normalised(ent[rows].astype(f32))
+        sums[0:1, :width] += jnp.sum(d_normed * hat, axis=0, keepdims=True)
+        sums[1:2, :width] += jnp.sum(d_normed, axis=0, keepdims=True)
+        total = coming[rows].astype(f32) + norm_backward(hat, scale, gain, d_normed)
+        leaving[rows] = total.astype(bf16)
+
+    sums[...] = jnp.zeros_like(sums)
+    ent_load = pltpu.make_async_copy(ent_ref, ent, load.at[0])
+    ent_load.start()
+
+    @pl.when(kind == 0)
+    def _():
+        loads = [pltpu.make_async_copy(w_attn_ref, w.at[:, :, :, pl.ds(0, wide)], load.at[1])]
+        for i, ref in enumerate((q_ref, k_ref, k1_ref, v_ref, v1_ref)):
+            loads.append(pltpu.make_async_copy(ref, slots.at[i], load.at[2 + i]))
+        loads.append(pltpu.make_async_copy(o_ref, o, load.at[7]))
+        loads.append(pltpu.make_async_copy(lse_ref, lse, load.at[8]))
+        for copy in loads:
+            copy.start()
+        for copy in loads:
+            copy.wait()
+        ent_load.wait()
+        gain = norm_ref[0:1, :width]
+        lane = lax.broadcasted_iota(jnp.int32, (size, LANES), 1)
+        low = lane < HEAD
+        da[...] = jnp.zeros_like(da)
+        pairs = ((coming, coming_out), (leaving, leaving_out), (dq, dq_out), (dk, dk_out), (dv, dv_out))
+
+        def swap_copy(which, u):
+            rows = pl.ds(u * size, size)
+            return remote(
+                give.at[which, rows], take.at[which, rows], swap_send.at[which, u], swap_recv.at[which, u],
+                1 - section, ctx, shard,
+            )
+
+        for u in order:
+            rows = pl.ds(u * size, size)
+            keys = pl.ds(0, (u + 1) * size)
+            hop_wait(u)
+            da[:, :width] = mm_t(coming[rows], weight(3, 0, width)).astype(bf16)
+
+            @pl.loop(0, wide // LANES)
+            def _(pair):
+                cols = pl.ds(pl.multiple_of(pair * LANES, LANES), LANES)
+                q2 = stack_heads(slots[0, rows, cols], low)
+                grad = da[:, cols]
+                a2 = stack_heads(grad, low)
+                level = lse[rows, :]
+                product = grad.astype(f32) * o[rows, cols]
+                column = lambda which: jnp.sum(jnp.where(lane == 2 * pair + which, level, 0.0), axis=1, keepdims=True)
+                level2 = jnp.concatenate([column(0), column(1)], axis=0)
+                delta2 = jnp.concatenate(
+                    [
+                        jnp.sum(jnp.where(low, product, 0.0), axis=1, keepdims=True),
+                        jnp.sum(jnp.where(low, 0.0, product), axis=1, keepdims=True),
+                    ],
+                    axis=0,
+                )
+                dq2 = 0.0
+                for part in range(2):
+                    keys_now, values_now = slots[1 + part, keys, cols], slots[3 + part, keys, cols]
+                    p = jnp.exp(mask_last(mm_t(q2, keys_now), mask_ref[part]) - level2)
+                    ds = (p * (mm_t(a2, values_now) - delta2)).astype(bf16)
+                    dq2 = dq2 + mm(ds, keys_now)
+                    d_keys, d_values = t_mm(ds, q2), t_mm(p.astype(bf16), a2)
+                    if u == chunks - 1:
+                        big[2 * part, keys, cols] = d_keys
+                        big[2 * part + 1, keys, cols] = d_values
+                    else:
+                        big[2 * part, keys, cols] += d_keys
+                        big[2 * part + 1, keys, cols] += d_values
+                dq[rows, cols] = (unstack_heads(dq2, low) * score_scale).astype(bf16)
+
+            for which in range(2):
+                give[which, rows] = big[2 + which, rows].astype(bf16)
+                swap_copy(which, u).start()
+            d_normed = mm_t(dq[rows], weight(0, 0, wide))
+            for which, ref in enumerate((dk, dv)):
+                swap_copy(which, u).wait_recv()
+                ref[rows] = (big[which, rows] + take[which, rows].astype(f32)).astype(bf16)
+                d_normed = d_normed + mm_t(ref[rows], weight(1 + which, 0, wide))
+            finish_chunk(rows, d_normed, gain)
+
+            @pl.when(shard > 0)
+            def _():
+                hop_copy(u).start()
+
+            for copy in saves(u, pairs):
+                copy.start()
+        for u in order:
+            for which in range(2):
+                swap_copy(which, u).wait_send()
+
+            @pl.when(shard > 0)
+            def _():
+                hop_copy(u).wait_send()
+
+            for copy in saves(u, pairs):
+                copy.wait()
+
+    @pl.when(kind == 1)
+    def _():
+        loads = [pltpu.make_async_copy(w_ff_ref, w, load.at[1])]
+        for i in range(2):
+            for part, (start, columns) in enumerate(parts):
+                loads.append(
+                    pltpu.make_async_copy(
+                        up_ref.at[i, :, pl.ds(start, columns)], big.at[2 * i + part, :, pl.ds(0, columns)], load.at[2 + 2 * i + part]
+                    )
+                )
+        g_load = pltpu.make_async_copy(g_ref, coming, load.at[6])
+
+        @pl.when(shard == 3)
+        def _():
+            g_load.start()
+
+        for copy in loads:
+            copy.start()
+        for copy in loads:
+            copy.wait()
+
+        @pl.when(shard == 3)
+        def _():
+            g_load.wait()
+
+        ent_load.wait()
+        gain = norm_ref[1:2, :width]
+        pairs = [(coming, coming_out), (leaving, leaving_out)]
+        for i in range(2):
+            for part, (start, columns) in enumerate(parts):
+                pairs.append((slots.at[2 * i + part, :, pl.ds(0, columns)], d_up_out.at[i, :, pl.ds(start, columns)]))
+
+        for u in order:
+            rows = pl.ds(u * size, size)
+
+            @pl.when(shard < 3)
+            def _():
+                hop_wait(u)
+
+            grad = coming[rows]
+            d_normed = 0.0
+            for i in range(2):
+                for part, (start, columns) in enumerate(parts):
+                    cols = pl.ds(0, columns)
+                    d_hidden = mm(grad, weight(2 + i, start, columns))
+                    _, back = jax.vjp(lambda value: jax.nn.gelu(value, approximate=True), big[2 * i + part, rows, cols])
+                    d_upper = back(d_hidden)[0].astype(bf16)
+                    slots[2 * i + part, rows, cols] = d_upper
+                    d_normed = d_normed + mm_t(d_upper, weight(i, start, columns))
+            finish_chunk(rows, d_normed, gain)
+            hop_copy(u).start()
+            for copy in saves(u, pairs):
+                copy.start()
+        for u in order:
+            hop_copy(u).wait_send()
+            for copy in saves(u, pairs):
+                copy.wait()
+
+    sums_save = pltpu.make_async_copy(sums, sums_out, keep.at[0])
+    sums_save.start()
+    sums_save.wait()
+
+
+def backward_relay(w_attn, w_ff, g, norms, mask, ent, q, k, k1, v, v1, o, lse, up):
+    tokens, width = ent.shape
+    wide = q.shape[1]
+    size = mask.shape[2]
+    chunks = tokens // size
+    dma = pltpu.SemaphoreType.DMA
+    vmem = pl.BlockSpec(memory_space=pltpu.VMEM)
+    narrow, broad = ((tokens, width), bf16), ((tokens, wide), bf16)
+    outs = [narrow, narrow, broad, broad, broad, (up.shape, bf16), (norms.shape, f32)]
+    scratch = [
+        ((4,) + w_ff.shape[1:], bf16), narrow, narrow, narrow, ((5, tokens, wide), bf16),
+        (o.shape, f32), (lse.shape, f32), ((size, wide), bf16), broad, broad, broad,
+        ((2, tokens, wide), bf16), ((2, tokens, wide), bf16), ((4, tokens, wide), f32), (norms.shape, f32),
+    ]
+    return pl.pallas_call(
+        backward_kernel,
+        in_specs=[ANY] * 3 + [vmem] * 2 + [ANY] * 9,
+        out_specs=[ANY] * len(outs),
+        out_shape=[jax.ShapeDtypeStruct(s, t) for s, t in outs],
+        scratch_shapes=[pltpu.VMEM(s, t) for s, t in scratch]
+        + [
+            dma((9,)), dma((chunks,)), dma((chunks,)), dma((2, chunks)), dma((2, chunks)), dma((6, chunks)), dma((1,)),
+        ],
+        compiler_params=pltpu.CompilerParams(has_side_effects=True, vmem_limit_bytes=62 * 2**20),
+        name="backward_relay",
+    )(w_attn, w_ff, g, norms, mask, ent, q, k, k1, v, v1, o, lse, up)
+
+
 def add_into(total, term):
     total[...] = (total[...].astype(f32) + term[...].astype(f32)).astype(bf16)
 
@@ -695,15 +806,13 @@
     x_own = lax.dynamic_slice_in_dim(inputs[0], section * half, half, 1)
     g_own = lax.dynamic_slice_in_dim(cotangent[0], section * half, half, 1)
     mask = attention_masks(section, half)
+    mask = jnp.concatenate([mask, mask], axis=1)
     w_attn, w_ff, g_all, norms, ent, nrm, q, k, k1, v, v1, o, lse, up, hid, y = forward_relay(
         lax.dynamic_index_in_dim(attn_src, ctx, 0, keepdims=False),
         lax.dynamic_index_in_dim(ff_src, ctx, 0, keepdims=False),
-        x_own, g_own, norm_own, jnp.concatenate([mask, mask], axis=1),
-    )
-    w_attn = w_attn.reshape(4, width, wide)
-    w_ff = w_ff.reshape(4, width, ff // 2)
+        x_own, g_own, norm_own, mask,
+    )
     own_place = jnp.arange(4)[:, None, None]
-    gain1, gain2 = norms[0, :width], norms[1, :width]
 
     def bring_tokens(every, own):
         mine = jnp.where((own_place[..., None] == ctx) & (shard == ctx), own, every)
@@ -715,57 +824,23 @@
     spread = (feature // group * group_pad + feature % group == place).astype(bf16)
     grouped = lambda v: mm(v, spread).astype(bf16)
 
-    def ff_backward(g, state):
-        hat, scale, normed, upper, hidden = state
-        d_upper = []
-        for i in range(2):
-            d_hidden = mm(g, w_ff[2 + i])
-            _, back = jax.vjp(lambda u: jax.nn.gelu(u, approximate=True), upper[i])
-            d_upper.append(back(d_hidden)[0].astype(bf16))
-        d_normed = mm_t(d_upper[0], w_ff[0]) + mm_t(d_upper[1], w_ff[1])
-        d_middle = g.astype(f32) + norm_backward(hat, scale, gain2, d_normed)
-        return d_middle.astype(bf16), d_upper, d_normed
-
-    def attn_backward(d_middle, state):
-        hat, scale, normed, q, k, k1, v, v1, o, ob, lse = state
-        d_att = mm_t(jnp.pad(d_middle, ((0, 0), (0, wide - width))), w_attn[3]).astype(bf16)
-        d_att = jnp.pad(d_att, ((0, 0), (0, wide - width)))
-        dq, dk, dk_other, dv, dv_other = attention_backward(mask, q, k, k1, v, v1, d_att, o, lse, half)
-        dk = (dk + swap_cores(dk_other).astype(f32)).astype(bf16)
-        dv = (dv + swap_cores(dv_other).astype(f32)).astype(bf16)
-        d_mixed = (dq, dk, dv)
-        d_normed = mm_t(dq, w_attn[0]) + mm_t(dk, w_attn[1]) + mm_t(dv, w_attn[2])
-        dx = d_middle.astype(f32) + norm_backward(hat, scale, gain1, d_normed)
-        return dx.astype(bf16), d_mixed, d_normed
-
-    hat, scale = normalised(ent.astype(f32))
-    attn_state = (hat, scale, nrm, q, k, k1, v, v1, o, o.astype(bf16), lse)
-    ff_state = (hat, scale, nrm, (up[0], up[1]), (hid[0], hid[1]))
-
-    d_middle, _, _ = ff_backward(g_last, ff_state)
-    d_middle1 = hop(d_middle, 3, 2)
-    dx, _, _ = attn_backward(d_middle1, attn_state)
-    g = jnp.where(shard == 3, g_last, hop(dx, 2, 1))
-    d_middle, d_upper, d_normed2 = ff_backward(g, ff_state)
-    hat2, _, normed2, _, hidden = ff_state
-    g_grouped, n2_grouped = grouped(g), grouped(normed2)
-    ff_grads = [t_mm(n2_grouped, d_upper[0]), t_mm(n2_grouped, d_upper[1]), t_mm(g_grouped, hidden[0]), t_mm(g_grouped, hidden[1])]
-    d_middle = jnp.where(shard == 2, d_middle1, hop(d_middle, 1, 0))
-    dx, d_mixed, d_normed1 = attn_backward(d_middle, attn_state)
-    hat1, _, normed, _, _, _, _, _, _, ob, _ = attn_state
-    n1_grouped, att_grouped = grouped(normed), grouped(ob[:, :width])
-    attn_grads = [t_mm(n1_grouped, d) for d in d_mixed] + [t_mm(att_grouped, jnp.pad(d_middle, ((0, 0), (0, wide - width))))]
+    coming, leaving, dq, dk, dv, d_up, sums = backward_relay(
+        w_attn, w_ff, g_last, norms, mask, ent, q, k, k1, v, v1, o, lse, up
+    )
+    nrm_grouped, coming_grouped = grouped(nrm), grouped(coming)
+    ff_grads = [t_mm(nrm_grouped, d_up[i]) for i in range(2)] + [t_mm(coming_grouped, hid[i]) for i in range(2)]
+    o_grouped = grouped(o[:, :width].astype(bf16))
+    attn_grads = [t_mm(nrm_grouped, d) for d in (dq, dk, dv)]
+    attn_grads.append(t_mm(o_grouped, jnp.pad(coming, ((0, 0), (0, wide - width)))))
     attn_sums, ff_sums = reduce_all([v.astype(bf16) for v in attn_grads], [v.astype(bf16) for v in ff_grads])
 
-    own_hat = jnp.where(is_attn, hat1, hat2)
-    own_grad = jnp.where(is_attn, d_normed1, d_normed2)
-    terms = jnp.stack([jnp.sum(own_grad * own_hat, axis=0), jnp.sum(own_grad, axis=0)])
+    terms = sums[:2, :width]
     terms = jnp.where(jnp.arange(4)[:, None, None] == shard, terms[None], 0.0)
     totals = lax.psum(terms, ("section", "ctx", "shard")).reshape(2, 2, 2, width)
     totals = lax.dynamic_index_in_dim(totals, section, 0, keepdims=False)
     totals = lax.dynamic_slice_in_dim(totals, (ctx * 4 + shard) * group, group, 2)
 
-    final = jnp.where(is_attn, dx, y).reshape(blocks, 4, half, width)
+    final = jnp.where(is_attn, leaving, y).reshape(blocks, 4, half, width)
     final = lax.all_to_all(jnp.swapaxes(final, 0, 1), "ctx", 0, 0)
     final = lax.all_to_all(final, "shard", 0, 0).reshape(2, 2, blocks, half, width)
     final = lax.all_to_all(final, "section", 0, 0)

time: 726 us -> 575 us (0.79)
  the two profiles are of different devices: /device:TPU:24 before, /device:TPU:0 now
where the time goes in v4:
time: 575 us; the launch traced here: 566 us
  Pallas kernels  422 us (73%)
  blocking collectives  49.9 us (9%)
  matrix products  43.9 us (8%)
  local copies, waits for them, and re-layouts  23.2 us (4%)
  other arithmetic  14 us (2%)
  starting transfers between devices  12.2 us (2%)
    pallas_call x1, Pallas kernels, backward_relay(): pl.pallas_call(backward_kernel, in_specs=[ANY] * 3 + [vmem] * 2 + [ANY] *...  177 us
    pallas_call x1, Pallas kernels, forward_relay(): pl.pallas_call(forward_kernel, in_specs=[ANY] * 5 + [vmem], out_specs=[AN...  146 us
    pallas_call x1, Pallas kernels, reduce_all(): pl.pallas_call(reduce_kernel, in_specs=[ANY] * (2 * count), out_specs=[AN...  98.5 us
    psum x1, blocking collectives, chain(): lax.psum(terms, ('section', 'ctx', 'shard')).reshape(2, 2, 2, width)  45.2 us
    dot_general x10, matrix products, dot(): return lax.dot_general(a, b, (dims, ((), ())), preferred_element_type=f32)  43.9 us
  transfers between devices with their start and end apart: 2, of which 0 were waited for; matrix products, arithmetic and copies ran while one was open for 10% of the time, Pallas kernels for 17%

profile of v4, /device:TPU:0, one launch (start us, length us, event | category | flops | bytes accessed | tf_op | source)
XLA Modules:
  0.0 566.0 jit_solution(14596291955581106827)
XLA Ops:
  0.7 0.0 copy-start.7
  0.7 0.0 copy-start.8
  0.7 1.6 fusion.32
  2.4 0.4 constant_dynamic-slice_fusion.1
  2.7 1.0 copy.34
  3.7 1.0 copy.33
  4.7 0.1 fusion.19
  4.8 0.0 copy-start.6
  4.8 0.0 copy-start.9
  4.8 0.7 pad_maximum_fusion.mask_ref
  5.6 0.5 compare_and_fusion
  6.1 1.2 pad_bitcast_fusion.1
  7.3 0.0 copy-done.9
  7.3 2.4 fusion.17
  9.7 1.4 slice_bitcast_fusion
  11.1 1.3 fusion.29
  12.4 0.6 broadcast_in_dim.54
  13.0 1.4 dynamic_update_slice.3.norm_ref
  14.4 2.5 fusion.16.attn_ref
  16.9 2.0 fusion.11.ff_ref
  18.8 146.0 %forward_relay.1 = (bf16[4,4,272,1152]{3,2,1,0:T(8,128)(2,1)}, bf16[4,4,272,2176]{3,2,1,0:T(8,128)(2,1)}, bf16[4,2,64,1088]{3,2,1,0:T(8,128)(2,1)}, f32[8,1152]{...) custom-call(bf16[272,1152]{1,0:T(8,128)(2,1)} %fusion.16.attn_ref, ...), custom_call_target="tpu_custom_call" | custom-call | tf_op jit(solution)/shard_map/forward_relay/pallas_call | solution.py:402
  164.9 1.5 select_bitcast_fusion
  166.4 1.1 copy.35
  167.5 177.1 %backward_relay.1 = (bf16[512,1088]{1,0:T(8,128)(2,1)}, bf16[512,1088]{1,0:T(8,128)(2,1)}, bf16[512,1152]{1,0:T(8,128)(2,1)}, bf16[512,1152]{1,0:T(8,128)(2,1)},...) custom-call(bf16[4,4,272,1152]{3,2,1,0:T(8,128)(2,1)} %get-tuple-element.33.w_attn_ref, ...), custom_call_target="tpu_custom_call" | custom-call | tf_op jit(solution)/shard_map/backward_relay/pallas_call | solution.py:637
  344.6 1.4 broadcast_select_fusion
  346.0 1.1 copy.46
  347.2 4.4 all-to-all-start
  351.6 0.0 slice-start.1
  351.6 2.6 convolution_convert_fusion.8
  354.2 0.0 slice-start.2
  354.2 5.2 convolution_convert_fusion
  359.5 5.2 convolution_convert_fusion.1
  364.7 2.6 convolution_convert_fusion.10
  367.3 0.0 copy-start.16
  367.3 5.4 convolution_convert_fusion.2
  372.7 5.3 convolution_convert_fusion.3
  378.0 7.1 %convolution_convert_fusion.4 = bf16[1152,1152]{1,0:T(8,128)(2,1)} fusion(bf16[512,1088]{1,0:T(8,128)(2,1)} %get-tuple-element.52, f32[512,1152]{1,0:T(8,128)S(1)} %copy-done.4, s32[1088]{0:T(1024)S(1)} %get-tuple-element.113, s32[1088]{0:T(1024)S(1)} %get-tuple-element.114, s32[1088]{0:T(1024)S(1)} %get-tuple-element.112, s32[1088]{0:T(1024)S(1)} %get-tuple-element.115, ...), kind=kOutput, calls=%fused_computation.4 | convolution fusion | flops 2650595328 | bytes 4984832 | tf_op jit(solution)/shard_map/dot_general | solution.py:26
  385.2 5.0 convolution_convert_fusion.5
  390.2 3.2 convolution_convert_fusion.6
  393.5 2.2 convolution_convert_fusion.7
  395.6 98.5 %reduce_all.1 = (bf16[4,72,1152]{2,1,0:T(8,128)(2,1)S(1)}, bf16[4,72,2176]{2,1,0:T(8,128)(2,1)S(1)}) custom-call(bf16[4,2,2,72,1152]{4,3,2,1,0:T(8,128)(2,1)S(1)} %bitcast.101, bf16[4,2,2,72,1152]{4,3,2,1,0:T(8,128)(2,1)} %bitcast.115, bf16[4,2,2,72,1152]{4,3,2,1,0:T(8,128)(2,1)} %bitcast.114, bf16[4,2,2,72,1152]{4,3,2,1,0:T(8,128)(2,1)} %bitcast.113, ...), custom_call_target="tpu_custom_call" | custom-call | tf_op jit(solution)/shard_map/reduce_all/pallas_call | solution.py:761
  494.1 0.2 slice_convert_fusion.1
  494.3 1.0 slice_bitcast_fusion.5
  495.3 0.1 maximum_bitcast_fusion.1
  495.4 2.2 copy.44
  497.6 1.2 maximum_bitcast_fusion
  498.8 2.2 copy.43
  501.0 0.0 all-to-all-done
  501.0 7.8 %all-to-all-start.1 = ((bf16[4,2,64,1088]{3,2,1,0:T(8,128)(2,1)}), bf16[4,2,64,1088]{3,2,1,0:T(8,128)(2,1)S(1)}, u32[]{:S(2)}, u32[]{:S(2)}) async-start(bf16[4,2,64,1088]{3,2,1,0:T(8,128)(2,1)} %all-to-all-done), calls=%async_computation.1 | async-start | bytes 2359296 | tf_op jit(solution)/shard_map/all_to_all | solution.py:845
  508.8 0.1 slice_convert_fusion.5
  508.9 0.1 fusion.33
  509.0 0.2 concatenate.17
  509.2 1.9 copy.41
  511.1 1.0 copy.42
  512.1 0.8 slice.109
  512.9 0.1 broadcast_select_fusion.1
  513.0 45.2 %psum.7 = f32[2,2,2,1088]{3,2,1,0:T(2,128)S(1)} all-reduce(f32[2,2,2,1088]{3,2,1,0:T(2,128)S(1)} %bitcast.124), channel_id=1, replica_groups=mesh['section'=2,'ctx'=4,'shard'=4] {'section','ctx','shard'}, use_global_device_ids=true, to_apply=%region_0.1 | all-reduce | flops 8704 | bytes 69632 | tf_op jit(solution)/shard_map/psum | solution.py:839
  558.2 0.1 fusion.30
  558.3 0.6 fusion.35
  558.9 0.0 all-to-all-done.1
  558.9 4.7 all_to_all.15
  563.5 0.1 fusion.34
  563.7 1.1 copy.39
  564.8 1.1 copy.40
  (47 shorter events, 0.2 us)
Async XLA Ops:
  0.7 1.7 copy-start.7
  0.7 1.7 copy-start.8
  4.8 2.4 copy-start.6
  4.8 2.4 copy-start.9
  6.1 3.6 copy-start.3
  7.3 2.4 copy-start.2
  9.7 1.4 copy-start.10
  14.4 2.5 copy-start
  18.8 146.1 %copy-start.1 = (bf16[1,2,64,1088]{3,2,1,0:T(8,128)(2,1)S(1)}, bf16[1,2,64,1088]{3,2,1,0:T(8,128)(2,1)}, u32[]{:S(2)}) copy-start(bf16[1,2,64,1088]{3,2,1,0:T(8,128)(2,1)} %copy.34) | copy-start | bytes 835588
  18.8 146.1 %copy-start.11 = (pred[4]{0:T(512)(128)(4,1)S(1)}, pred[4]{0:T(512)(128)(4,1)}, u32[]{:S(2)}) copy-start(pred[4]{0:T(512)(128)(4,1)} %compare_and_fusion) | copy-start | bytes 16
  167.5 177.1 %copy-start.5 = (bf16[512,1088]{1,0:T(8,128)(2,1)S(1)}, bf16[512,1088]{1,0:T(8,128)(2,1)}, u32[]{:S(2)}) copy-start(bf16[512,1088]{1,0:T(8,128)(2,1)} %get-tuple-element.47) | copy-start | bytes 3342340
  347.2 4.4 copy-start.15
  347.2 7.0 %slice-start = ((s8[4456448]{0:T(1024)(128)(4,1)}), s8[262144]{0:T(1024)(128)(4,1)S(1)}, s32[]{:S(2)}) async-start(s8[4456448]{0:T(1024)(128)(4,1)} %bitcast.129), calls=%async_computation.3 | async-start | bytes 524288
  347.2 153.8 %all-to-all-start = ((bf16[4,2,64,1088]{3,2,1,0:T(8,128)(2,1)}), bf16[4,2,64,1088]{3,2,1,0:T(8,128)(2,1)}, u32[]{:S(2)}, u32[]{:S(2)}) async-start(bf16[4,2,64,1088]{3,2,1,0:T(8,128)(2,1)} %bitcast.100), calls=%async_computation | async-start | bytes 2359296 | tf_op jit(solution)/shard_map/all_to_all | solution.py:844
  351.6 2.6 slice-start.1
  354.2 13.1 %slice-start.2 = ((s8[4456448]{0:T(1024)(128)(4,1)}), s8[4194304]{0:T(1024)(128)(4,1)S(1)}, s32[]{:S(2)}) async-start(s8[4456448]{0:T(1024)(128)(4,1)} %bitcast.131), calls=%async_computation.5 | async-start | bytes 8388608
  359.5 5.2 copy-start.12
  359.5 7.8 %slice-start.3 = ((s8[4456448]{0:T(1024)(128)(4,1)}), s8[262144]{0:T(1024)(128)(4,1)S(1)}, s32[]{:S(2)}) async-start(s8[4456448]{0:T(1024)(128)(4,1)} %bitcast.131), calls=%async_computation.6 | async-start | bytes 524288
  367.3 5.5 copy-start.16
  372.7 5.3 copy-start.4
  385.1 5.1 copy-start.14
  385.1 5.1 copy-start.17
  390.2 3.2 copy-start.13
  501.0 57.9 %all-to-all-start.1 = ((bf16[4,2,64,1088]{3,2,1,0:T(8,128)(2,1)}), bf16[4,2,64,1088]{3,2,1,0:T(8,128)(2,1)S(1)}, u32[]{:S(2)}, u32[]{:S(2)}) async-start(bf16[4,2,64,1088]{3,2,1,0:T(8,128)(2,1)} %all-to-all-done), calls=%async_computation.1 | async-start | bytes 2359296 | tf_op jit(solution)/shard_map/all_to_all | solution.py:845

commit v5 on v4

--- a/solution.py
+++ b/solution.py
@@ -420,17 +420,25 @@
     )(attn_piece, ff_piece, x_own, g_own, norm_own, mask)
 
 
+def add_into(total, term):
+    total[...] = (total[...].astype(f32) + term[...].astype(f32)).astype(bf16)
+
+
 def backward_kernel(
-    w_attn_ref, w_ff_ref, g_ref, norm_ref, mask_ref,
-    ent_ref, q_ref, k_ref, k1_ref, v_ref, v1_ref, o_ref, lse_ref, up_ref,
-    coming_out, leaving_out, dq_out, dk_out, dv_out, d_up_out, sums_out,
-    w, coming, leaving, ent, slots, o, lse, da, dq, dk, dv, give, take, big, sums,
-    load, hop_send, hop_recv, swap_send, swap_recv, save, keep,
+    w_attn_ref, w_ff_ref, g_ref, norm_ref, mask_ref, place_ref,
+    ent_ref, nrm_ref, q_ref, k_ref, k1_ref, v_ref, v1_ref, o_ref, lse_ref, up_ref, hid_ref, y_ref,
+    attn_out, ff_out, rows_out, sums_out,
+    w, coming, leaving, ent, slots, o, lse, da, take, big, sums, sums_in, spread, first, second, third,
+    load, hop_send, hop_recv, swap_send, swap_recv, rows_send, rows_recv, free,
+    sums_send, sums_recv, first_send, first_recv, second_send, second_recv, third_send, third_recv, last_send, last_recv,
 ):
     section, ctx, shard = lax.axis_index("section"), lax.axis_index("ctx"), lax.axis_index("shard")
     kind = lax.rem(shard, 2)
     width = ent.shape[1]
-    wide = dq.shape[1]
+    wide = da.shape[1]
+    half = da.shape[0] // 2
+    x_ctx, y_ctx = near_ctx(ctx, 1), near_ctx(ctx, 2)
+    d_ctx = near_ctx(x_ctx, 2)
     size = da.shape[0]
     chunks = ent.shape[0] // size
     ff_half = w_ff_ref.shape[3]
@@ -449,12 +457,33 @@
         rows = pl.ds(u * size, size)
         remote(leaving.at[rows], coming.at[rows], hop_send.at[u], hop_recv.at[u], section, ctx, shard).wait_recv()
 
-    def saves(u, pairs):
-        rows = pl.ds(u * size, size)
-        return [
-            pltpu.make_async_copy(src.at[rows], dst.at[rows], save.at[index, u])
-            for index, (src, dst) in enumerate(pairs)
-        ]
+    def rows_copy(src, t, local):
+        block, c = t // 4, t % 4
+        src = src.at[pl.ds(t * half, half)]
+        dst = rows_out.at[kind, block, pl.ds(pl.multiple_of(section * half, half), half)]
+        recv = rows_recv.at[kind, section, block]
+        if local:
+            return pltpu.make_async_copy(src, dst, recv)
+        return remote(src, dst, rows_send.at[t], recv, shard // 2, c, ctx)
+
+    def rows_stay(t):
+        return (section == shard // 2) & (ctx == t % 4) & (ctx == shard)
+
+    def rows_start(src, t):
+        @pl.when(rows_stay(t))
+        def _():
+            rows_copy(src, t, True).start()
+
+        @pl.when(jnp.logical_not(rows_stay(t)))
+        def _():
+            rows_copy(src, t, False).start()
+
+    def rows_finish(src):
+        for t in range(2 * chunks):
+
+            @pl.when(jnp.logical_not(rows_stay(t)))
+            def _():
+                rows_copy(src, t, False).wait_send()
 
     def finish_chunk(rows, d_normed, gain):
         hat, scale = normalised(ent[rows].astype(f32))
@@ -466,6 +495,151 @@
     sums[...] = jnp.zeros_like(sums)
     ent_load = pltpu.make_async_copy(ent_ref, ent, load.at[0])
     ent_load.start()
+
+    nrm_load = pltpu.make_async_copy(nrm_ref, ent, load.at[9])
+
+    def group_columns(index, value):
+        columns = spread.shape[3]
+        feature = lax.broadcasted_iota(jnp.int32, (width, LANES), 0)
+        for side in range(2):
+            for start in range(0, columns, LANES):
+                chosen = feature == place_ref[side, 0:1, start : start + LANES]
+                value_now = mm(value, jnp.where(chosen, 1.0, 0.0).astype(bf16))
+                spread[index, side, :, start : start + LANES] = value_now.astype(bf16)
+
+    def reduce(arrays, columns_all, out_ref, which, later_loads):
+        rows = first.shape[3]
+        cols_all = pl.ds(0, columns_all)
+        count = len(arrays)
+        gap = up_to(rows, 16)
+        own = lambda i, c, j: w.at[i, c, pl.ds(gap * j, rows), cols_all]
+
+        def terms(i, side):
+            _, index, pieces = arrays[i]
+            grouped = spread.at[index, side, :, pl.ds(0, 8 * rows)]
+
+            def store(value, cols):
+                for n in range(8):
+                    part = value[n * rows : (n + 1) * rows].astype(bf16)
+                    if side == 0:
+                        w[2 * (i % 2) + n % 2, n // 2, pl.ds(2 * gap, rows), cols] = part
+                    else:
+                        w[i, n // 2, pl.ds(gap * (n % 2), rows), cols] = part
+
+            for ref, columns, start in pieces:
+                step = 2 * LANES
+
+                @pl.loop(0, columns // step)
+                def _(b):
+                    at = pl.multiple_of(b * step, step)
+                    store(t_mm(grouped[...], ref[:, pl.ds(at, step)]), pl.ds(pl.multiple_of(start + at, LANES), step))
+
+                rest = columns % step
+                if rest:
+                    at = columns - rest
+                    store(t_mm(grouped[...], ref[:, pl.ds(at, rest)]), pl.ds(start + at, rest))
+
+        def first_copy(i, j):
+            return remote(
+                w.at[2 * (i % 2) + j, :, pl.ds(2 * gap, rows), cols_all], first.at[i % 2, j, :, :, cols_all],
+                first_send.at[i, j], first_recv.at[i, j], 1 - section, ctx, shard,
+            )
+
+        def second_copy(i, j, part):
+            to = (x_ctx, y_ctx)[j]
+            return remote(
+                own(i, (to, d_ctx)[part], j), second.at[i, j, part, :, cols_all],
+                second_send.at[i, j, part], second_recv.at[i, j, part], section, to, shard,
+            )
+
+        def third_copy(i, j):
+            to = (y_ctx, x_ctx)[j]
+            return remote(
+                own(i, to, j), third.at[i, j, :, cols_all], third_send.at[i, j], third_recv.at[i, j], section, to, shard
+            )
+
+        def last_copy(i, j):
+            return remote(
+                own(i, ctx, j), out_ref.at[arrays[i][0]], last_send.at[i, j], last_recv.at[which, arrays[i][0]],
+                shard // 2, ctx, 2 * (1 - section) + j,
+            )
+
+        def sums_copy(step):
+            to_core, to_ctx = ((1 - section, ctx), (section, x_ctx), (section, y_ctx))[step]
+            return remote(sums, sums_in.at[step], sums_send.at[step], sums_recv.at[step], to_core, to_ctx, shard)
+
+        def sums_last(j):
+            return remote(
+                sums, sums_out.at[which], sums_send.at[3 + j], sums_recv.at[3 + which],
+                shard // 2, ctx, 2 * (1 - section) + j,
+            )
+
+        sums_copy(0).start()
+        for step in range(count + 2):
+            i = step
+            if i < count:
+                if i >= 2:
+                    for j in range(2):
+                        first_copy(i - 2, j).wait_send()
+                if later_loads is not None and i == count - 1:
+                    for copy in later_loads:
+                        copy.wait()
+                terms(i, 0)
+                if i >= 2:
+                    pl.semaphore_wait(free, 1)
+                for j in range(2):
+                    first_copy(i, j).start()
+                terms(i, 1)
+                if later_loads is not None and i == 0:
+                    for copy in later_loads:
+                        copy.start()
+                for j in range(2):
+                    first_copy(i, j).wait_recv()
+
+                    @pl.loop(0, 4)
+                    def _(c):
+                        add_into(own(i, c, j), first.at[i % 2, j, c, :, cols_all])
+
+                if i + 2 < count:
+                    pl.semaphore_signal(
+                        free, inc=1, device_id=(1 - section, ctx, shard), device_id_type=pl.DeviceIdType.MESH
+                    )
+                for part in (1, 0):
+                    for j in range(2):
+                        second_copy(i, j, part).start()
+            i = step - 1
+            if 0 <= i < count:
+                for j in range(2):
+                    second_copy(i, j, 1).wait_recv()
+                    add_into(own(i, (y_ctx, x_ctx)[j], j), second.at[i, j, 1, :, cols_all])
+                    third_copy(i, j).start()
+                for j in range(2):
+                    second_copy(i, j, 0).wait_recv()
+                    add_into(own(i, ctx, j), second.at[i, j, 0, :, cols_all])
+            i = step - 2
+            if 0 <= i < count:
+                for j in range(2):
+                    third_copy(i, j).wait_recv()
+                    add_into(own(i, ctx, j), third.at[i, j, :, cols_all])
+                    last_copy(i, j).start()
+            if step < 3:
+                sums_copy(step).wait()
+                sums[...] += sums_in[step]
+                if step < 2:
+                    sums_copy(step + 1).start()
+                else:
+                    for j in range(2):
+                        sums_last(j).start()
+        for i in range(count):
+            for j in range(2):
+                if i >= count - 2:
+                    first_copy(i, j).wait_send()
+                for part in range(2):
+                    second_copy(i, j, part).wait_send()
+                third_copy(i, j).wait_send()
+                last_copy(i, j).wait_send()
+        for j in range(2):
+            sums_last(j).wait_send()
 
     @pl.when(kind == 0)
     def _():
@@ -483,12 +657,11 @@
         lane = lax.broadcasted_iota(jnp.int32, (size, LANES), 1)
         low = lane < HEAD
         da[...] = jnp.zeros_like(da)
-        pairs = ((coming, coming_out), (leaving, leaving_out), (dq, dq_out), (dk, dk_out), (dv, dv_out))
 
         def swap_copy(which, u):
             rows = pl.ds(u * size, size)
             return remote(
-                give.at[which, rows], take.at[which, rows], swap_send.at[which, u], swap_recv.at[which, u],
+                slots.at[2 + 2 * which, rows], take.at[which, rows], swap_send.at[which, u], swap_recv.at[which, u],
                 1 - section, ctx, shard,
             )
 
@@ -528,34 +701,41 @@
                     else:
                         big[2 * part, keys, cols] += d_keys
                         big[2 * part + 1, keys, cols] += d_values
-                dq[rows, cols] = (unstack_heads(dq2, low) * score_scale).astype(bf16)
+                slots[0, rows, cols] = (unstack_heads(dq2, low) * score_scale).astype(bf16)
 
             for which in range(2):
-                give[which, rows] = big[2 + which, rows].astype(bf16)
+                slots[2 + 2 * which, rows] = big[2 + which, rows].astype(bf16)
                 swap_copy(which, u).start()
-            d_normed = mm_t(dq[rows], weight(0, 0, wide))
-            for which, ref in enumerate((dk, dv)):
+            d_normed = mm_t(slots[0, rows], weight(0, 0, wide))
+            for which, index in enumerate((1, 3)):
                 swap_copy(which, u).wait_recv()
-                ref[rows] = (big[which, rows] + take[which, rows].astype(f32)).astype(bf16)
-                d_normed = d_normed + mm_t(ref[rows], weight(1 + which, 0, wide))
+                slots[index, rows] = (big[which, rows] + take[which, rows].astype(f32)).astype(bf16)
+                d_normed = d_normed + mm_t(slots[index, rows], weight(1 + which, 0, wide))
             finish_chunk(rows, d_normed, gain)
 
             @pl.when(shard > 0)
             def _():
                 hop_copy(u).start()
 
-            for copy in saves(u, pairs):
-                copy.start()
+            for t in (2 * u, 2 * u + 1):
+                rows_start(leaving, t)
         for u in order:
             for which in range(2):
                 swap_copy(which, u).wait_send()
+        nrm_load.start()
+        group_columns(1, o[:, :width].astype(bf16))
+        nrm_load.wait()
+        group_columns(0, ent[...])
+        whole = lambda index: ((slots.at[index], wide, 0),)
+        reduce(
+            ((3, 1, ((coming, width, 0),)), (0, 0, whole(0)), (1, 0, whole(1)), (2, 0, whole(3))), wide, attn_out, 0, None
+        )
+        rows_finish(leaving)
+        for u in order:
 
             @pl.when(shard > 0)
             def _():
                 hop_copy(u).wait_send()
-
-            for copy in saves(u, pairs):
-                copy.wait()
 
     @pl.when(kind == 1)
     def _():
@@ -569,11 +749,22 @@
                 )
         g_load = pltpu.make_async_copy(g_ref, coming, load.at[6])
 
+        def hidden_loads(i):
+            return [
+                pltpu.make_async_copy(
+                    hid_ref.at[i, :, pl.ds(start, columns)], take.at[part, :, pl.ds(0, columns)], load.at[7 + part]
+                )
+                for part, (start, columns) in enumerate(parts)
+            ]
+
+        for t in range(2 * chunks):
+            rows_start(y_ref, t)
+
         @pl.when(shard == 3)
         def _():
             g_load.start()
 
-        for copy in loads:
+        for copy in loads + hidden_loads(0):
             copy.start()
         for copy in loads:
             copy.wait()
@@ -584,11 +775,6 @@
 
         ent_load.wait()
         gain = norm_ref[1:2, :width]
-        pairs = [(coming, coming_out), (leaving, leaving_out)]
-        for i in range(2):
-            for part, (start, columns) in enumerate(parts):
-                pairs.append((slots.at[2 * i + part, :, pl.ds(0, columns)], d_up_out.at[i, :, pl.ds(start, columns)]))
-
         for u in order:
             rows = pl.ds(u * size, size)
 
@@ -608,177 +794,65 @@
                     d_normed = d_normed + mm_t(d_upper, weight(i, start, columns))
             finish_chunk(rows, d_normed, gain)
             hop_copy(u).start()
-            for copy in saves(u, pairs):
-                copy.start()
+        nrm_load.start()
+        group_columns(1, coming[...])
+        nrm_load.wait()
+        group_columns(0, ent[...])
+        for copy in hidden_loads(0):
+            copy.wait()
+        upper = lambda i: tuple((slots.at[2 * i + p], columns, start) for p, (start, columns) in enumerate(parts))
+        hidden = tuple((take.at[p], columns, start) for p, (start, columns) in enumerate(parts))
+        reduce(((2, 1, hidden), (0, 0, upper(0)), (1, 0, upper(1)), (3, 1, hidden)), ff_half, ff_out, 1, hidden_loads(1))
+        rows_finish(y_ref)
         for u in order:
             hop_copy(u).wait_send()
-            for copy in saves(u, pairs):
-                copy.wait()
-
-    sums_save = pltpu.make_async_copy(sums, sums_out, keep.at[0])
-    sums_save.start()
-    sums_save.wait()
-
-
-def backward_relay(w_attn, w_ff, g, norms, mask, ent, q, k, k1, v, v1, o, lse, up):
+
+    for index in range(attn_out.shape[0]):
+        for which, ref in enumerate((attn_out, ff_out)):
+            remote(
+                ref.at[index], ref.at[index], last_send.at[index, 0], last_recv.at[which, index], section, ctx, shard
+            ).wait_recv()
+    for which in range(2):
+        remote(sums, sums_out.at[which], sums_send.at[3], sums_recv.at[3 + which], section, ctx, shard).wait_recv()
+        for core in range(2):
+            for block in range(2):
+                ref = rows_out.at[which, block, pl.ds(core * half, half)]
+                pltpu.make_async_copy(ref, ref, rows_recv.at[which, core, block]).wait()
+
+
+def backward_relay(w_attn, w_ff, g, norms, mask, place, ent, nrm, q, k, k1, v, v1, o, lse, up, hid, y, group_pad):
     tokens, width = ent.shape
     wide = q.shape[1]
     size = mask.shape[2]
     chunks = tokens // size
+    ff_half = up.shape[2]
     dma = pltpu.SemaphoreType.DMA
     vmem = pl.BlockSpec(memory_space=pltpu.VMEM)
-    narrow, broad = ((tokens, width), bf16), ((tokens, wide), bf16)
-    outs = [narrow, narrow, broad, broad, broad, (up.shape, bf16), (norms.shape, f32)]
+    narrow = ((tokens, width), bf16)
+    outs = [
+        ((4, group_pad, wide), bf16), ((4, group_pad, ff_half), bf16), ((2, 2, size, width), bf16), ((2,) + norms.shape, f32),
+    ]
     scratch = [
         ((4,) + w_ff.shape[1:], bf16), narrow, narrow, narrow, ((5, tokens, wide), bf16),
-        (o.shape, f32), (lse.shape, f32), ((size, wide), bf16), broad, broad, broad,
-        ((2, tokens, wide), bf16), ((2, tokens, wide), bf16), ((4, tokens, wide), f32), (norms.shape, f32),
+        (o.shape, f32), (lse.shape, f32), ((size, wide), bf16), ((2, tokens, wide), bf16), ((4, tokens, wide), f32),
+        (norms.shape, f32), ((3,) + norms.shape, f32), ((2, 2, tokens, place.shape[2]), bf16),
+        ((2, 2, 4, group_pad, ff_half), bf16), ((4, 2, 2, group_pad, ff_half), bf16), ((4, 2, group_pad, ff_half), bf16),
     ]
     return pl.pallas_call(
         backward_kernel,
-        in_specs=[ANY] * 3 + [vmem] * 2 + [ANY] * 9,
+        in_specs=[ANY] * 3 + [vmem] * 3 + [ANY] * 12,
         out_specs=[ANY] * len(outs),
         out_shape=[jax.ShapeDtypeStruct(s, t) for s, t in outs],
         scratch_shapes=[pltpu.VMEM(s, t) for s, t in scratch]
         + [
-            dma((9,)), dma((chunks,)), dma((chunks,)), dma((2, chunks)), dma((2, chunks)), dma((6, chunks)), dma((1,)),
+            dma((10,)), dma((chunks,)), dma((chunks,)), dma((2, chunks)), dma((2, chunks)),
+            dma((2 * chunks,)), dma((2, 2, 2)), pltpu.SemaphoreType.REGULAR,
+            dma((5,)), dma((5,)), dma((4, 2)), dma((4, 2)), dma((4, 2, 2)), dma((4, 2, 2)), dma((4, 2)), dma((4, 2)),
+            dma((4, 2)), dma((2, 4)),
         ],
         compiler_params=pltpu.CompilerParams(has_side_effects=True, vmem_limit_bytes=62 * 2**20),
         name="backward_relay",
-    )(w_attn, w_ff, g, norms, mask, ent, q, k, k1, v, v1, o, lse, up)
-
-
-def add_into(total, term):
-    total[...] = (total[...].astype(f32) + term[...].astype(f32)).astype(bf16)
-
-
-def reduce_kernel(*refs):
-    attn_terms, ff_terms = refs[0:4], refs[4:8]
-    attn_out, ff_out = refs[8:10]
-    held, first, second, third = refs[10:14]
-    load, first_send, first_recv, second_send, second_recv, third_send, third_recv, last_send, last_recv = refs[14:]
-    section, ctx, shard = lax.axis_index("section"), lax.axis_index("ctx"), lax.axis_index("shard")
-    kind = lax.rem(shard, 2)
-    near = lambda c, step: c + step - 2 * step * lax.rem(c // step, 2)
-    x_ctx, y_ctx = near(ctx, 1), near(ctx, 2)
-    d_ctx = near(x_ctx, 2)
-    count = len(attn_terms)
-
-    def reduce(terms, out_ref, which):
-        width = terms[0].shape[-1]
-        cols = pl.ds(0, width)
-        own = lambda i, c, j: held.at[i, c, j, :, cols]
-
-        def give(i):
-            return remote(
-                terms[i].at[:, section], first.at[i, :, :, :, cols], first_send.at[i], first_recv.at[i],
-                1 - section, ctx, shard,
-            )
-
-        def take(i):
-            return pltpu.make_async_copy(terms[i].at[:, 1 - section], held.at[i, :, :, :, cols], load.at[i])
-
-        def second_copy(i, j, part):
-            to = (x_ctx, y_ctx)[j]
-            return remote(
-                own(i, (to, d_ctx)[part], j), second.at[i, j, part, :, cols],
-                second_send.at[i, j, part], second_recv.at[i, j, part], section, to, shard,
-            )
-
-        def third_copy(i, j):
-            to = (y_ctx, x_ctx)[j]
-            return remote(
-                own(i, to, j), third.at[i, j, :, cols], third_send.at[i, j], third_recv.at[i, j], section, to, shard
-            )
-
-        def last_copy(i, j):
-            return remote(
-                own(i, ctx, j), out_ref.at[i], last_send.at[i, j], last_recv.at[which, i],
-                shard // 2, ctx, 2 * (1 - section) + j,
-            )
-
-        for i in range(count):
-            give(i).start()
-            take(i).start()
-        for step in range(count + 2):
-            i = step
-            if i < count:
-                take(i).wait()
-                give(i).wait_recv()
-
-                @pl.loop(0, 4)
-                def _(c):
-                    for j in range(2):
-                        add_into(own(i, c, j), first.at[i, c, j, :, cols])
-
-                for part in (1, 0):
-                    for j in range(2):
-                        second_copy(i, j, part).start()
-            i = step - 1
-            if 0 <= i < count:
-                for j in range(2):
-                    second_copy(i, j, 1).wait_recv()
-                    add_into(own(i, (y_ctx, x_ctx)[j], j), second.at[i, j, 1, :, cols])
-                    third_copy(i, j).start()
-                for j in range(2):
-                    second_copy(i, j, 0).wait_recv()
-                    add_into(own(i, ctx, j), second.at[i, j, 0, :, cols])
-            i = step - 2
-            if 0 <= i < count:
-                for j in range(2):
-                    third_copy(i, j).wait_recv()
-                    add_into(own(i, ctx, j), third.at[i, j, :, cols])
-                    last_copy(i, j).start()
-        for i in range(count):
-            give(i).wait_send()
-            for j in range(2):
-                for part in range(2):
-                    second_copy(i, j, part).wait_send()
-                third_copy(i, j).wait_send()
-                last_copy(i, j).wait_send()
-
-    @pl.when(kind == 0)
-    def _():
-        reduce(attn_terms, attn_out, 0)
-
-    @pl.when(kind == 1)
-    def _():
-        reduce(ff_terms, ff_out, 1)
-
-    for i in range(count):
-        for which, out_ref in enumerate((attn_out, ff_out)):
-            remote(
-                out_ref.at[i], out_ref.at[i], last_send.at[i, 0], last_recv.at[which, i], section, ctx, shard
-            ).wait_recv()
-
-
-def reduce_all(attn_terms, ff_terms):
-    rows = attn_terms[0].shape[0] // 16
-    count = len(attn_terms)
-    split = lambda v: v.reshape(4, 2, 2, rows, v.shape[1])
-    width = ff_terms[0].shape[1]
-    dma = pltpu.SemaphoreType.DMA
-    return pl.pallas_call(
-        reduce_kernel,
-        in_specs=[ANY] * (2 * count),
-        out_specs=[ANY] * 2,
-        out_shape=[
-            jax.ShapeDtypeStruct((count, rows, attn_terms[0].shape[1]), bf16),
-            jax.ShapeDtypeStruct((count, rows, width), bf16),
-        ],
-        scratch_shapes=[
-            pltpu.VMEM((count, 4, 2, rows, width), bf16),
-            pltpu.VMEM((count, 4, 2, rows, width), bf16),
-            pltpu.VMEM((count, 2, 2, rows, width), bf16),
-            pltpu.VMEM((count, 2, rows, width), bf16),
-            dma((count,)), dma((count,)), dma((count,)),
-            dma((count, 2, 2)), dma((count, 2, 2)),
-            dma((count, 2)), dma((count, 2)),
-            dma((count, 2)), dma((2, count)),
-        ],
-        compiler_params=pltpu.CompilerParams(has_side_effects=True, vmem_limit_bytes=48 * 2**20),
-        name="reduce_all",
-    )(*[split(v) for v in attn_terms], *[split(v) for v in ff_terms])
+    )(w_attn, w_ff, g, norms, mask, place, ent, nrm, q, k, k1, v, v1, o, lse, up, hid, y)
 
 
 def chain(inputs, cotangent, qkv_weight, out_weight, up_weight, down_weight, norm_gain, norm_bias):
@@ -819,38 +893,22 @@
         return jnp.swapaxes(mine, 0, 1).reshape(tokens, width)
 
     g_last = bring_tokens(g_all, g_own)
-    feature = lax.broadcasted_iota(jnp.int32, (width, 16 * group_pad), 0)
-    place = lax.broadcasted_iota(jnp.int32, (width, 16 * group_pad), 1)
-    spread = (feature // group * group_pad + feature % group == place).astype(bf16)
-    grouped = lambda v: mm(v, spread).astype(bf16)
-
-    coming, leaving, dq, dk, dv, d_up, sums = backward_relay(
-        w_attn, w_ff, g_last, norms, mask, ent, q, k, k1, v, v1, o, lse, up
-    )
-    nrm_grouped, coming_grouped = grouped(nrm), grouped(coming)
-    ff_grads = [t_mm(nrm_grouped, d_up[i]) for i in range(2)] + [t_mm(coming_grouped, hid[i]) for i in range(2)]
-    o_grouped = grouped(o[:, :width].astype(bf16))
-    attn_grads = [t_mm(nrm_grouped, d) for d in (dq, dk, dv)]
-    attn_grads.append(t_mm(o_grouped, jnp.pad(coming, ((0, 0), (0, wide - width)))))
-    attn_sums, ff_sums = reduce_all([v.astype(bf16) for v in attn_grads], [v.astype(bf16) for v in ff_grads])
-
-    terms = sums[:2, :width]
-    terms = jnp.where(jnp.arange(4)[:, None, None] == shard, terms[None], 0.0)
-    totals = lax.psum(terms, ("section", "ctx", "shard")).reshape(2, 2, 2, width)
-    totals = lax.dynamic_index_in_dim(totals, section, 0, keepdims=False)
-    totals = lax.dynamic_slice_in_dim(totals, (ctx * 4 + shard) * group, group, 2)
-
-    final = jnp.where(is_attn, leaving, y).reshape(blocks, 4, half, width)
-    final = lax.all_to_all(jnp.swapaxes(final, 0, 1), "ctx", 0, 0)
-    final = lax.all_to_all(final, "shard", 0, 0).reshape(2, 2, blocks, half, width)
-    final = lax.all_to_all(final, "section", 0, 0)
-    final = jnp.moveaxis(final, 0, 2).reshape(2, blocks, slice_len, width)
-
+    slot = jnp.arange(up_to(8 * group_pad, LANES))
+    row = slot % group_pad
+    place = []
+    for side in (section, 1 - section):
+        owner = (slot // (2 * group_pad)) * 4 + 2 * side + (slot // group_pad) % 2
+        place.append(jnp.where((row < group) & (slot < 8 * group_pad), owner * group + row, -1))
+    place = jnp.broadcast_to(jnp.stack(place)[:, None].astype(jnp.int32), (2, ROWS, slot.shape[0]))
+    attn_sums, ff_sums, rows, totals = backward_relay(
+        w_attn, w_ff, g_last, norms, mask, place, ent, nrm, q, k, k1, v, v1, o, lse, up, hid, y, group_pad
+    )
+    totals = lax.dynamic_slice_in_dim(totals[:, :2], (ctx * 4 + shard) * group, group, 2)
     attn_sums = attn_sums[:, :group, :width].astype(f32)
     ff_sums = ff_sums[:, :group].astype(f32)
     return (
-        final[1][None, None],
-        final[0][None, None],
+        rows[1][None, None],
+        rows[0][None, None],
         jnp.concatenate([attn_sums[0], attn_sums[1], attn_sums[2]], axis=1)[None],
         attn_sums[3][None],
         jnp.concatenate([ff_sums[0], ff_sums[1]], axis=1)[None],

time: 575 us -> 457 us (0.79)
  the two profiles are of different devices: /device:TPU:0 before, /device:TPU:24 now
where the time goes in v5:
time: 457 us; the launch traced here: 449 us
  Pallas kernels  420 us (92%)
  local copies, waits for them, and re-layouts  21.2 us (5%)
  other arithmetic  6.99 us (2%)
    pallas_call x1, Pallas kernels, backward_relay(): pl.pallas_call(backward_kernel, in_specs=[ANY] * 3 + [vmem] * 3 + [ANY] *...  235 us
    pallas_call x1, Pallas kernels, forward_relay(): pl.pallas_call(forward_kernel, in_specs=[ANY] * 5 + [vmem], out_specs=[AN...  185 us
    unnamed x26, local copies, waits for them, and re-layouts  11.6 us

profile of v5, /device:TPU:24, one launch (start us, length us, event | category | flops | bytes accessed | tf_op | source)
XLA Modules:
  0.0 448.8 jit_solution(1185764830934928470)
XLA Ops:
  0.6 0.0 copy-start.7
  0.8 0.8 fusion.14
  1.5 0.1 fusion.10
  1.6 0.6 broadcast_in_dim.46.place_ref
  2.3 0.3 dynamic_update_slice.3.norm_ref
  2.5 0.0 copy-start.8
  2.6 0.7 pad_maximum_fusion.mask_ref
  3.3 0.0 copy-done.7
  3.3 0.0 copy-start.3
  3.3 1.6 constant_dynamic-slice_fusion.1
  4.8 0.0 copy-done.8
  4.8 1.0 copy.17
  5.8 1.0 copy.16
  6.8 0.0 copy-done.3
  6.8 0.3 fusion.17
  7.0 0.0 copy-start.6
  7.1 0.0 copy-start.9
  7.1 0.1 pad_bitcast_fusion.1
  7.2 0.9 copy-done.6
  8.1 0.0 copy-done.9
  8.1 0.0 copy-start.2
  8.1 0.1 fusion.8
  8.3 0.0 copy-start.1
  8.3 1.3 fusion.7.attn_ref
  9.6 0.3 copy-done.2
  9.9 0.9 copy-done.1
  10.8 0.4 slice_bitcast_fusion
  11.2 2.0 fusion.3.ff_ref
  13.1 0.0 copy-start
  13.1 184.5 %forward_relay.1 = (bf16[4,4,272,1152]{3,2,1,0:T(8,128)(2,1)}, bf16[4,4,272,2176]{3,2,1,0:T(8,128)(2,1)}, bf16[4,2,64,1088]{3,2,1,0:T(8,128)(2,1)}, f32[8,1152]{...) custom-call(bf16[272,1152]{1,0:T(8,128)(2,1)} %fusion.7.attn_ref, ...), custom_call_target="tpu_custom_call" | custom-call | tf_op jit(solution)/shard_map/forward_relay/pallas_call | solution.py:402
  197.7 0.0 copy-done
  197.7 1.5 select_bitcast_fusion
  199.1 1.1 copy.18
  200.2 235.0 %backward_relay.1 = (bf16[4,72,1152]{2,1,0:T(8,128)(2,1)}, bf16[4,72,2176]{2,1,0:T(8,128)(2,1)}, bf16[2,2,128,1088]{3,2,1,0:T(8,128)(2,1)}, f32[2,8,1152]{2,1,0:T(8,128)}) custom-call(bf16[4,4,272,1152]{3,2,1,0:T(8,128)(2,1)} %get-tuple-element.28.w_attn_ref, bf16[4,4,272,2176]{3,2,1,0:T(8,128)(2,1)} %get-tuple-element.29.w_ff_ref, ...), custom_call_target="tpu_custom_call" | custom-call | tf_op jit(solution)/shard_map/backward_relay/pallas_call | solution.py:841
  435.3 1.3 slice_bitcast_fusion.8
  436.6 0.0 copy-start.5
  436.6 1.1 copy.20
  437.7 0.9 slice.86
  438.6 0.6 constant_dynamic-slice_fusion
  439.2 1.1 copy.19
  440.3 0.0 copy-done.5
  440.3 0.1 slice_convert_fusion.1
  440.4 0.1 fusion.18
  440.5 1.0 copy.22
  441.5 0.2 concatenate.17
  441.7 0.0 copy-start.4
  441.7 1.9 copy.21
  443.6 0.0 copy-done.4
  443.6 0.2 slice_convert_fusion
  443.8 0.2 slice_bitcast_fusion.5
  443.9 0.1 maximum_bitcast_fusion.1
  444.0 2.2 copy.24
  446.3 0.1 maximum_bitcast_fusion
  446.3 2.2 copy.23
  (7 shorter events, 0.1 us)
Async XLA Ops:
  0.6 2.6 copy-start.7
  2.5 2.3 copy-start.8
  3.3 3.5 copy-start.3
  7.0 1.1 copy-start.6
  7.1 1.1 copy-start.9
  8.1 1.8 copy-start.2
  8.3 2.5 copy-start.1
  13.1 184.5 %copy-start = (bf16[1,2,64,1088]{3,2,1,0:T(8,128)(2,1)S(1)}, bf16[1,2,64,1088]{3,2,1,0:T(8,128)(2,1)}, u32[]{:S(2)}) copy-start(bf16[1,2,64,1088]{3,2,1,0:T(8,128)(2,1)} %copy.17) | copy-start | bytes 835588
  436.6 3.7 copy-start.5
  441.7 1.9 copy-start.4

commit v6 on v0

--- a/solution.py
+++ b/solution.py
@@ -1,13 +1,852 @@
+import functools
+
 import jax
 import jax.numpy as jnp
 from jax import lax
+from jax.experimental import pallas as pl
+from jax.experimental.pallas import tpu as pltpu
 from jax.sharding import PartitionSpec as P
 
 HEAD = 64
-
+LANES = 128
+ROWS = 8
+NEG = -1e30
+VMEM_BYTES = 66_900_000
 
 eps_norm = 1e-05
 score_scale = 0.125
+f32 = jnp.float32
+bf16 = jnp.bfloat16
+
+
+def up_to(width, step):
+    return -(-width // step) * step
+
+
+def dot(a, b, dims):
+    return lax.dot_general(a, b, (dims, ((), ())), preferred_element_type=f32)
+
+
+def mm(a, b):
+    return dot(a, b, ((1,), (0,)))
+
+
+def mm_t(a, b):
+    return dot(a, b, ((1,), (1,)))
+
+
+def t_mm(a, b):
+    return dot(a, b, ((0,), (0,)))
+
+
+def attention_masks(core, half):
+    row = lax.broadcasted_iota(jnp.int32, (2 * half, 2 * half), 0)
+    col = lax.broadcasted_iota(jnp.int32, (2 * half, 2 * half), 1)
+    row_slice, col_slice = row // half, col // half
+    own = (col_slice < row_slice) | ((col_slice == row_slice) & (col <= row))
+    other = (col_slice < row_slice) | ((col_slice == row_slice) & (core == 1))
+    return jnp.where(jnp.stack([own, other]), 0.0, NEG).astype(f32)
+
+
+def norm_backward(hat, scale, gain, grad):
+    scaled = grad * gain
+    mean = jnp.mean(scaled, axis=-1, keepdims=True)
+    along = jnp.mean(scaled * hat, axis=-1, keepdims=True)
+    return scale * (scaled - mean - hat * along)
+
+
+ANY = pl.BlockSpec(memory_space=pl.ANY)
+
+
+def remote(src, dst, send, recv, section, ctx, shard):
+    return pltpu.make_async_remote_copy(
+        src_ref=src,
+        dst_ref=dst,
+        send_sem=send,
+        recv_sem=recv,
+        device_id=(section, ctx, shard),
+        device_id_type=pl.DeviceIdType.MESH,
+    )
+
+
+def normalised(values):
+    mean = jnp.mean(values, axis=-1, keepdims=True)
+    centred = values - mean
+    var = jnp.mean(centred * centred, axis=-1, keepdims=True)
+    scale = lax.rsqrt(var + eps_norm)
+    return centred * scale, scale
+
+
+def stack_heads(value, low):
+    zero = jnp.zeros_like(value)
+    return jnp.concatenate([jnp.where(low, value, zero), jnp.where(low, zero, value)], axis=0)
+
+
+def unstack_heads(value, low):
+    rows = value.shape[0] // 2
+    return jnp.where(low, value[:rows], value[rows:])
+
+
+def mask_last(scores, mask):
+    width = mask.shape[1]
+    last = scores[:, scores.shape[1] - width :] + mask
+    if scores.shape[1] == width:
+        return last
+    return jnp.concatenate([scores[:, : scores.shape[1] - width], last], axis=1)
+
+
+def attend_chunk(u, rows, mask_ref, q, k, k1, v, v1, o, lse):
+    size = rows.size
+    keys = pl.ds(0, (u + 1) * size)
+    lane = lax.broadcasted_iota(jnp.int32, (size, LANES), 1)
+    low = lane < HEAD
+
+    @pl.loop(0, q.shape[1] // LANES, unroll=3)
+    def _(pair):
+        cols = pl.ds(pl.multiple_of(pair * LANES, LANES), LANES)
+        q2 = stack_heads(q[rows, cols], low)
+        scores = [mask_last(mm_t(q2, ref[keys, cols]), mask_ref[part]) for part, ref in enumerate((k, k1))]
+        top = jnp.maximum(
+            jnp.max(scores[0], axis=1, keepdims=True), jnp.max(scores[1], axis=1, keepdims=True)
+        )
+        total, acc = 0.0, 0.0
+        for s, ref in zip(scores, (v, v1)):
+            p = jnp.exp(s - top)
+            total = total + jnp.sum(p, axis=1, keepdims=True)
+            acc = acc + mm(p.astype(bf16), ref[keys, cols])
+        o[rows, cols] = unstack_heads(acc / total, low)
+        level = top + jnp.log(total)
+        lse[rows, :] = jnp.where(
+            lane == 2 * pair, level[:size], jnp.where(lane == 2 * pair + 1, level[size:], lse[rows, :])
+        )
+
+
+def near_ctx(c, step):
+    return c + step - 2 * step * lax.rem(c // step, 2)
+
+
+def add_into(total, term):
+    total[...] = (total[...].astype(f32) + term[...].astype(f32)).astype(bf16)
+
+
+def relay_kernel(
+    attn_ref, ff_ref, x_ref, g_ref, norm_ref, mask_ref, place_ref,
+    attn_out, ff_out, rows_out, sums_out,
+    w, tokens, norm_all, norms, ent, nrm, lea, coming, slots, o, lse, da, big, sums, sums_in, spread, first, second, third,
+    send, recv, token_send, token_recv, norm_send, norm_recv, far_send,
+    up_send, up_recv, down_send, down_recv, pair_send, pair_recv, swap_send, swap_recv, rows_send, rows_recv, free,
+    sums_send, sums_recv, first_send, first_recv, second_send, second_recv, third_send, third_recv, last_send, last_recv,
+):
+    section, ctx, shard = lax.axis_index("section"), lax.axis_index("ctx"), lax.axis_index("shard")
+    kind = lax.rem(shard, 2)
+    late = shard // 2
+    far_core = 1 - late
+    x_ctx, y_ctx = near_ctx(ctx, 1), near_ctx(ctx, 2)
+    d_ctx = near_ctx(x_ctx, 2)
+    width = ent.shape[1]
+    wide = attn_ref.shape[1]
+    size = da.shape[0]
+    half = size // 2
+    chunks = ent.shape[0] // size
+    ff_half = ff_ref.shape[1]
+    attn_cols = pl.ds(0, wide)
+    ff_cols = pl.ds(0, ff_half)
+    parts = ((0, wide), (wide, ff_half - wide))
+
+    x_copy = remote(x_ref, tokens.at[ctx], token_send.at[0], token_recv.at[ctx], section, shard, 0)
+    g_copy = remote(g_ref, tokens.at[ctx], token_send.at[1], token_recv.at[ctx], section, shard, 3)
+    x_stays = (shard == 0) & (ctx == 0)
+    g_stays = (shard == 3) & (ctx == 3)
+    attn_copy = remote(
+        attn_ref, w.at[ctx, shard, :, attn_cols], far_send.at[0], recv.at[ctx, shard], far_core, ctx, 2 * section
+    )
+    ff_copy = remote(
+        ff_ref, w.at[ctx, shard, :, ff_cols], far_send.at[1], recv.at[ctx, shard], far_core, ctx, 2 * section + 1
+    )
+    norm_local = pltpu.make_async_copy(norm_ref, norm_all.at[shard], norm_recv.at[shard])
+
+    def start_unless(stays, copy, src):
+        @pl.when(stays)
+        def _():
+            pltpu.make_async_copy(src, tokens.at[ctx], token_recv.at[ctx]).start()
+
+        @pl.when(jnp.logical_not(stays))
+        def _():
+            copy.start()
+
+    attn_copy.start()
+    start_unless(x_stays, x_copy, x_ref)
+    norm_copies = []
+    for core in range(2):
+        for stage in range(2):
+            copy = remote(
+                norm_ref, norm_all.at[shard], norm_send.at[core * 2 + stage], norm_recv.at[shard],
+                core, ctx, 2 * section + stage,
+            )
+            stays = (section == core) & (shard == 2 * section + stage)
+            norm_copies.append((copy, stays))
+
+            @pl.when(stays)
+            def _():
+                norm_local.start()
+
+            @pl.when(jnp.logical_not(stays))
+            def _():
+                copy.start()
+
+    ff_copy.start()
+    start_unless(g_stays, g_copy, g_ref)
+
+    def piece(cols, c, s, which, core, to_ctx):
+        ref = w.at[c, s, :, cols]
+        return remote(ref, ref, send.at[which], recv.at[c, s], core, to_ctx, shard)
+
+    def collect(cols):
+        here = lax.rem(section + late, 2)
+        mine = [
+            here * shard + (1 - here) * (2 - late),
+            here * (shard + 1 - 2 * kind) + (1 - here) * (3 - 3 * late),
+        ]
+        started = []
+
+        def go(c, s, core, to_ctx):
+            copy = piece(cols, c, s, len(started), core, to_ctx)
+            copy.start()
+            started.append(copy)
+
+        def arrived(c, s):
+            piece(cols, c, s, 0, section, ctx).wait_recv()
+
+        for s in mine:
+            arrived(ctx, s)
+            go(ctx, s, section, x_ctx)
+            go(ctx, s, section, y_ctx)
+            go(ctx, s, 1 - section, ctx)
+        arrived(x_ctx, mine[0])
+        go(x_ctx, mine[0], section, y_ctx)
+        go(x_ctx, mine[0], 1 - section, ctx)
+        arrived(y_ctx, mine[0])
+        go(y_ctx, mine[0], 1 - section, ctx)
+        arrived(y_ctx, mine[1])
+        go(y_ctx, mine[1], section, x_ctx)
+        go(y_ctx, mine[1], 1 - section, ctx)
+        arrived(x_ctx, mine[1])
+        go(x_ctx, mine[1], 1 - section, ctx)
+        for s in mine:
+            arrived(d_ctx, s)
+            go(d_ctx, s, 1 - section, ctx)
+        for c in (ctx, x_ctx, y_ctx, d_ctx):
+            for j in range(2):
+                arrived(c, 2 * section + j)
+        for s in range(4):
+            pltpu.make_async_copy(norm_ref, norm_all.at[s], norm_recv.at[s]).wait()
+        norms[...] = (norm_all[0] + norm_all[1]) + (norm_all[2] + norm_all[3])
+        return started
+
+    def tokens_arrived():
+        for c in range(4):
+            pltpu.make_async_copy(x_ref, tokens.at[c], token_recv.at[c]).wait()
+
+    def tokens_of(u):
+        return tokens[pl.ds(2 * lax.rem(u, 2), 2), u // 2].reshape(size, width)
+
+    def chunk_rows(u):
+        return pl.ds(pl.multiple_of(u * size, size), size)
+
+    def up_copy(u, stage):
+        rows = chunk_rows(u)
+        return remote(lea.at[rows], ent.at[rows], up_send.at[u], up_recv.at[u], section, ctx, stage)
+
+    def down_copy(u, stage):
+        rows = chunk_rows(u)
+        return remote(ent.at[rows], coming.at[rows], down_send.at[u], down_recv.at[u], section, ctx, stage)
+
+    def weight(c, start, columns):
+        value = w[c, :, :, pl.ds(start, columns)]
+        return value.reshape(value.shape[0] * value.shape[1], columns)
+
+    def rows_copy(src, t, local):
+        block, c = t // 4, lax.rem(t, 4)
+        src = src.at[pl.ds(pl.multiple_of(t * half, half), half)]
+        dst = rows_out.at[kind, block, pl.ds(pl.multiple_of(section * half, half), half)]
+        recv = rows_recv.at[kind, section, block]
+        if local:
+            return pltpu.make_async_copy(src, dst, recv)
+        return remote(src, dst, rows_send.at[t], recv, shard // 2, c, ctx)
+
+    def rows_stay(t):
+        return (section == shard // 2) & (ctx == lax.rem(t, 4)) & (ctx == shard)
+
+    def rows_start(src, t):
+        @pl.when(rows_stay(t))
+        def _():
+            rows_copy(src, t, True).start()
+
+        @pl.when(jnp.logical_not(rows_stay(t)))
+        def _():
+            rows_copy(src, t, False).start()
+
+    def rows_finish(src):
+        @pl.loop(0, 2 * chunks)
+        def _(t):
+
+            @pl.when(jnp.logical_not(rows_stay(t)))
+            def _():
+                rows_copy(src, t, False).wait_send()
+
+    def finish_chunk(rows, d_normed, gain):
+        hat, scale = normalised(ent[rows].astype(f32))
+        sums[0:1, :width] += jnp.sum(d_normed * hat, axis=0, keepdims=True)
+        sums[1:2, :width] += jnp.sum(d_normed, axis=0, keepdims=True)
+        total = coming[rows].astype(f32) + norm_backward(hat, scale, gain, d_normed)
+        ent[rows] = total.astype(bf16)
+
+    sums[...] = jnp.zeros_like(sums)
+
+    def group_columns(index, ref):
+        feature = lax.broadcasted_iota(jnp.int32, (LANES, width), 1)
+
+        @pl.loop(0, 2)
+        def _(side):
+            @pl.loop(0, spread.shape[2] // LANES)
+            def _(tile):
+                at = pl.ds(pl.multiple_of(tile * LANES, LANES), LANES)
+                chosen = jnp.where(feature == place_ref[side, at, 0:1], 1.0, 0.0).astype(bf16)
+                spread[index, side, at, :] = mm_t(chosen, ref[...]).astype(bf16)
+
+    def reduce(source, pieces, turn, out_ref, which):
+        rows = first.shape[3]
+        gap = up_to(rows, 16)
+        count = out_ref.shape[0]
+        lanes = lambda p: pl.ds(pieces[p][0], pieces[p][1])
+        own = lambda a, p, c, j: w.at[a, c, pl.ds(gap * j, rows), lanes(p)]
+        array = lambda a: lax.rem(a + turn, count)
+
+        def first_copy(a, p, j):
+            even = lax.rem(a, 2)
+            return remote(
+                w.at[2 * even + j, :, pl.ds(2 * gap, rows), lanes(p)], first.at[even, j, :, :, lanes(p)],
+                first_send.at[a, p, j], first_recv.at[a, p, j], 1 - section, ctx, shard,
+            )
+
+        def second_copy(a, p, j, part):
+            to = (x_ctx, y_ctx)[j]
+            return remote(
+                own(a, p, (to, d_ctx)[part], j), second.at[a, j, part, :, lanes(p)],
+                second_send.at[a, p, j, part], second_recv.at[a, p, j, part], section, to, shard,
+            )
+
+        def third_copy(a, p, j):
+            to = (y_ctx, x_ctx)[j]
+            return remote(
+                own(a, p, to, j), third.at[a, j, :, lanes(p)],
+                third_send.at[a, p, j], third_recv.at[a, p, j], section, to, shard,
+            )
+
+        def last_copy(a, p, j):
+            return remote(
+                own(a, p, ctx, j), out_ref.at[array(a), :, lanes(p)],
+                last_send.at[a, p, j], last_recv.at[which, array(a), p],
+                shard // 2, ctx, 2 * (1 - section) + j,
+            )
+
+        def terms(a, p):
+            @pl.loop(0, 2)
+            def _(side):
+                def emit(index, ref, columns):
+                    def block(at, step):
+                        value = mm(spread[index, side, pl.ds(0, 8 * rows), :], ref[:, pl.ds(at, step)])
+                        cols = pl.ds(pl.multiple_of(pieces[p][0] + at, LANES), step)
+                        for n in range(8):
+                            lead = side * a + (1 - side) * (2 * lax.rem(a, 2) + n % 2)
+                            row = pl.multiple_of(side * (gap * (n % 2)) + (1 - side) * 2 * gap, 16)
+                            w[lead, n // 2, pl.ds(row, rows), cols] = value[n * rows : (n + 1) * rows].astype(bf16)
+
+                    step = 2 * LANES
+
+                    @pl.loop(0, columns // step)
+                    def _(b):
+                        block(pl.multiple_of(b * step, step), step)
+
+                    if columns % step:
+                        block(columns - columns % step, columns % step)
+
+                source(a, p, side, emit)
+
+                @pl.when(side == 0)
+                def _():
+                    for j in range(2):
+                        first_copy(a, p, j).start()
+
+        def stage_one(a, p):
+            @pl.when(a >= 2)
+            def _():
+                for j in range(2):
+                    first_copy(a - 2, p, j).wait_send()
+                pl.semaphore_wait(free, 1)
+
+            terms(a, p)
+            for j in range(2):
+                first_copy(a, p, j).wait_recv()
+
+                @pl.loop(0, 4)
+                def _(c):
+                    add_into(own(a, p, c, j), first.at[lax.rem(a, 2), j, c, :, lanes(p)])
+
+            @pl.when(a + 2 < count)
+            def _():
+                pl.semaphore_signal(
+                    free, inc=1, device_id=(1 - section, ctx, shard), device_id_type=pl.DeviceIdType.MESH
+                )
+
+            for part in (1, 0):
+                for j in range(2):
+                    second_copy(a, p, j, part).start()
+
+        def stage_two(a, p):
+            for j in range(2):
+                second_copy(a, p, j, 1).wait_recv()
+                add_into(own(a, p, (y_ctx, x_ctx)[j], j), second.at[a, j, 1, :, lanes(p)])
+                third_copy(a, p, j).start()
+            for j in range(2):
+                second_copy(a, p, j, 0).wait_recv()
+                add_into(own(a, p, ctx, j), second.at[a, j, 0, :, lanes(p)])
+
+        def stage_three(a, p):
+            for j in range(2):
+                third_copy(a, p, j).wait_recv()
+                add_into(own(a, p, ctx, j), third.at[a, j, :, lanes(p)])
+                last_copy(a, p, j).start()
+
+        def sums_copy(step):
+            to_core, to_ctx = ((1 - section, ctx), (section, x_ctx), (section, y_ctx))[step]
+            return remote(sums, sums_in.at[step], sums_send.at[step], sums_recv.at[step], to_core, to_ctx, shard)
+
+        def sums_last(j):
+            return remote(
+                sums, sums_out.at[which], sums_send.at[3 + j], sums_recv.at[3 + which],
+                shard // 2, ctx, 2 * (1 - section) + j,
+            )
+
+        sums_copy(0).start()
+        items = len(pieces)
+
+        @pl.loop(0, count + 2)
+        def _(a):
+            for p in range(items):
+
+                @pl.when(a < count)
+                def _():
+                    stage_one(a, p)
+
+                back = [(-(-(d - p) // items), (p - d) % items) for d in (1, 2)]
+
+                @pl.when((a >= back[0][0]) & (a < count + back[0][0]))
+                def _():
+                    stage_two(a - back[0][0], back[0][1])
+
+                @pl.when((a >= back[1][0]) & (a < count + back[1][0]))
+                def _():
+                    stage_three(a - back[1][0], back[1][1])
+
+            for step in range(3):
+
+                @pl.when(a == step)
+                def _():
+                    sums_copy(step).wait()
+                    sums[...] += sums_in[step]
+                    if step < 2:
+                        sums_copy(step + 1).start()
+                    else:
+                        for j in range(2):
+                            sums_last(j).start()
+
+        @pl.loop(0, count)
+        def _(a):
+            for p in range(items):
+                for j in range(2):
+
+                    @pl.when(a >= count - 2)
+                    def _():
+                        first_copy(a, p, j).wait_send()
+
+                    for part in range(2):
+                        second_copy(a, p, j, part).wait_send()
+                    third_copy(a, p, j).wait_send()
+                    last_copy(a, p, j).wait_send()
+
+        for j in range(2):
+            sums_last(j).wait_send()
+
+    @pl.when(kind == 0)
+    def _():
+        started = collect(attn_cols)
+
+        @pl.when(shard == 0)
+        def _():
+            tokens_arrived()
+
+        lse[...] = jnp.zeros_like(lse)
+        da[...] = jnp.zeros_like(da)
+        gain, bias = norms[0:1, :width], norms[2:3, :width]
+
+        def pair_copy(which, u):
+            rows = chunk_rows(u)
+            return remote(
+                slots.at[1 + which, rows], slots.at[3 + which, rows], pair_send.at[which, u], pair_recv.at[which, u],
+                1 - section, ctx, shard,
+            )
+
+        @pl.loop(0, chunks)
+        def _(u):
+            rows = chunk_rows(u)
+
+            @pl.when(shard == 0)
+            def _():
+                ent[rows] = tokens_of(u)
+
+            @pl.when(shard > 0)
+            def _():
+                up_copy(u, shard).wait_recv()
+
+            hat, _ = normalised(ent[rows].astype(f32))
+            normed = (hat * gain + bias).astype(bf16)
+            nrm[rows] = normed
+
+            @pl.loop(0, 3)
+            def _(turn):
+                index = lax.rem(turn + 1, 3)
+                scale = jnp.where(turn == 2, score_scale, 1.0)
+                slots[index, rows] = (mm(normed, weight(index, 0, wide)) * scale).astype(bf16)
+
+                @pl.when(turn < 2)
+                def _():
+                    pair_copy(turn, u).start()
+
+            for which in range(2):
+                pair_copy(which, u).wait_recv()
+            for index in range(chunks):
+
+                @pl.when(u == index)
+                def _():
+                    attend_chunk(
+                        index, pl.ds(index * size, size), mask_ref,
+                        slots.at[0], slots.at[1], slots.at[3], slots.at[2], slots.at[4], o, lse,
+                    )
+
+            out = mm(o[rows, :width].astype(bf16), weight(3, 0, wide))[:, :width]
+            lea[rows] = (ent[rows].astype(f32) + out).astype(bf16)
+            up_copy(u, shard + 1).start()
+
+        @pl.loop(0, chunks)
+        def _(u):
+            for which in range(2):
+                pair_copy(which, u).wait_send()
+            up_copy(u, shard + 1).wait_send()
+
+        for copy in started:
+            copy.wait_send()
+
+        lane = lax.broadcasted_iota(jnp.int32, (size, LANES), 1)
+        low = lane < HEAD
+
+        def swap_copy(which, u):
+            rows = chunk_rows(u)
+            return remote(
+                slots.at[3 + which, rows], slots.at[5 + which, rows], swap_send.at[which, u], swap_recv.at[which, u],
+                1 - section, ctx, shard,
+            )
+
+        @pl.loop(0, chunks)
+        def _(step):
+            u = chunks - 1 - step
+            rows_now = chunk_rows(u)
+            down_copy(u, shard).wait_recv()
+            da[:, :width] = mm_t(coming[rows_now], weight(3, 0, width)).astype(bf16)
+            for index in range(chunks):
+
+                @pl.when(u == index)
+                def _():
+                    rows = pl.ds(index * size, size)
+                    keys = pl.ds(0, (index + 1) * size)
+
+                    @pl.loop(0, wide // LANES, unroll=3)
+                    def _(pair):
+                        cols = pl.ds(pl.multiple_of(pair * LANES, LANES), LANES)
+                        q2 = stack_heads(slots[0, rows, cols], low)
+                        grad = da[:, cols]
+                        a2 = stack_heads(grad, low)
+                        level = lse[rows, :]
+                        product = grad.astype(f32) * o[rows, cols]
+                        column = lambda which: jnp.sum(jnp.where(lane == 2 * pair + which, level, 0.0), axis=1, keepdims=True)
+                        level2 = jnp.concatenate([column(0), column(1)], axis=0)
+                        delta2 = jnp.concatenate(
+                            [
+                                jnp.sum(jnp.where(low, product, 0.0), axis=1, keepdims=True),
+                                jnp.sum(jnp.where(low, 0.0, product), axis=1, keepdims=True),
+                            ],
+                            axis=0,
+                        )
+                        dq2 = 0.0
+                        for part in range(2):
+                            keys_now, values_now = slots[1 + 2 * part, keys, cols], slots[2 + 2 * part, keys, cols]
+                            p = jnp.exp(mask_last(mm_t(q2, keys_now), mask_ref[part]) - level2)
+                            ds = (p * (mm_t(a2, values_now) - delta2)).astype(bf16)
+                            dq2 = dq2 + mm(ds, keys_now)
+                            d_keys, d_values = t_mm(ds, q2), t_mm(p.astype(bf16), a2)
+                            if index == chunks - 1:
+                                big[2 * part, keys, cols] = d_keys
+                                big[2 * part + 1, keys, cols] = d_values
+                            else:
+                                big[2 * part, keys, cols] += d_keys
+                                big[2 * part + 1, keys, cols] += d_values
+                        slots[0, rows, cols] = (unstack_heads(dq2, low) * score_scale).astype(bf16)
+
+            rows = rows_now
+            for which in range(2):
+                slots[3 + which, rows] = big[2 + which, rows].astype(bf16)
+                swap_copy(which, u).start()
+
+            def finish_part(which, total):
+                swap_copy(which, u).wait_recv()
+                slots[1 + which, rows] = (big[which, rows] + slots[5 + which, rows].astype(f32)).astype(bf16)
+                return total + mm_t(slots[1 + which, rows], weight(1 + which, 0, wide))
+
+            d_normed = lax.fori_loop(0, 2, finish_part, mm_t(slots[0, rows], weight(0, 0, wide)))
+            finish_chunk(rows, d_normed, gain)
+
+            @pl.when(shard > 0)
+            def _():
+                down_copy(u, shard - 1).start()
+
+            for part in range(2):
+                rows_start(ent, 2 * u + part)
+
+        @pl.loop(0, chunks)
+        def _(u):
+            for which in range(2):
+                swap_copy(which, u).wait_send()
+
+        slots[3] = o[...].astype(bf16)
+        group_columns(0, nrm)
+        group_columns(1, slots.at[3, :, pl.ds(0, width)])
+
+        def attn_source(a, p, side, emit):
+            @pl.when(a == 0)
+            def _():
+                emit(1, coming, width)
+
+            @pl.when(a > 0)
+            def _():
+                emit(0, slots.at[jnp.maximum(a - 1, 0)], wide)
+
+        reduce(attn_source, ((0, wide),), 3, attn_out, 0)
+        rows_finish(ent)
+
+        @pl.loop(0, chunks)
+        def _(u):
+
+            @pl.when(shard > 0)
+            def _():
+                down_copy(u, shard - 1).wait_send()
+
+    @pl.when(kind == 1)
+    def _():
+        started = collect(ff_cols)
+        gain, bias = norms[1:2, :width], norms[3:4, :width]
+
+        @pl.loop(0, chunks)
+        def _(u):
+            rows = chunk_rows(u)
+            up_copy(u, shard).wait_recv()
+            hat, _ = normalised(ent[rows].astype(f32))
+            normed = (hat * gain + bias).astype(bf16)
+            nrm[rows] = normed
+
+            def add_half(i, total):
+                for part, (start, columns) in enumerate(parts):
+                    cols = pl.ds(0, columns)
+                    upper = mm(normed, weight(i, start, columns))
+                    big[2 * i + part, rows, cols] = upper
+                    hidden = jax.nn.gelu(upper, approximate=True).astype(bf16)
+                    slots[4 + 2 * i + part, rows, cols] = hidden
+                    total = total + mm_t(hidden, weight(2 + i, start, columns))
+                return total
+
+            lea[rows] = lax.fori_loop(0, 2, add_half, ent[rows].astype(f32)).astype(bf16)
+
+            @pl.when(shard < 3)
+            def _():
+                up_copy(u, shard + 1).start()
+
+            for part in range(2):
+                rows_start(lea, 2 * u + part)
+
+        @pl.when(shard == 3)
+        def _():
+            tokens_arrived()
+
+        @pl.loop(0, chunks)
+        def _(step):
+            u = chunks - 1 - step
+            rows = chunk_rows(u)
+
+            @pl.when(shard == 3)
+            def _():
+                coming[rows] = tokens_of(u)
+
+            @pl.when(shard < 3)
+            def _():
+                down_copy(u, shard).wait_recv()
+
+            grad = coming[rows]
+
+            def back_half(i, total):
+                for part, (start, columns) in enumerate(parts):
+                    cols = pl.ds(0, columns)
+                    d_hidden = mm(grad, weight(2 + i, start, columns))
+                    _, back = jax.vjp(lambda value: jax.nn.gelu(value, approximate=True), big[2 * i + part, rows, cols])
+                    d_upper = back(d_hidden)[0].astype(bf16)
+                    slots[2 * i + part, rows, cols] = d_upper
+                    total = total + mm_t(d_upper, weight(i, start, columns))
+                return total
+
+            finish_chunk(rows, lax.fori_loop(0, 2, back_half, jnp.zeros((size, width), f32)), gain)
+            down_copy(u, shard - 1).start()
+
+        for copy in started:
+            copy.wait_send()
+        group_columns(1, coming)
+        group_columns(0, nrm)
+
+        def ff_source(a, p, side, emit):
+            emit(1 - a // 2, slots.at[lax.rem(2 * a + 4, 8) + p], parts[p][1])
+
+        reduce(ff_source, parts, 2, ff_out, 1)
+        rows_finish(lea)
+
+        @pl.loop(0, chunks)
+        def _(u):
+
+            @pl.when(shard < 3)
+            def _():
+                up_copy(u, shard + 1).wait_send()
+
+            down_copy(u, shard - 1).wait_send()
+
+    @pl.loop(0, attn_out.shape[0])
+    def _(index):
+        arrivals = [(0, attn_out, 0, 0, wide)] + [(1, ff_out, p, start, columns) for p, (start, columns) in enumerate(parts)]
+        for which, ref, p, start, columns in arrivals:
+            ref = ref.at[index, :, pl.ds(start, columns)]
+            remote(ref, ref, last_send.at[index, 0, 0], last_recv.at[which, index, p], section, ctx, shard).wait_recv()
+
+    for which in range(2):
+        remote(sums, sums_out.at[which], sums_send.at[3], sums_recv.at[3 + which], section, ctx, shard).wait_recv()
+        for core in range(2):
+            for block in range(2):
+                ref = rows_out.at[which, block, pl.ds(core * half, half)]
+                pltpu.make_async_copy(ref, ref, rows_recv.at[which, core, block]).wait()
+
+    attn_copy.wait_send()
+    ff_copy.wait_send()
+    for copy, stays in norm_copies + [(x_copy, x_stays), (g_copy, g_stays)]:
+
+        @pl.when(jnp.logical_not(stays))
+        def _():
+            copy.wait_send()
+
+
+def relay(attn_piece, ff_piece, x_own, g_own, norm_own, mask, place, group_pad):
+    share, ff_half = ff_piece.shape
+    wide = attn_piece.shape[1]
+    blocks, half, width = x_own.shape
+    tokens = blocks * 4 * half
+    size = 2 * half
+    chunks = tokens // size
+    dma = pltpu.SemaphoreType.DMA
+    vmem = pl.BlockSpec(memory_space=pltpu.VMEM)
+    narrow = ((tokens, width), bf16)
+    outs = [
+        ((4, group_pad, wide), bf16), ((4, group_pad, ff_half), bf16), ((2, blocks, size, width), bf16), ((2,) + norm_own.shape, f32),
+    ]
+    scratch = [
+        ((4, 4, share, ff_half), bf16), ((4,) + x_own.shape, bf16), ((4,) + norm_own.shape, f32), (norm_own.shape, f32),
+        narrow, narrow, narrow, narrow, ((8, tokens, wide), bf16),
+        ((tokens, wide), f32), ((tokens, LANES), f32), ((size, wide), bf16), ((4, tokens, wide), f32),
+        (norm_own.shape, f32), ((3,) + norm_own.shape, f32), ((2, 2, place.shape[1], tokens), bf16),
+        ((2, 2, 4, group_pad, ff_half), bf16), ((4, 2, 2, group_pad, ff_half), bf16), ((4, 2, group_pad, ff_half), bf16),
+    ]
+    return pl.pallas_call(
+        relay_kernel,
+        in_specs=[ANY] * 5 + [vmem] * 2,
+        out_specs=[ANY] * len(outs),
+        out_shape=[jax.ShapeDtypeStruct(s, t) for s, t in outs],
+        scratch_shapes=[pltpu.VMEM(s, t) for s, t in scratch]
+        + [
+            dma((14,)), dma((4, 4)), dma((2,)), dma((4,)), dma((4,)), dma((4,)), dma((2,)),
+            dma((chunks,)), dma((chunks,)), dma((chunks,)), dma((chunks,)),
+            dma((2, chunks)), dma((2, chunks)), dma((2, chunks)), dma((2, chunks)),
+            dma((2 * chunks,)), dma((2, 2, 2)), pltpu.SemaphoreType.REGULAR,
+            dma((5,)), dma((5,)), dma((4, 2, 2)), dma((4, 2, 2)), dma((4, 2, 2, 2)), dma((4, 2, 2, 2)),
+            dma((4, 2, 2)), dma((4, 2, 2)), dma((4, 2, 2)), dma((2, 4, 2)),
+        ],
+        compiler_params=pltpu.CompilerParams(has_side_effects=True, vmem_limit_bytes=VMEM_BYTES),
+        name="relay",
+    )(attn_piece, ff_piece, x_own, g_own, norm_own, mask, place)
+
+
+def chain(inputs, cotangent, qkv_weight, out_weight, up_weight, down_weight, norm_gain, norm_bias):
+    section, ctx, shard = lax.axis_index("section"), lax.axis_index("ctx"), lax.axis_index("shard")
+    seq_count, blocks, slice_len, width = inputs.shape
+    half = slice_len // 2
+    tokens = blocks * 4 * half
+    share = width // 4
+    group = share // 4
+    group_pad = up_to(group, ROWS)
+    wide = up_to(width, LANES)
+    ff = up_weight.shape[2]
+    is_attn = shard % 2 == 0
+
+    pad = lambda w: jnp.pad(w, ((0, 0), (0, wide - width)))
+    own_qkv, own_out = qkv_weight[0], out_weight[0]
+    attn_src = jnp.stack([pad(own_qkv[:, i * width : (i + 1) * width]) for i in range(3)] + [pad(own_out)])
+    down_t = down_weight[0].T
+    up0 = up_weight[0]
+    ff_src = jnp.stack([up0[:, : ff // 2], up0[:, ff // 2 :], down_t[:, : ff // 2], down_t[:, ff // 2 :]])
+    norm_own = jnp.concatenate([norm_gain[0], norm_bias[0]], axis=0).astype(f32)
+    norm_own = lax.dynamic_update_slice(
+        jnp.zeros((ROWS, wide), f32), jnp.pad(norm_own, ((0, ROWS - 4), (0, 0))), (0, shard * share)
+    )
+    x_own = lax.dynamic_slice_in_dim(inputs[0], section * half, half, 1)
+    g_own = lax.dynamic_slice_in_dim(cotangent[0], section * half, half, 1)
+    mask = attention_masks(section, half)
+    mask = jnp.concatenate([mask, mask], axis=1)
+    slot = jnp.arange(up_to(8 * group_pad, LANES))
+    row = slot % group_pad
+    place = []
+    for side in (section, 1 - section):
+        owner = (slot // (2 * group_pad)) * 4 + 2 * side + (slot // group_pad) % 2
+        place.append(jnp.where((row < group) & (slot < 8 * group_pad), owner * group + row, -1))
+    place = jnp.broadcast_to(jnp.stack(place)[:, :, None].astype(jnp.int32), (2, slot.shape[0], LANES))
+    attn_sums, ff_sums, rows, totals = relay(
+        lax.dynamic_index_in_dim(attn_src, ctx, 0, keepdims=False),
+        lax.dynamic_index_in_dim(ff_src, ctx, 0, keepdims=False),
+        x_own, g_own, norm_own, mask, place, group_pad,
+    )
+    totals = lax.dynamic_slice_in_dim(totals[:, :2], (ctx * 4 + shard) * group, group, 2)
+    attn_sums = attn_sums[:, :group, :width].astype(f32)
+    ff_sums = ff_sums[:, :group].astype(f32)
+    return (
+        rows[1][None, None],
+        rows[0][None, None],
+        jnp.concatenate([attn_sums[0], attn_sums[1], attn_sums[2]], axis=1)[None],
+        attn_sums[3][None],
+        jnp.concatenate([ff_sums[0], ff_sums[1]], axis=1)[None],
+        jnp.concatenate([ff_sums[2].T, ff_sums[3].T], axis=0)[None],
+        totals[:, 0][None],
+        totals[:, 1][None],
+    )
 
 
 def passed_along(value, axis, steps):
@@ -396,4 +1235,5 @@
         P("section", None, ("ctx", "shard")),
         P("section", None, ("ctx", "shard")),
     )
-    return jax.shard_map(shards, mesh=mesh, in_specs=in_specs, out_specs=out_specs, check_vma=False)
+    relay = mesh.shape["section"] == 2 and mesh.shape["shard"] == 4 and mesh.shape["ctx"] == 4
+    return jax.shard_map(chain if relay else shards, mesh=mesh, in_specs=in_specs, out_specs=out_specs, check_vma=False)

time: 2690 us -> 402 us (0.15)
  blocking collectives: 1440 us -> 0 us
  waiting for transfers between devices: 641 us -> 0 us
  Pallas kernels: 0 us -> 374 us
  matrix products: 361 us -> 0 us
  local copies, waits for them, and re-layouts: 125 us -> 19.5 us
  starting transfers between devices: 36.2 us -> 0 us
  other arithmetic: 39.3 us -> 7.3 us
    unnamed x3 -> x0, blocking collectives: 1350 us -> none
    all_gather x13 -> x0, waiting for transfers between devices: 635 us -> none  [the longest x1 164 us: shards(): lax.all_gather(up_weight[0], 'shard', axis=0, tiled=True)]
    pallas_call x0 -> x1, Pallas kernels: none -> 374 us  [relay(): pl.pallas_call(relay_kernel, in_specs=[ANY] * 5 + [vmem] * 2, out_specs=[...]
    dot_general x78 -> x0, matrix products: 361 us -> none  [the longest x12 38.7 us: score_grads(): jnp.einsum('sqhe,kshe->sqhk', queries, key_rows, preferred_element_type=j...]
    all_gather x8 -> x0, blocking collectives: 94 us -> none  [the longest x3 25.3 us: shards(): lax.all_gather(log_total, 'ctx', axis=1, tiled=True)]
    unnamed x405 -> x28, local copies, waits for them, and re-layouts: 60.3 us -> 11.7 us
    slice x12 -> x4, local copies, waits for them, and re-layouts: 39.2 us -> 3.18 us  [the longest x1 1.56 us: chain(): own_qkv[:, i * width:(i + 1) * width]]
    unnamed x6 -> x0, starting transfers between devices: 28.5 us -> none
  transfers between devices with their start and end apart: 23 -> 0, of which waited for: 12 -> 0; matrix products, arithmetic and copies ran while one was open for 26% -> 0% of each run, Pallas kernels for 0% -> 0%
where the time goes in v6:
time: 402 us
  Pallas kernels  374 us (93%)
  local copies, waits for them, and re-layouts  19.5 us (5%)
  other arithmetic  7.3 us (2%)
    pallas_call x1, Pallas kernels, relay(): pl.pallas_call(relay_kernel, in_specs=[ANY] * 5 + [vmem] * 2, out_specs=[...  374 us
    unnamed x28, local copies, waits for them, and re-layouts  11.7 us

profile of v6, /device:TPU:24, one launch (start us, length us, event | category | flops | bytes accessed | tf_op | source)
XLA Modules:
  0.0 402.1 jit_solution(16973912926552575865)
XLA Ops:
  0.6 1.6 fusion.17
  2.2 0.0 copy-start.4
  2.2 0.0 copy-start.8
  2.2 0.1 pad_bitcast_fusion.1
  2.4 0.9 copy-done.4
  3.3 0.0 copy-done.8
  3.3 0.0 copy-start.1
  3.3 1.4 fusion.8
  4.6 0.0 copy-start
  4.7 1.3 fusion.7.attn_ref
  6.0 0.0 copy-done.1
  6.0 0.7 copy-done
  6.7 0.4 slice_bitcast_fusion
  7.1 0.0 copy-start.5
  7.1 0.0 copy-start.6
  7.1 2.0 fusion.3.ff_ref
  9.1 0.0 copy-done.5
  9.1 0.0 copy-done.6
  9.1 0.4 constant_dynamic-slice_fusion.1
  9.4 0.9 copy.16
  10.4 0.0 copy-start.9
  10.4 0.0 copy-start.10
  10.4 0.9 copy.17
  11.4 1.1 broadcast_in_dim.32.place_ref
  12.5 0.1 fusion.10
  12.6 0.7 pad_maximum_fusion.mask_ref
  13.4 0.0 copy-done.9
  13.4 0.0 copy-done.10
  13.4 0.3 dynamic_update_slice.3.norm_ref
  13.7 0.0 copy-start.7
  13.7 0.6 copy-done.7
  14.3 374.4 %relay.1 = (bf16[4,72,1152]{2,1,0:T(8,128)(2,1)}, bf16[4,72,2176]{2,1,0:T(8,128)(2,1)}, bf16[2,2,128,1088]{3,2,1,0:T(8,128)(2,1)}, f32[2,8,1152]{2,1,0:T(8,128)}) custom-call(bf16[272,1152]{1,0:T(8,128)(2,1)} %fusion.7.attn_ref, bf16[272,2176]{1,0:T(8,128)(2,1)} %fusion.3.ff_ref, bf16[2,64,1088]{2,1,0:T(8,128)(2,1)} %bitcast.64, ...), custom_call_target="tpu_custom_call" | custom-call | tf_op jit(solution)/shard_map/relay/pallas_call | solution.py:780
  388.8 1.5 slice_convert_fusion
  390.2 0.2 slice_bitcast_fusion.5
  390.4 0.1 maximum_bitcast_fusion.1
  390.5 2.2 copy.23
  392.7 0.1 maximum_bitcast_fusion
  392.8 0.0 copy-start.3
  392.8 2.2 copy.22
  395.1 0.0 copy-done.3
  395.1 0.1 slice_convert_fusion.1
  395.1 0.1 fusion.18
  395.2 0.2 concatenate.17
  395.5 0.0 copy-start.2
  395.5 1.9 copy.20
  397.3 1.0 copy.21
  398.4 0.0 copy-done.2
  398.4 0.1 slice_bitcast_fusion.8
  398.5 1.1 copy.18
  399.5 1.0 copy.19
  400.6 0.9 slice.86
  401.5 0.6 constant_dynamic-slice_fusion
  (7 shorter events, 0.1 us)
Async XLA Ops:
  2.2 1.1 copy-start.4
  2.2 1.1 copy-start.8
  3.3 2.7 copy-start.1
  4.6 2.0 copy-start
  7.1 2.0 copy-start.5
  7.1 2.0 copy-start.6
  10.4 3.0 copy-start.9
  10.4 3.0 copy-start.10
  13.7 0.6 copy-start.7
  392.8 2.2 copy-start.3
  395.5 2.9 copy-start.2

commit v7 on v6

--- a/solution.py
+++ b/solution.py
@@ -153,8 +153,12 @@
     ff_cols = pl.ds(0, ff_half)
     parts = ((0, wide), (wide, ff_half - wide))
 
-    x_copy = remote(x_ref, tokens.at[ctx], token_send.at[0], token_recv.at[ctx], section, shard, 0)
-    g_copy = remote(g_ref, tokens.at[ctx], token_send.at[1], token_recv.at[ctx], section, shard, 3)
+    def token_copy(which, block):
+        src, stage = ((x_ref, 0), (g_ref, 3))[which]
+        return remote(
+            src.at[block], tokens.at[ctx, block], token_send.at[which, block], token_recv.at[ctx, block], section, shard, stage
+        )
+
     x_stays = (shard == 0) & (ctx == 0)
     g_stays = (shard == 3) & (ctx == 3)
     attn_copy = remote(
@@ -165,17 +169,20 @@
     )
     norm_local = pltpu.make_async_copy(norm_ref, norm_all.at[shard], norm_recv.at[shard])
 
-    def start_unless(stays, copy, src):
+    def token_start(which, block, stays):
+        src = (x_ref, g_ref)[which]
+
         @pl.when(stays)
         def _():
-            pltpu.make_async_copy(src, tokens.at[ctx], token_recv.at[ctx]).start()
+            pltpu.make_async_copy(src.at[block], tokens.at[ctx, block], token_recv.at[ctx, block]).start()
 
         @pl.when(jnp.logical_not(stays))
         def _():
-            copy.start()
-
+            token_copy(which, block).start()
+
+    token_start(0, 0, x_stays)
     attn_copy.start()
-    start_unless(x_stays, x_copy, x_ref)
+    token_start(0, 1, x_stays)
     norm_copies = []
     for core in range(2):
         for stage in range(2):
@@ -195,7 +202,8 @@
                 copy.start()
 
     ff_copy.start()
-    start_unless(g_stays, g_copy, g_ref)
+    for block in (1, 0):
+        token_start(1, block, g_stays)
 
     def piece(cols, c, s, which, core, to_ctx):
         ref = w.at[c, s, :, cols]
@@ -243,9 +251,10 @@
         norms[...] = (norm_all[0] + norm_all[1]) + (norm_all[2] + norm_all[3])
         return started
 
-    def tokens_arrived():
-        for c in range(4):
-            pltpu.make_async_copy(x_ref, tokens.at[c], token_recv.at[c]).wait()
+    def tokens_arrived(u):
+        for c in range(2):
+            at = 2 * lax.rem(u, 2) + c
+            pltpu.make_async_copy(x_ref.at[0], tokens.at[at, u // 2], token_recv.at[at, u // 2]).wait()
 
     def tokens_of(u):
         return tokens[pl.ds(2 * lax.rem(u, 2), 2), u // 2].reshape(size, width)
@@ -482,10 +491,6 @@
     def _():
         started = collect(attn_cols)
 
-        @pl.when(shard == 0)
-        def _():
-            tokens_arrived()
-
         lse[...] = jnp.zeros_like(lse)
         da[...] = jnp.zeros_like(da)
         gain, bias = norms[0:1, :width], norms[2:3, :width]
@@ -503,6 +508,7 @@
 
             @pl.when(shard == 0)
             def _():
+                tokens_arrived(u)
                 ent[rows] = tokens_of(u)
 
             @pl.when(shard > 0)
@@ -547,6 +553,9 @@
         for copy in started:
             copy.wait_send()
 
+        slots[7] = o[...].astype(bf16)
+        group_columns(0, nrm)
+        group_columns(1, slots.at[7, :, pl.ds(0, width)])
         lane = lax.broadcasted_iota(jnp.int32, (size, LANES), 1)
         low = lane < HEAD
 
@@ -627,10 +636,6 @@
             for which in range(2):
                 swap_copy(which, u).wait_send()
 
-        slots[3] = o[...].astype(bf16)
-        group_columns(0, nrm)
-        group_columns(1, slots.at[3, :, pl.ds(0, width)])
-
         def attn_source(a, p, side, emit):
             @pl.when(a == 0)
             def _():
@@ -682,9 +687,9 @@
             for part in range(2):
                 rows_start(lea, 2 * u + part)
 
-        @pl.when(shard == 3)
+        @pl.when(shard < 3)
         def _():
-            tokens_arrived()
+            group_columns(0, nrm)
 
         @pl.loop(0, chunks)
         def _(step):
@@ -693,6 +698,7 @@
 
             @pl.when(shard == 3)
             def _():
+                tokens_arrived(u)
                 coming[rows] = tokens_of(u)
 
             @pl.when(shard < 3)
@@ -716,13 +722,21 @@
 
         for copy in started:
             copy.wait_send()
-        group_columns(1, coming)
-        group_columns(0, nrm)
+
+        @pl.when(shard == 3)
+        def _():
+            group_columns(0, nrm)
 
         def ff_source(a, p, side, emit):
-            emit(1 - a // 2, slots.at[lax.rem(2 * a + 4, 8) + p], parts[p][1])
-
-        reduce(ff_source, parts, 2, ff_out, 1)
+            if p == 0:
+
+                @pl.when((a == 2) & (side == 0))
+                def _():
+                    group_columns(1, coming)
+
+            emit(a // 2, slots.at[2 * a + p], parts[p][1])
+
+        reduce(ff_source, parts, 0, ff_out, 1)
         rows_finish(lea)
 
         @pl.loop(0, chunks)
@@ -750,7 +764,9 @@
 
     attn_copy.wait_send()
     ff_copy.wait_send()
-    for copy, stays in norm_copies + [(x_copy, x_stays), (g_copy, g_stays)]:
+    for copy, stays in norm_copies + [
+        (token_copy(which, block), stays) for which, stays in enumerate((x_stays, g_stays)) for block in range(2)
+    ]:
 
         @pl.when(jnp.logical_not(stays))
         def _():
@@ -784,7 +800,7 @@
         out_shape=[jax.ShapeDtypeStruct(s, t) for s, t in outs],
         scratch_shapes=[pltpu.VMEM(s, t) for s, t in scratch]
         + [
-            dma((14,)), dma((4, 4)), dma((2,)), dma((4,)), dma((4,)), dma((4,)), dma((2,)),
+            dma((14,)), dma((4, 4)), dma((2, 2)), dma((4, 2)), dma((4,)), dma((4,)), dma((2,)),
             dma((chunks,)), dma((chunks,)), dma((chunks,)), dma((chunks,)),
             dma((2, chunks)), dma((2, chunks)), dma((2, chunks)), dma((2, chunks)),
             dma((2 * chunks,)), dma((2, 2, 2)), pltpu.SemaphoreType.REGULAR,

time: 402 us -> 399 us (level); the launches traced: 402 us -> 391 us
  Pallas kernels: 374 us -> 363 us
    pallas_call x1, Pallas kernels: 374 us -> 363 us  [relay(): pl.pallas_call(relay_kernel, in_specs=[ANY] * 5 + [vmem] * 2, out_specs=[...]
where the time goes in v7:
time: 399 us; the launch traced here: 391 us
  Pallas kernels  363 us (91%)
  local copies, waits for them, and re-layouts  19.5 us (5%)
  other arithmetic  7.3 us (2%)
    pallas_call x1, Pallas kernels, relay(): pl.pallas_call(relay_kernel, in_specs=[ANY] * 5 + [vmem] * 2, out_specs=[...  363 us
    unnamed x28, local copies, waits for them, and re-layouts  11.7 us

profile of v7, /device:TPU:24, one launch (start us, length us, event | category | flops | bytes accessed | tf_op | source)
XLA Modules:
  0.0 391.1 jit_solution(9338915925082449374)
XLA Ops:
  0.6 1.6 fusion.17
  2.2 0.0 copy-start.4
  2.2 0.0 copy-start.8
  2.2 0.1 pad_bitcast_fusion.1
  2.4 0.9 copy-done.4
  3.3 0.0 copy-done.8
  3.3 0.0 copy-start.1
  3.3 1.4 fusion.8
  4.6 0.0 copy-start
  4.7 1.3 fusion.7.attn_ref
  6.0 0.0 copy-done.1
  6.0 0.7 copy-done
  6.7 0.4 slice_bitcast_fusion
  7.1 0.0 copy-start.5
  7.1 0.0 copy-start.6
  7.1 2.0 fusion.3.ff_ref
  9.1 0.0 copy-done.5
  9.1 0.0 copy-done.6
  9.1 0.4 constant_dynamic-slice_fusion.1
  9.4 0.9 copy.16
  10.4 0.0 copy-start.9
  10.4 0.0 copy-start.10
  10.4 0.9 copy.17
  11.4 1.1 broadcast_in_dim.32.place_ref
  12.5 0.1 fusion.10
  12.6 0.7 pad_maximum_fusion.mask_ref
  13.4 0.0 copy-done.9
  13.4 0.0 copy-done.10
  13.4 0.3 dynamic_update_slice.3.norm_ref
  13.7 0.0 copy-start.7
  13.7 0.6 copy-done.7
  14.3 362.9 %relay.1 = (bf16[4,72,1152]{2,1,0:T(8,128)(2,1)}, bf16[4,72,2176]{2,1,0:T(8,128)(2,1)}, bf16[2,2,128,1088]{3,2,1,0:T(8,128)(2,1)}, f32[2,8,1152]{2,1,0:T(8,128)}) custom-call(bf16[272,1152]{1,0:T(8,128)(2,1)} %fusion.7.attn_ref, bf16[272,2176]{1,0:T(8,128)(2,1)} %fusion.3.ff_ref, bf16[2,64,1088]{2,1,0:T(8,128)(2,1)} %bitcast.64, ...), custom_call_target="tpu_custom_call" | custom-call | tf_op jit(solution)/shard_map/relay/pallas_call | solution.py:796
  377.3 1.5 slice_convert_fusion
  378.7 0.2 slice_bitcast_fusion.5
  378.9 0.1 maximum_bitcast_fusion.1
  379.0 2.2 copy.23
  381.2 0.1 maximum_bitcast_fusion
  381.3 0.0 copy-start.3
  381.3 2.2 copy.22
  383.6 0.0 copy-done.3
  383.6 0.1 slice_convert_fusion.1
  383.7 0.1 fusion.18
  383.8 0.2 concatenate.17
  384.0 0.0 copy-start.2
  384.0 1.9 copy.20
  385.8 1.0 copy.21
  386.9 0.0 copy-done.2
  386.9 0.1 slice_bitcast_fusion.8
  387.0 1.1 copy.18
  388.0 1.0 copy.19
  389.1 0.9 slice.86
  390.0 0.6 constant_dynamic-slice_fusion
  (7 shorter events, 0.1 us)
Async XLA Ops:
  2.2 1.1 copy-start.4
  2.2 1.1 copy-start.8
  3.3 2.7 copy-start.1
  4.6 2.0 copy-start
  7.1 2.0 copy-start.5
  7.1 2.0 copy-start.6
  10.4 3.0 copy-start.9
  10.4 3.0 copy-start.10
  13.7 0.6 copy-start.7
  381.3 2.2 copy-start.3
  384.0 2.9 copy-start.2

commit v8 on v7

--- a/solution.py
+++ b/solution.py
@@ -132,10 +132,11 @@
 def relay_kernel(
     attn_ref, ff_ref, x_ref, g_ref, norm_ref, mask_ref, place_ref,
     attn_out, ff_out, rows_out, sums_out,
-    w, tokens, norm_all, norms, ent, nrm, lea, coming, slots, o, lse, da, big, sums, sums_in, spread, first, second, third,
+    w, staged, norm_all, norms, ent, nrm, lea, coming, slots, o, lse, da, big, sums, sums_in, spread, first, second, third,
     send, recv, token_send, token_recv, norm_send, norm_recv, far_send,
     up_send, up_recv, down_send, down_recv, pair_send, pair_recv, swap_send, swap_recv, rows_send, rows_recv, free,
     sums_send, sums_recv, first_send, first_recv, second_send, second_recv, third_send, third_recv, last_send, last_recv,
+    staged_recv, pass_send,
 ):
     section, ctx, shard = lax.axis_index("section"), lax.axis_index("ctx"), lax.axis_index("shard")
     kind = lax.rem(shard, 2)
@@ -153,12 +154,29 @@
     ff_cols = pl.ds(0, ff_half)
     parts = ((0, wide), (wide, ff_half - wide))
 
-    def token_copy(which, block):
-        src, stage = ((x_ref, 0), (g_ref, 3))[which]
+    def token_rows(ref, c, block):
+        return ref.at[pl.ds(pl.multiple_of((block * 4 + c) * half, half), half)]
+
+    def x_copy(block, straight):
+        index = jnp.maximum(shard - 1, 0)
+        dst = token_rows(ent, ctx, block) if straight else staged.at[index, block]
+        arrived = token_recv.at[ctx, block] if straight else staged_recv.at[index, block]
         return remote(
-            src.at[block], tokens.at[ctx, block], token_send.at[which, block], token_recv.at[ctx, block], section, shard, stage
-        )
-
+            x_ref.at[block], dst, token_send.at[0, block], arrived, section, ctx * jnp.minimum(shard, 1), 0
+        )
+
+    def g_copy(block):
+        return remote(
+            g_ref.at[block], token_rows(coming, ctx, block), token_send.at[1, block], token_recv.at[ctx, block], section, shard, 3
+        )
+
+    def pass_copy(s, block):
+        return remote(
+            staged.at[s - 1, block], token_rows(ent, ctx, block), pass_send.at[s - 1, block], token_recv.at[ctx, block],
+            section, s, 0,
+        )
+
+    x_straight = (shard == 0) | (ctx == shard)
     x_stays = (shard == 0) & (ctx == 0)
     g_stays = (shard == 3) & (ctx == 3)
     attn_copy = remote(
@@ -169,20 +187,34 @@
     )
     norm_local = pltpu.make_async_copy(norm_ref, norm_all.at[shard], norm_recv.at[shard])
 
-    def token_start(which, block, stays):
-        src = (x_ref, g_ref)[which]
-
-        @pl.when(stays)
+    def stay_copy(src, dst, block):
+        return pltpu.make_async_copy(src.at[block], token_rows(dst, ctx, block), token_recv.at[ctx, block])
+
+    def x_start(block):
+        @pl.when(x_stays)
         def _():
-            pltpu.make_async_copy(src.at[block], tokens.at[ctx, block], token_recv.at[ctx, block]).start()
-
-        @pl.when(jnp.logical_not(stays))
+            stay_copy(x_ref, ent, block).start()
+
+        @pl.when(x_straight & jnp.logical_not(x_stays))
         def _():
-            token_copy(which, block).start()
-
-    token_start(0, 0, x_stays)
+            x_copy(block, True).start()
+
+        @pl.when(jnp.logical_not(x_straight))
+        def _():
+            x_copy(block, False).start()
+
+    def pass_on(block):
+        for s in range(1, 4):
+
+            @pl.when((shard == 0) & (ctx != s))
+            def _():
+                ref = staged.at[s - 1, block]
+                pltpu.make_async_copy(ref, ref, staged_recv.at[s - 1, block]).wait()
+                pass_copy(s, block).start()
+
+    x_start(0)
     attn_copy.start()
-    token_start(0, 1, x_stays)
+    x_start(1)
     norm_copies = []
     for core in range(2):
         for stage in range(2):
@@ -203,7 +235,15 @@
 
     ff_copy.start()
     for block in (1, 0):
-        token_start(1, block, g_stays)
+
+        @pl.when(g_stays)
+        def _():
+            stay_copy(g_ref, coming, block).start()
+
+        @pl.when(jnp.logical_not(g_stays))
+        def _():
+            g_copy(block).start()
+
 
     def piece(cols, c, s, which, core, to_ctx):
         ref = w.at[c, s, :, cols]
@@ -225,11 +265,13 @@
         def arrived(c, s):
             piece(cols, c, s, 0, section, ctx).wait_recv()
 
-        for s in mine:
+        for turn, s in enumerate(mine):
             arrived(ctx, s)
             go(ctx, s, section, x_ctx)
             go(ctx, s, section, y_ctx)
             go(ctx, s, 1 - section, ctx)
+            if cols is attn_cols:
+                pass_on(turn)
         arrived(x_ctx, mine[0])
         go(x_ctx, mine[0], section, y_ctx)
         go(x_ctx, mine[0], 1 - section, ctx)
@@ -251,13 +293,11 @@
         norms[...] = (norm_all[0] + norm_all[1]) + (norm_all[2] + norm_all[3])
         return started
 
-    def tokens_arrived(u):
+    def tokens_arrived(u, ref):
         for c in range(2):
             at = 2 * lax.rem(u, 2) + c
-            pltpu.make_async_copy(x_ref.at[0], tokens.at[at, u // 2], token_recv.at[at, u // 2]).wait()
-
-    def tokens_of(u):
-        return tokens[pl.ds(2 * lax.rem(u, 2), 2), u // 2].reshape(size, width)
+            dst = token_rows(ref, at, u // 2)
+            pltpu.make_async_copy(dst, dst, token_recv.at[at, u // 2]).wait()
 
     def chunk_rows(u):
         return pl.ds(pl.multiple_of(u * size, size), size)
@@ -328,7 +368,8 @@
         gap = up_to(rows, 16)
         count = out_ref.shape[0]
         lanes = lambda p: pl.ds(pieces[p][0], pieces[p][1])
-        own = lambda a, p, c, j: w.at[a, c, pl.ds(gap * j, rows), lanes(p)]
+        own = lambda a, p, c, j: w.at[a, c, pl.ds(pl.multiple_of(gap * j, 16), rows), lanes(p)]
+        x_or_y = lambda j: x_ctx + j * (y_ctx - x_ctx)
         array = lambda a: lax.rem(a + turn, count)
 
         def first_copy(a, p, j):
@@ -339,14 +380,14 @@
             )
 
         def second_copy(a, p, j, part):
-            to = (x_ctx, y_ctx)[j]
+            to = x_or_y(j)
             return remote(
                 own(a, p, (to, d_ctx)[part], j), second.at[a, j, part, :, lanes(p)],
                 second_send.at[a, p, j, part], second_recv.at[a, p, j, part], section, to, shard,
             )
 
         def third_copy(a, p, j):
-            to = (y_ctx, x_ctx)[j]
+            to = x_or_y(1 - j)
             return remote(
                 own(a, p, to, j), third.at[a, j, :, lanes(p)],
                 third_send.at[a, p, j], third_recv.at[a, p, j], section, to, shard,
@@ -395,7 +436,9 @@
                 pl.semaphore_wait(free, 1)
 
             terms(a, p)
-            for j in range(2):
+
+            @pl.loop(0, 2)
+            def _(j):
                 first_copy(a, p, j).wait_recv()
 
                 @pl.loop(0, 4)
@@ -413,16 +456,20 @@
                     second_copy(a, p, j, part).start()
 
         def stage_two(a, p):
-            for j in range(2):
+            @pl.loop(0, 2)
+            def _(j):
                 second_copy(a, p, j, 1).wait_recv()
-                add_into(own(a, p, (y_ctx, x_ctx)[j], j), second.at[a, j, 1, :, lanes(p)])
+                add_into(own(a, p, x_or_y(1 - j), j), second.at[a, j, 1, :, lanes(p)])
                 third_copy(a, p, j).start()
-            for j in range(2):
+
+            @pl.loop(0, 2)
+            def _(j):
                 second_copy(a, p, j, 0).wait_recv()
                 add_into(own(a, p, ctx, j), second.at[a, j, 0, :, lanes(p)])
 
         def stage_three(a, p):
-            for j in range(2):
+            @pl.loop(0, 2)
+            def _(j):
                 third_copy(a, p, j).wait_recv()
                 add_into(own(a, p, ctx, j), third.at[a, j, :, lanes(p)])
                 last_copy(a, p, j).start()
@@ -508,8 +555,7 @@
 
             @pl.when(shard == 0)
             def _():
-                tokens_arrived(u)
-                ent[rows] = tokens_of(u)
+                tokens_arrived(u, ent)
 
             @pl.when(shard > 0)
             def _():
@@ -698,8 +744,7 @@
 
             @pl.when(shard == 3)
             def _():
-                tokens_arrived(u)
-                coming[rows] = tokens_of(u)
+                tokens_arrived(u, coming)
 
             @pl.when(shard < 3)
             def _():
@@ -764,9 +809,19 @@
 
     attn_copy.wait_send()
     ff_copy.wait_send()
-    for copy, stays in norm_copies + [
-        (token_copy(which, block), stays) for which, stays in enumerate((x_stays, g_stays)) for block in range(2)
-    ]:
+    for block in range(2):
+
+        @pl.when(jnp.logical_not(x_stays))
+        def _():
+            x_copy(block, True).wait_send()
+
+        for s in range(1, 4):
+
+            @pl.when((shard == 0) & (ctx != s))
+            def _():
+                pass_copy(s, block).wait_send()
+
+    for copy, stays in norm_copies + [(g_copy(block), g_stays) for block in range(2)]:
 
         @pl.when(jnp.logical_not(stays))
         def _():
@@ -787,7 +842,7 @@
         ((4, group_pad, wide), bf16), ((4, group_pad, ff_half), bf16), ((2, blocks, size, width), bf16), ((2,) + norm_own.shape, f32),
     ]
     scratch = [
-        ((4, 4, share, ff_half), bf16), ((4,) + x_own.shape, bf16), ((4,) + norm_own.shape, f32), (norm_own.shape, f32),
+        ((4, 4, share, ff_half), bf16), ((3,) + x_own.shape, bf16), ((4,) + norm_own.shape, f32), (norm_own.shape, f32),
         narrow, narrow, narrow, narrow, ((8, tokens, wide), bf16),
         ((tokens, wide), f32), ((tokens, LANES), f32), ((size, wide), bf16), ((4, tokens, wide), f32),
         (norm_own.shape, f32), ((3,) + norm_own.shape, f32), ((2, 2, place.shape[1], tokens), bf16),
@@ -805,7 +860,7 @@
             dma((2, chunks)), dma((2, chunks)), dma((2, chunks)), dma((2, chunks)),
             dma((2 * chunks,)), dma((2, 2, 2)), pltpu.SemaphoreType.REGULAR,
             dma((5,)), dma((5,)), dma((4, 2, 2)), dma((4, 2, 2)), dma((4, 2, 2, 2)), dma((4, 2, 2, 2)),
-            dma((4, 2, 2)), dma((4, 2, 2)), dma((4, 2, 2)), dma((2, 4, 2)),
+            dma((4, 2, 2)), dma((4, 2, 2)), dma((4, 2, 2)), dma((2, 4, 2)), dma((3, 2)), dma((3, 2)),
         ],
         compiler_params=pltpu.CompilerParams(has_side_effects=True, vmem_limit_bytes=VMEM_BYTES),
         name="relay",

time: 399 us -> 388 us (0.972); the launches traced: 391 us -> 388 us
  no operation moved by 1% of the time
where the time goes in v8:
time: 388 us
  Pallas kernels  360 us (93%)
  local copies, waits for them, and re-layouts  19.5 us (5%)
  other arithmetic  7.3 us (2%)
    pallas_call x1, Pallas kernels, relay(): pl.pallas_call(relay_kernel, in_specs=[ANY] * 5 + [vmem] * 2, out_specs=[...  360 us
    unnamed x28, local copies, waits for them, and re-layouts  11.7 us

profile of v8, /device:TPU:24, one launch (start us, length us, event | category | flops | bytes accessed | tf_op | source)
XLA Modules:
  0.0 387.9 jit_solution(3075311242053044933)
XLA Ops:
  0.6 1.6 fusion.17
  2.2 0.0 copy-start.4
  2.2 0.0 copy-start.8
  2.2 0.1 pad_bitcast_fusion.1
  2.4 0.9 copy-done.4
  3.3 0.0 copy-done.8
  3.3 0.0 copy-start.1
  3.3 1.4 fusion.8
  4.6 0.0 copy-start
  4.7 1.3 fusion.7.attn_ref
  6.0 0.0 copy-done.1
  6.0 0.7 copy-done
  6.7 0.4 slice_bitcast_fusion
  7.1 0.0 copy-start.5
  7.1 0.0 copy-start.6
  7.1 2.0 fusion.3.ff_ref
  9.1 0.0 copy-done.5
  9.1 0.0 copy-done.6
  9.1 0.4 constant_dynamic-slice_fusion.1
  9.4 0.9 copy.16
  10.4 0.0 copy-start.9
  10.4 0.0 copy-start.10
  10.4 0.9 copy.17
  11.4 1.1 broadcast_in_dim.32.place_ref
  12.5 0.1 fusion.10
  12.6 0.7 pad_maximum_fusion.mask_ref
  13.4 0.0 copy-done.9
  13.4 0.0 copy-done.10
  13.4 0.3 dynamic_update_slice.3.norm_ref
  13.7 0.0 copy-start.7
  13.7 0.6 copy-done.7
  14.3 360.2 %relay.1 = (bf16[4,72,1152]{2,1,0:T(8,128)(2,1)}, bf16[4,72,2176]{2,1,0:T(8,128)(2,1)}, bf16[2,2,128,1088]{3,2,1,0:T(8,128)(2,1)}, f32[2,8,1152]{2,1,0:T(8,128)}) custom-call(bf16[272,1152]{1,0:T(8,128)(2,1)} %fusion.7.attn_ref, bf16[272,2176]{1,0:T(8,128)(2,1)} %fusion.3.ff_ref, bf16[2,64,1088]{2,1,0:T(8,128)(2,1)} %bitcast.64, ...), custom_call_target="tpu_custom_call" | custom-call | tf_op jit(solution)/shard_map/relay/pallas_call | solution.py:851
  374.6 1.5 slice_convert_fusion
  376.0 0.2 slice_bitcast_fusion.5
  376.2 0.1 maximum_bitcast_fusion.1
  376.3 2.2 copy.23
  378.5 0.1 maximum_bitcast_fusion
  378.6 0.0 copy-start.3
  378.6 2.2 copy.22
  380.9 0.0 copy-done.3
  380.9 0.1 slice_convert_fusion.1
  381.0 0.1 fusion.18
  381.1 0.2 concatenate.17
  381.3 0.0 copy-start.2
  381.3 1.9 copy.20
  383.1 1.0 copy.21
  384.2 0.0 copy-done.2
  384.2 0.1 slice_bitcast_fusion.8
  384.3 1.1 copy.18
  385.3 1.0 copy.19
  386.4 0.9 slice.86
  387.3 0.6 constant_dynamic-slice_fusion
  (7 shorter events, 0.1 us)
Async XLA Ops:
  2.2 1.1 copy-start.4
  2.2 1.1 copy-start.8
  3.3 2.7 copy-start.1
  4.6 2.0 copy-start
  7.1 2.0 copy-start.5
  7.1 2.0 copy-start.6
  10.4 3.0 copy-start.9
  10.4 3.0 copy-start.10
  13.7 0.6 copy-start.7
  378.6 2.2 copy-start.3
  381.3 2.9 copy-start.2

commit v9 on v8

--- a/solution.py
+++ b/solution.py
@@ -157,17 +157,20 @@
     def token_rows(ref, c, block):
         return ref.at[pl.ds(pl.multiple_of((block * 4 + c) * half, half), half)]
 
+    def own_rows(ref, block):
+        return ref.at[block, pl.ds(pl.multiple_of(section * half, half), half)]
+
     def x_copy(block, straight):
         index = jnp.maximum(shard - 1, 0)
         dst = token_rows(ent, ctx, block) if straight else staged.at[index, block]
         arrived = token_recv.at[ctx, block] if straight else staged_recv.at[index, block]
         return remote(
-            x_ref.at[block], dst, token_send.at[0, block], arrived, section, ctx * jnp.minimum(shard, 1), 0
+            own_rows(x_ref, block), dst, token_send.at[0, block], arrived, section, ctx * jnp.minimum(shard, 1), 0
         )
 
     def g_copy(block):
         return remote(
-            g_ref.at[block], token_rows(coming, ctx, block), token_send.at[1, block], token_recv.at[ctx, block], section, shard, 3
+            own_rows(g_ref, block), token_rows(coming, ctx, block), token_send.at[1, block], token_recv.at[ctx, block], section, shard, 3
         )
 
     def pass_copy(s, block):
@@ -188,7 +191,7 @@
     norm_local = pltpu.make_async_copy(norm_ref, norm_all.at[shard], norm_recv.at[shard])
 
     def stay_copy(src, dst, block):
-        return pltpu.make_async_copy(src.at[block], token_rows(dst, ctx, block), token_recv.at[ctx, block])
+        return pltpu.make_async_copy(own_rows(src, block), token_rows(dst, ctx, block), token_recv.at[ctx, block])
 
     def x_start(block):
         @pl.when(x_stays)
@@ -212,9 +215,7 @@
                 pltpu.make_async_copy(ref, ref, staged_recv.at[s - 1, block]).wait()
                 pass_copy(s, block).start()
 
-    x_start(0)
     attn_copy.start()
-    x_start(1)
     norm_copies = []
     for core in range(2):
         for stage in range(2):
@@ -234,16 +235,20 @@
                 copy.start()
 
     ff_copy.start()
-    for block in (1, 0):
-
-        @pl.when(g_stays)
-        def _():
-            stay_copy(g_ref, coming, block).start()
-
-        @pl.when(jnp.logical_not(g_stays))
-        def _():
-            g_copy(block).start()
-
+    x_start(0)
+    x_start(1)
+    def g_start():
+        for block in (1, 0):
+
+            @pl.when(g_stays)
+            def _():
+                stay_copy(g_ref, coming, block).start()
+
+            @pl.when(jnp.logical_not(g_stays))
+            def _():
+                g_copy(block).start()
+
+    g_start()
 
     def piece(cols, c, s, which, core, to_ctx):
         ref = w.at[c, s, :, cols]
@@ -831,9 +836,9 @@
 def relay(attn_piece, ff_piece, x_own, g_own, norm_own, mask, place, group_pad):
     share, ff_half = ff_piece.shape
     wide = attn_piece.shape[1]
-    blocks, half, width = x_own.shape
+    blocks, size, width = x_own.shape
+    half = size // 2
     tokens = blocks * 4 * half
-    size = 2 * half
     chunks = tokens // size
     dma = pltpu.SemaphoreType.DMA
     vmem = pl.BlockSpec(memory_space=pltpu.VMEM)
@@ -842,7 +847,7 @@
         ((4, group_pad, wide), bf16), ((4, group_pad, ff_half), bf16), ((2, blocks, size, width), bf16), ((2,) + norm_own.shape, f32),
     ]
     scratch = [
-        ((4, 4, share, ff_half), bf16), ((3,) + x_own.shape, bf16), ((4,) + norm_own.shape, f32), (norm_own.shape, f32),
+        ((4, 4, share, ff_half), bf16), ((3, blocks, half, width), bf16), ((4,) + norm_own.shape, f32), (norm_own.shape, f32),
         narrow, narrow, narrow, narrow, ((8, tokens, wide), bf16),
         ((tokens, wide), f32), ((tokens, LANES), f32), ((size, wide), bf16), ((4, tokens, wide), f32),
         (norm_own.shape, f32), ((3,) + norm_own.shape, f32), ((2, 2, place.shape[1], tokens), bf16),
@@ -889,8 +894,6 @@
     norm_own = lax.dynamic_update_slice(
         jnp.zeros((ROWS, wide), f32), jnp.pad(norm_own, ((0, ROWS - 4), (0, 0))), (0, shard * share)
     )
-    x_own = lax.dynamic_slice_in_dim(inputs[0], section * half, half, 1)
-    g_own = lax.dynamic_slice_in_dim(cotangent[0], section * half, half, 1)
     mask = attention_masks(section, half)
     mask = jnp.concatenate([mask, mask], axis=1)
     slot = jnp.arange(up_to(8 * group_pad, LANES))
@@ -903,7 +906,7 @@
     attn_sums, ff_sums, rows, totals = relay(
         lax.dynamic_index_in_dim(attn_src, ctx, 0, keepdims=False),
         lax.dynamic_index_in_dim(ff_src, ctx, 0, keepdims=False),
-        x_own, g_own, norm_own, mask, place, group_pad,
+        inputs[0], cotangent[0], norm_own, mask, place, group_pad,
     )
     totals = lax.dynamic_slice_in_dim(totals[:, :2], (ctx * 4 + shard) * group, group, 2)
     attn_sums = attn_sums[:, :group, :width].astype(f32)

time: 388 us -> 384 us (0.990)
    unnamed x28 -> x30, local copies, waits for them, and re-layouts: 11.7 us -> 13.2 us
where the time goes in v9:
time: 384 us
  Pallas kernels  357 us (93%)
  local copies, waits for them, and re-layouts  18.8 us (5%)
  other arithmetic  7.31 us (2%)
    pallas_call x1, Pallas kernels, relay(): pl.pallas_call(relay_kernel, in_specs=[ANY] * 5 + [vmem] * 2, out_specs=[...  357 us
    unnamed x30, local copies, waits for them, and re-layouts  13.2 us

profile of v9, /device:TPU:24, one launch (start us, length us, event | category | flops | bytes accessed | tf_op | source)
XLA Modules:
  0.0 384.0 jit_solution(4773226119908954385)
XLA Ops:
  0.6 1.6 fusion.17
  2.2 0.0 copy-start.4
  2.2 0.0 copy-start.8
  2.2 0.1 pad_bitcast_fusion.1
  2.4 0.9 copy-done.4
  3.3 0.0 copy-done.8
  3.3 0.0 copy-start.1
  3.3 1.4 fusion.8
  4.6 0.0 copy-start
  4.7 1.3 fusion.7.attn_ref
  6.0 0.0 copy-done.1
  6.0 0.7 copy-done
  6.7 0.4 slice_bitcast_fusion
  7.1 0.0 copy-start.9
  7.1 0.0 copy-start.10
  7.1 2.0 fusion.3.ff_ref
  9.1 0.0 copy-start.5
  9.1 0.0 copy-start.6
  9.1 1.1 broadcast_in_dim.32.place_ref
  10.2 0.0 copy-done.9
  10.2 0.0 copy-done.10
  10.2 0.3 dynamic_update_slice.3.norm_ref
  10.6 0.0 copy-start.7
  10.6 0.1 fusion.10
  10.8 0.7 pad_maximum_fusion.mask_ref
  11.5 0.0 copy-done.5
  11.5 1.1 copy.16
  12.6 0.0 copy-done.6
  12.6 1.1 copy.17
  13.6 0.0 copy-done.7
  13.6 357.0 %relay.1 = (bf16[4,72,1152]{2,1,0:T(8,128)(2,1)}, bf16[4,72,2176]{2,1,0:T(8,128)(2,1)}, bf16[2,2,128,1088]{3,2,1,0:T(8,128)(2,1)}, f32[2,8,1152]{2,1,0:T(8,128)}) custom-call(bf16[272,1152]{1,0:T(8,128)(2,1)} %fusion.7.attn_ref, bf16[272,2176]{1,0:T(8,128)(2,1)} %fusion.3.ff_ref, bf16[2,128,1088]{2,1,0:T(8,128)(2,1)} %bitcast.62, ...), custom_call_target="tpu_custom_call" | custom-call | tf_op jit(solution)/shard_map/relay/pallas_call | solution.py:856
  370.7 1.5 slice_convert_fusion
  372.1 0.2 slice_bitcast_fusion.5
  372.3 0.1 maximum_bitcast_fusion.1
  372.4 2.2 copy.23
  374.6 0.1 maximum_bitcast_fusion
  374.7 0.0 copy-start.3
  374.7 2.2 copy.22
  377.0 0.0 copy-done.3
  377.0 0.1 slice_convert_fusion.1
  377.0 0.1 fusion.18
  377.1 0.2 concatenate.17
  377.4 0.0 copy-start.2
  377.4 1.9 copy.20
  379.2 0.9 slice.86
  380.1 0.6 constant_dynamic-slice_fusion
  380.8 1.0 copy.21
  381.8 0.0 copy-done.2
  381.8 0.1 slice_bitcast_fusion.8
  381.9 1.1 copy.18
  383.0 1.0 copy.19
  (7 shorter events, 0.1 us)
Async XLA Ops:
  2.2 1.1 copy-start.4
  2.2 1.1 copy-start.8
  3.3 2.7 copy-start.1
  4.6 2.0 copy-start
  7.1 3.1 copy-start.9
  7.1 3.1 copy-start.10
  9.1 2.4 copy-start.5
  9.1 3.4 copy-start.6
  10.6 3.0 copy-start.7
  374.7 2.2 copy-start.3
  377.4 4.4 %copy-start.2 = (bf16[2,2,128,1088]{3,2,1,0:T(8,128)(2,1)S(1)}, bf16[2,2,128,1088]{3,2,1,0:T(8,128)(2,1)}, u32[]{:S(2)}) copy-start(bf16[2,2,128,1088]{3,2,1,0:T(8,128)(2,1)} %get-tuple-element.12) | copy-start | bytes 3342340

commit v10 on v9

--- a/solution.py
+++ b/solution.py
@@ -216,6 +216,7 @@
                 pass_copy(s, block).start()
 
     attn_copy.start()
+    ff_copy.start()
     norm_copies = []
     for core in range(2):
         for stage in range(2):
@@ -234,7 +235,6 @@
             def _():
                 copy.start()
 
-    ff_copy.start()
     x_start(0)
     x_start(1)
     def g_start():

time: 384 us -> 383 us (level)
  no operation moved by 1% of the time
where the time goes in v10:
time: 383 us; the launch traced here: 382 us
  Pallas kernels  355 us (93%)
  local copies, waits for them, and re-layouts  18.8 us (5%)
  other arithmetic  7.31 us (2%)
    pallas_call x1, Pallas kernels, relay(): pl.pallas_call(relay_kernel, in_specs=[ANY] * 5 + [vmem] * 2, out_specs=[...  355 us
    unnamed x30, local copies, waits for them, and re-layouts  13.2 us

profile of v10, /device:TPU:24, one launch (start us, length us, event | category | flops | bytes accessed | tf_op | source)
XLA Modules:
  0.0 382.4 jit_solution(16234420394184132907)
XLA Ops:
  0.6 1.6 fusion.17
  2.2 0.0 copy-start.4
  2.2 0.0 copy-start.8
  2.2 0.1 pad_bitcast_fusion.1
  2.4 0.9 copy-done.4
  3.3 0.0 copy-done.8
  3.3 0.0 copy-start.1
  3.3 1.4 fusion.8
  4.6 0.0 copy-start
  4.7 1.3 fusion.7.attn_ref
  6.0 0.0 copy-done.1
  6.0 0.7 copy-done
  6.7 0.4 slice_bitcast_fusion
  7.1 0.0 copy-start.9
  7.1 0.0 copy-start.10
  7.1 2.0 fusion.3.ff_ref
  9.1 0.0 copy-start.5
  9.1 0.0 copy-start.6
  9.1 1.1 broadcast_in_dim.32.place_ref
  10.2 0.0 copy-done.9
  10.2 0.0 copy-done.10
  10.2 0.3 dynamic_update_slice.3.norm_ref
  10.6 0.0 copy-start.7
  10.6 0.1 fusion.10
  10.8 0.7 pad_maximum_fusion.mask_ref
  11.5 0.0 copy-done.5
  11.5 1.1 copy.16
  12.6 0.0 copy-done.6
  12.6 1.1 copy.17
  13.6 0.0 copy-done.7
  13.6 355.4 %relay.1 = (bf16[4,72,1152]{2,1,0:T(8,128)(2,1)}, bf16[4,72,2176]{2,1,0:T(8,128)(2,1)}, bf16[2,2,128,1088]{3,2,1,0:T(8,128)(2,1)}, f32[2,8,1152]{2,1,0:T(8,128)}) custom-call(bf16[272,1152]{1,0:T(8,128)(2,1)} %fusion.7.attn_ref, bf16[272,2176]{1,0:T(8,128)(2,1)} %fusion.3.ff_ref, bf16[2,128,1088]{2,1,0:T(8,128)(2,1)} %bitcast.62, ...), custom_call_target="tpu_custom_call" | custom-call | tf_op jit(solution)/shard_map/relay/pallas_call | solution.py:856
  369.1 1.5 slice_convert_fusion
  370.5 0.2 slice_bitcast_fusion.5
  370.7 0.1 maximum_bitcast_fusion.1
  370.8 2.2 copy.23
  373.0 0.1 maximum_bitcast_fusion
  373.1 0.0 copy-start.3
  373.1 2.2 copy.22
  375.4 0.0 copy-done.3
  375.4 0.1 slice_convert_fusion.1
  375.4 0.1 fusion.18
  375.5 0.2 concatenate.17
  375.8 0.0 copy-start.2
  375.8 1.9 copy.20
  377.6 0.9 slice.86
  378.5 0.6 constant_dynamic-slice_fusion
  379.2 1.0 copy.21
  380.2 0.0 copy-done.2
  380.2 0.1 slice_bitcast_fusion.8
  380.3 1.1 copy.18
  381.4 1.0 copy.19
  (7 shorter events, 0.1 us)
Async XLA Ops:
  2.2 1.1 copy-start.4
  2.2 1.1 copy-start.8
  3.3 2.7 copy-start.1
  4.6 2.0 copy-start
  7.1 3.1 copy-start.9
  7.1 3.1 copy-start.10
  9.1 2.4 copy-start.5
  9.1 3.4 copy-start.6
  10.6 3.0 copy-start.7
  373.1 2.2 copy-start.3
  375.8 4.4 %copy-start.2 = (bf16[2,2,128,1088]{3,2,1,0:T(8,128)(2,1)S(1)}, bf16[2,2,128,1088]{3,2,1,0:T(8,128)(2,1)}, u32[]{:S(2)}) copy-start(bf16[2,2,128,1088]{3,2,1,0:T(8,128)(2,1)} %get-tuple-element.12) | copy-start | bytes 3342340
